TPU v7x, 128 devices: a whole 4x4x4 slice. The times are simulated.
128 devices in a mesh: row: 16 (over y, z), col: 8 (over x, core).
Axes of the slice: x: 4, y: 4, z: 4, core: 2. Of those that a mesh axis runs over, the one named last changes fastest.
Arguments:
- load_currents: float32 [32, 2048, 1024], P(None, 'row', 'col'), may hold values from -36 to 36
- labels: int32 [2048, 1024], P('row', 'col'), may hold values from 0 to 255, as said below
- bump_height: float32 [2048, 1024], P('row', 'col'), may hold values from 0.5 to 2
- horizontal_class: int32 [2048, 1024], P('row', 'col'), may hold values from 0 to 7
- vertical_class: int32 [2048, 1024], P('row', 'col'), may hold values from 0 to 7
- pad_class: int32 [2048, 1024], P('row', 'col'), may hold values from 0 to 7
- edge_table: float32 [8], replicated, may hold values from 0.5 to 4
- pad_table: float32 [8], replicated, may hold values from 0.02 to 0.5
Outputs:
- solution: float32 [32, 2048, 1024], P(None, 'row', 'col')
- residual: float32 [32, 2048, 1024], P(None, 'row', 'col')
Inputs may be any that keep to these rules, and one draw needn't show every extreme that they name: `labels`: every number from 0 to 255 is the label of some nodes; the label of node (i, j) is 16 * floor(16 * i2 / 2048) + floor(16 * j2 / 1024) for some node (i2, j2) of the grid with |i2 - i| <= 32 and |j2 - j| <= 16.
All inputs are finite; a program needn't handle non-finite values.
Results may differ from a plain program's by a relative error of at most 0.0003.
Values sent between devices are 32-bit elements; how exact they have to be, the bound alone decides.
No kernel may reach another device: no remote copies, remote signals or barrier semaphores. Data moves between devices by JAX's collectives and lax.ppermute only.
A program may use at most 128 MiB of HBM per device.

v0:
```python
import jax
import jax.numpy as jnp
from jax import lax
from jax.sharding import Mesh
from jax.sharding import PartitionSpec as P

REG = 16
ITERS = 2
ROW = ("row_0", "row_1")
COL = ("col_0", "col_1")


precise = lax.Precision.HIGHEST


def from_behind(value, axis, steps):
    count = lax.axis_size(axis)
    initial, last = (max(0, -steps), min(count, count - steps))
    return lax.ppermute(value, axis, [(source, source + steps) for source in range(initial, last)])


def extended(value, sides, width):
    edges = {}
    for axis, dim in sides:
        size, length = (lax.axis_size(axis), value.shape[dim])
        up = [(i, (i + 1) % size) for i in range(size - 1)]
        last = lax.slice_in_dim(value, length - width, length, axis=dim)
        initial = lax.slice_in_dim(value, 0, width, axis=dim)
        edges[dim] = (
            lax.ppermute(last, axis, up),
            lax.ppermute(initial, axis, [(b, a) for a, b in up]),
        )
    done = []
    for _, dim in sides:
        low, high = edges[dim]
        around = [(width, width) if d in done else (0, 0) for d in range(value.ndim)]
        value = jnp.concatenate([jnp.pad(low, around), value, jnp.pad(high, around)], axis=dim)
        done.append(dim)
    return value


def rows_for(lines, length):
    spare = -lines.shape[0] % length
    if not spare:
        return lines
    return jnp.concatenate([lines, jnp.zeros((spare, *lines.shape[1:]), lines.dtype)])


def from_everyone(value, axis):
    length = lax.axis_size(axis)
    return lax.all_to_all(
        jnp.broadcast_to(value[None], (length, *value.shape)), axis, 0, 0, tiled=True
    )


def in_order(pieces, dim):
    pieces = jnp.moveaxis(pieces, 0, dim)
    lengths = pieces.shape
    return pieces.reshape(*lengths[:dim], lengths[dim] * lengths[dim + 1], *lengths[dim + 2 :])


def gathered_by_axis(value, axes, dim):
    far, near = axes
    initial = from_everyone(value, far)
    pieces = jnp.swapaxes(from_everyone(initial, near), 0, 1)
    return in_order(pieces.reshape(-1, *value.shape), dim)


def split_up(value, dim, length):
    before, after = (value.shape[:dim], value.shape[dim + 1 :])
    return jnp.moveaxis(value.reshape(*before, length, -1, *after), dim, 0)


def sent_and_summed(value, axis, dim):
    length = lax.axis_size(axis)
    pieces = lax.all_to_all(split_up(value, dim, length), axis, 0, 0, tiled=True)
    return jnp.sum(pieces, axis=0)


def sum_in_two_steps(value, axes, dim):
    far, near = axes
    own = sent_and_summed(split_up(value, dim, lax.axis_size(far)), near, dim + 1)
    return jnp.sum(lax.all_to_all(own, far, 0, 0, tiled=True), axis=0)


def nested_sum(value, axes):
    lines = value.reshape(-1, value.shape[-1])
    padded = rows_for(lines, lax.axis_size(axes[0]) * lax.axis_size(axes[1]))
    whole = gathered_by_axis(sum_in_two_steps(padded, axes, 0), axes, 0)
    return lax.slice_in_dim(whole, 0, len(lines)).reshape(value.shape)


def over_copies(value, axis):
    everything = from_everyone(value, axis)
    return jnp.sum(everything, axis=0)


def one_axis_at_a_time(value, axes):
    far, near = axes
    return over_copies(over_copies(value, near), far)


def packed_total(arrays, axis):
    ends = [0]
    for a in arrays:
        ends.append(ends[-1] + a.size)
    so_far = one_axis_at_a_time(jnp.concatenate([a.ravel() for a in arrays]), axis)
    return tuple((so_far[b:e].reshape(a.shape) for a, b, e in zip(arrays, ends, ends[1:])))


def lookup(entries, classes):
    levels = lax.broadcasted_iota(jnp.int32, (entries.shape[0],) + classes.shape, 0)
    return jnp.sum(jnp.where(classes[None] == levels, entries[:, None, None], 0.0), axis=0)


def stencil(padded, coeffs):
    diagonal, right_link, left_link, down_link, upper_link = coeffs
    centre = padded[:, 1:-1, 1:-1]
    return (
        diagonal * centre
        - right_link * padded[:, 1:-1, 2:]
        - left_link * padded[:, 1:-1, :-2]
        - down_link * padded[:, 2:, 1:-1]
        - upper_link * padded[:, :-2, 1:-1]
    )


def invert(matrix):
    factor = jnp.linalg.cholesky(matrix)
    identity = jnp.eye(matrix.shape[0], dtype=matrix.dtype)
    lower_solved = lax.linalg.triangular_solve(factor, identity, left_side=True, lower=True)
    return lax.linalg.triangular_solve(
        factor, lower_solved, left_side=True, lower=True, transpose_a=True
    )


def body(
    load_currents,
    labels,
    bump_height,
    horizontal_class,
    vertical_class,
    pad_class,
    edge_table,
    pad_table,
):
    tile_rows, tile_cols = labels.shape
    regions = REG * REG
    load_count = load_currents.shape[0]
    tile_cells = tile_rows * tile_cols
    grid_rows = lax.axis_size(ROW) * tile_rows
    grid_cols = lax.axis_size(COL) * tile_cols
    row_ids = lax.axis_index(ROW) * tile_rows + lax.broadcasted_iota(jnp.int32, labels.shape, 0)
    col_ids = lax.axis_index(COL) * tile_cols + lax.broadcasted_iota(jnp.int32, labels.shape, 1)
    right_link = jnp.where(col_ids == grid_cols - 1, 0.0, lookup(edge_table, horizontal_class))
    down_link = jnp.where(row_ids == grid_rows - 1, 0.0, lookup(edge_table, vertical_class))
    left_edge = from_behind(right_link[:, -1:], COL, 1)
    left_link = jnp.concatenate([left_edge, right_link[:, :-1]], axis=1)
    upper_edge = from_behind(down_link[-1:, :], ROW, 1)
    upper_link = jnp.concatenate([upper_edge, down_link[:-1, :]], axis=0)
    diagonal = lookup(pad_table, pad_class) + right_link + left_link + down_link + upper_link
    coeffs = (diagonal, right_link, left_link, down_link, upper_link)
    levels = lax.broadcasted_iota(jnp.int32, (regions,) + labels.shape, 0)
    deflation = jnp.where(labels[None] == levels, bump_height[None], 0.0)
    deflation_image = stencil(extended(deflation, ((ROW, 1), (COL, 2)), 1), coeffs)
    basis_flat = deflation.reshape(regions, tile_cells)
    image_flat = deflation_image.reshape(regions, tile_cells)
    contract = (((1,), (1,)), ((), ()))
    partial_matrix = lax.dot_general(basis_flat, image_flat, contract, precision=precise)
    inverse = invert(nested_sum(partial_matrix, (("row_0", "row_1", "col_0"), "col_1")))

    def project(field):
        return lax.dot_general(
            field.reshape(load_count, tile_cells), basis_flat, contract, precision=precise
        )

    def expand(coarse):
        return jnp.dot(coarse, basis_flat, precision=precise).reshape(
            load_count, tile_rows, tile_cols
        )

    def correction_image(coarse):
        return jnp.dot(coarse, image_flat, precision=precise).reshape(
            load_count, tile_rows, tile_cols
        )

    def refresh(residual):
        scaled = residual / diagonal
        local_norm = jnp.sum(residual * scaled, axis=(1, 2))
        field_image = stencil(extended(scaled, ((ROW, 1), (COL, 2)), 1), coeffs)
        weighted_norm, projected = packed_total(
            (local_norm, project(field_image)), (("row_0", "row_1"), ("col_0", "col_1"))
        )
        coarse = jnp.dot(projected, inverse, precision=precise)
        return (scaled, weighted_norm, field_image, coarse)

    load_sums = one_axis_at_a_time(project(load_currents), (("row_0", "row_1"), ("col_0", "col_1")))
    coarse = jnp.dot(load_sums, inverse, precision=precise)
    solution = expand(coarse)
    residual = load_currents - correction_image(coarse)
    scaled, weighted_norm, field_image, coarse = refresh(residual)
    spread = expand(coarse)
    direction = scaled - spread
    direction_image = field_image - correction_image(coarse)
    for iteration in range(ITERS):
        local_curve = jnp.sum(direction * direction_image, axis=(1, 2))
        curvature = one_axis_at_a_time(local_curve, (("row_0", "row_1", "col_0"), "col_1"))
        step_size = (weighted_norm / curvature)[:, None, None]
        solution = solution + step_size * direction
        residual = residual - step_size * direction_image
        if iteration + 1 < ITERS:
            scaled, new_norm, field_image, coarse = refresh(residual)
            spread = expand(coarse)
            beta_ratio = (new_norm / weighted_norm)[:, None, None]
            direction = scaled - spread + beta_ratio * direction
            direction_image = field_image - correction_image(coarse) + beta_ratio * direction_image
            weighted_norm = new_norm
    return (solution, residual)


def solution(mesh):
    finer = Mesh(mesh.devices.reshape(4, 4, 4, 2), ("row_0", "row_1", "col_0", "col_1"))
    placed = (
        P(None, ROW, COL),
        P(ROW, COL),
        P(ROW, COL),
        P(ROW, COL),
        P(ROW, COL),
        P(ROW, COL),
        P(),
        P(),
    )
    return jax.shard_map(
        body,
        mesh=finer,
        in_specs=placed,
        out_specs=(P(None, ROW, COL), P(None, ROW, COL)),
        check_vma=False,
    )
```

profile of v0, /device:TPU:1, one launch (start us, length us, event | category | flops | bytes accessed | tf_op | source)
XLA Modules:
  0.0 522.4 jit_solution(6372291015990332203)
XLA Ops:
  28.3 32.9 %fusion.15 = f32[256,128,128]{0,2,1:T(8,128)S(1)} fusion(f32[256,128,128]{0,2,1:T(8,128)} %copy-done.1, f32[256,1,128]{0,2,1:T(8,128)S(1)} %collective-permute-done.2, f32[256,1,128]{0,2,1:T(8,128)S(1)} %collective-permute-done.3, f32[256,128,1]{0,2,1:T(1,128)S(1)} %collective-permute-done.5, f32[256,128,1]{0,2,1:T(1,128)S(1)} %collective-permute-done.4, ...), kind=kLoop, calls=%fused_computation.18 | loop fusion | flops 104857600 | bytes 34537472 | tf_op jit(solution)/shard_map/sub | solution.py:120
  61.3 15.8 %fusion.89 = f32[2,64,2,256]{3,1,2,0:T(8,128)S(1)} fusion(f32[256,16384,1,1]{0,1,3,2:T(8,128)S(1)} %bitcast.96, f32[16384]{0:T(1024)S(1)} %bitcast.100, s32[64,2,2]{0,2,1:T(2,128)S(1)} %multiply_add_fusion.3, s32[16384]{0:T(1024)S(1)} %bitcast.101), kind=kOutput, calls=%fused_computation.120 | convolution fusion | flops 12893290496 | bytes 17171456 | tf_op jit(solution)/shard_map/dot_general | solution.py:169
  81.5 12.5 %all-to-all-start.3 = ((f32[64,2,256]{2,1,0:T(2,128)}), f32[64,2,256]{2,1,0:T(2,128)S(1)}, u32[]{:S(2)}, u32[]{:S(2)}) async-start(f32[64,2,256]{2,1,0:T(2,128)} %copy.83), calls=%async_computation.3 | async-start | bytes 262144 | tf_op jit(solution)/shard_map/all_to_all | solution.py:83
  94.0 18.0 %fusion.92 = f32[32,256]{1,0:T(8,128)S(1)} fusion(f32[32,128,128]{2,1,0:T(8,128)S(1)} %copy-done.11, f32[128,128]{1,0:T(8,128)S(1)} %copy-done.12, s32[128,128]{1,0:T(8,128)S(1)} %copy-done.13), kind=kOutput, calls=%fused_computation.124 | convolution fusion | flops 1619001344 | bytes 2260992 | tf_op jit(solution)/shard_map/dot_general | solution.py:173
  124.9 8.1 %all-to-all-start.4 = ((f32[64,2,256]{2,1,0:T(2,128)}), f32[64,2,256]{2,1,0:T(2,128)S(1)}, u32[]{:S(2)}, u32[]{:S(2)}) async-start(f32[64,2,256]{2,1,0:T(2,128)} %broadcast_in_dim.86), calls=%async_computation.4 | async-start | bytes 262144 | tf_op jit(solution)/shard_map/all_to_all | solution.py:51
  133.1 8.8 %all-to-all-done.4 = f32[64,2,256]{2,1,0:T(2,128)S(1)} async-done(((f32[64,2,256]{2,1,0:T(2,128)}), f32[64,2,256]{2,1,0:T(2,128)S(1)}, u32[]{:S(2)}, u32[]{:S(2)}) %all-to-all-start.4) | async-done | bytes 131104 | tf_op jit(solution)/shard_map/all_to_all | solution.py:51
  153.0 11.7 %cholesky.53 = f32[128,128]{1,0:T(8,128)S(1)} custom-call(f32[128,128]{1,0:T(8,128)S(1)} %cholesky.121), custom_call_target="Cholesky" | custom-call | tf_op jit(solution)/shard_map/jit(cholesky)/cholesky | solution.py:129
  164.8 9.8 %custom-call.16 = f32[1,128,128]{1,2,0:T(8,128)S(1)} custom-call(f32[1,128,128]{2,1,0:T(8,128)S(1)} %get-tuple-element.56), custom_call_target="InvertDiagBlocksLowerTriangular" | custom-call | tf_op jit(solution)/shard_map/jit(cholesky)/cholesky | solution.py:129
  175.1 11.7 %cholesky.108 = f32[128,128]{1,0:T(8,128)S(1)} custom-call(f32[128,128]{1,0:T(8,128)S(1)} %convolution_subtract_fusion.2), custom_call_target="Cholesky" | custom-call | tf_op jit(solution)/shard_map/jit(cholesky)/cholesky | solution.py:129
  192.8 20.1 %custom-call.17 = f32[2,128,128]{1,2,0:T(8,128)S(1)} custom-call(f32[2,128,128]{2,1,0:T(8,128)S(1)} %get-tuple-element.9), custom_call_target="InvertDiagBlocksLowerTriangular" | custom-call | tf_op jit(solution)/shard_map/triangular_solve | solution.py:132
  214.9 18.5 %multiply_reduce_fusion.3 = (f32[32]{0:T(128)S(1)}, f32[32,128,128]{2,0,1:T(8,128)S(1)}, f32[32,128,128]{2,0,1:T(8,128)}) fusion(f32[128,128]{1,0:T(8,128)S(1)} %get-tuple-element.34, f32[32,256,1]{1,0,2:T(8,128)S(1)} %convolution_bitcast_fusion.2, f32[256,128,128]{0,2,1:T(8,128)} %copy-done, f32[32,128,128]{2,1,0:T(8,128)} %param.8), kind=kOutput, calls=%fused_computation.115 | convolution fusion | flops 1612709888 | bytes 23167104 | tf_op jit(solution)/shard_map/dot_general | solution.py:183
  262.1 16.5 %fusion.97 = f32[4,2,8,128]{3,2,1,0:T(8,128)S(1)} fusion(f32[32,128,128]{2,0,1:T(8,128)S(1)} %fusion.65, f32[128,128]{1,0:T(8,128)S(1)} %copy-done.12, s32[128,128]{1,0:T(8,128)S(1)} %copy-done.13), kind=kOutput, calls=%fused_computation.125 | convolution fusion | flops 1619001344 | bytes 2260992 | tf_op jit(solution)/shard_map/dot_general | solution.py:173
  278.9 9.5 %all_to_all.80 = f32[8,1,8224]{2,1,0:T(1,128)S(1)} all-to-all(f32[8,1,8224]{2,1,0:T(1,128)S(1)} %broadcast_in_dim.90), channel_id=1, replica_groups=mesh['row_0'=4,'row_1'=4,'col_0'=4,'col_1'=2] {'col_0','col_1'}, dimensions={0} | all-to-all | bytes 526336 | tf_op jit(solution)/shard_map/all_to_all | solution.py:51
  288.9 18.6 %all_to_all.81 = f32[16,1,8224]{2,1,0:T(1,128)S(1)} all-to-all(f32[16,1,8224]{2,1,0:T(1,128)S(1)} %broadcast_in_dim.91), channel_id=1, replica_groups=mesh['row_0'=4,'row_1'=4,'col_0'=4,'col_1'=2] {'row_0','row_1'}, dimensions={0} | all-to-all | bytes 1052672 | tf_op jit(solution)/shard_map/all_to_all | solution.py:51
  308.2 17.8 %fusion.84 = f32[32,128,128]{2,0,1:T(8,128)S(1)} fusion(f32[32,128,128]{2,0,1:T(8,128)} %copy-done.10, f32[32,256,1]{1,0,2:T(8,128)S(1)} %convolution_bitcast_fusion.1, f32[256,128,128]{0,2,1:T(8,128)} %copy-done), kind=kOutput, calls=%fused_computation.119 | convolution fusion | flops 1611137024 | bytes 21004288 | tf_op jit(solution)/shard_map/dot_general | solution.py:183
  326.1 20.1 %multiply_reduce_fusion.2 = (f32[32]{0:T(128)S(1)}, f32[32,128,128]{2,0,1:T(8,128)}) fusion(f32[32,128,128]{2,0,1:T(8,128)S(1)} %fusion.84, f32[32,256,1]{1,0,2:T(8,128)S(1)} %convolution_bitcast_fusion.1, f32[128,128]{1,0:T(8,128)S(1)} %copy-done.12, s32[128,128]{1,0:T(8,128)S(1)} %copy-done.13, f32[32,128,128]{2,0,1:T(8,128)S(1)} %copy-done.8, ...), kind=kOutput, calls=%fused_computation.114 | convolution fusion | flops 1621098496 | bytes 6520960 | tf_op jit(solution)/shard_map/dot_general | solution.py:178
  351.2 13.1 %all_to_all.83 = f32[64,1,32]{2,1,0:T(1,128)S(1)} all-to-all(f32[64,1,32]{2,1,0:T(1,128)S(1)} %broadcast_in_dim.93), channel_id=1, replica_groups=mesh['row_0'=4,'row_1'=4,'col_0'=4,'col_1'=2] {'row_0','row_1','col_0'}, dimensions={0} | all-to-all | bytes 16384 | tf_op jit(solution)/shard_map/all_to_all | solution.py:51
  396.2 16.5 %fusion.100 = f32[4,2,8,128]{3,2,1,0:T(8,128)S(1)} fusion(f32[32,128,128]{2,0,1:T(8,128)S(1)} %fusion.55, f32[128,128]{1,0:T(8,128)S(1)} %copy-done.12, s32[128,128]{1,0:T(8,128)S(1)} %copy-done.13), kind=kOutput, calls=%fused_computation.126 | convolution fusion | flops 1619001344 | bytes 2260992 | tf_op jit(solution)/shard_map/dot_general | solution.py:173
  413.0 10.5 %all_to_all.84 = f32[8,1,8224]{2,1,0:T(1,128)S(1)} all-to-all(f32[8,1,8224]{2,1,0:T(1,128)S(1)} %broadcast_in_dim.94), channel_id=1, replica_groups=mesh['row_0'=4,'row_1'=4,'col_0'=4,'col_1'=2] {'col_0','col_1'}, dimensions={0} | all-to-all | bytes 526336 | tf_op jit(solution)/shard_map/all_to_all | solution.py:51
  424.0 17.5 %all_to_all.85 = f32[16,1,8224]{2,1,0:T(1,128)S(1)} all-to-all(f32[16,1,8224]{2,1,0:T(1,128)S(1)} %broadcast_in_dim.95), channel_id=1, replica_groups=mesh['row_0'=4,'row_1'=4,'col_0'=4,'col_1'=2] {'row_0','row_1'}, dimensions={0} | all-to-all | bytes 1052672 | tf_op jit(solution)/shard_map/all_to_all | solution.py:51
  442.2 17.9 %multiply_add_fusion.1 = f32[32,128,128]{2,0,1:T(8,128)S(1)} fusion(f32[32,128,128]{2,0,1:T(8,128)S(1)} %copy-done.3, f32[32,128,128]{2,0,1:T(8,128)} %copy-done.9, f32[32,256,1]{1,0,2:T(8,128)S(1)} %convolution_bitcast_fusion, f32[256,128,128]{0,2,1:T(8,128)} %copy-done, f32[32]{0:T(128)S(1)} %slice_divide_fusion), kind=kOutput, calls=%fused_computation.110 | convolution fusion | flops 1612185600 | bytes 23101568 | tf_op jit(solution)/shard_map/dot_general | solution.py:183
  460.2 18.9 %multiply_reduce_fusion = (f32[32]{0:T(128)S(1)}, f32[32,128,128]{2,0,1:T(8,128)}) fusion(f32[32,128,128]{2,0,1:T(8,128)S(1)} %multiply_add_fusion.1, f32[32,128,128]{2,0,1:T(8,128)S(1)} %copy-done.16, f32[32]{0:T(128)S(1)} %slice_divide_fusion, f32[32,256,1]{1,0,2:T(8,128)S(1)} %convolution_bitcast_fusion, f32[128,128]{1,0:T(8,128)S(1)} %copy-done.12, ...), kind=kOutput, calls=%fused_computation.109 | convolution fusion | flops 1622147072 | bytes 8618240 | tf_op jit(solution)/shard_map/dot_general | solution.py:178
  484.1 13.2 %all_to_all.87 = f32[64,1,32]{2,1,0:T(1,128)S(1)} all-to-all(f32[64,1,32]{2,1,0:T(1,128)S(1)} %broadcast_in_dim.173), channel_id=1, replica_groups=mesh['row_0'=4,'row_1'=4,'col_0'=4,'col_1'=2] {'row_0','row_1','col_0'}, dimensions={0} | all-to-all | bytes 16384 | tf_op jit(solution)/shard_map/all_to_all | solution.py:51
  502.1 17.3 %multiply_add_fusion = f32[32,128,128]{2,0,1:T(8,128)S(1)} fusion(f32[32,128,128]{2,0,1:T(8,128)S(1)} %copy-done.18, f32[32,128,128]{2,0,1:T(8,128)S(1)} %copy-done.17, f32[32,256,1]{1,0,2:T(8,128)S(1)} %convolution_bitcast_fusion.2, f32[128,128]{1,0:T(8,128)S(1)} %copy-done.12, s32[128,128]{1,0:T(8,128)S(1)} %copy-done.13, f32[32]{0:T(128)S(1)} %slice_divide_fusion.1, ...), kind=kOutput, calls=%fused_computation.108 | convolution fusion | flops 1621098496 | bytes 6455552 | tf_op jit(solution)/shard_map/dot_general | solution.py:178
  (175 shorter events, 147.7 us)
Async XLA Ops:
  1.8 20.9 %collective-permute-start = (f32[128,1]{1,0:T(8,128)S(1)}, f32[128,1]{1,0:T(8,128)S(1)}, u32[]{:S(2)}, u32[]{:S(2)}) collective-permute-start(f32[128,1]{1,0:T(8,128)S(1)} %slice.204), channel_id=1, source_target_pairs={{0,1},{1,2},{2,3},{3,4},{4,5},{5,6},{6,7},{8,9},{9,10},{10,11},{11... | collective-permute-start | bytes 1544 | tf_op jit(solution)/shard_map/ppermute | solution.py:19
  6.5 21.9 %copy-start.12 = (f32[128,128]{1,0:T(8,128)S(1)}, f32[128,128]{1,0:T(8,128)}, u32[]{:S(2)}) copy-start(f32[128,128]{1,0:T(8,128)} %param.10) | copy-start | bytes 196612
  6.5 21.9 %copy-start.13 = (s32[128,128]{1,0:T(8,128)S(1)}, s32[128,128]{1,0:T(8,128)}, u32[]{:S(2)}) copy-start(s32[128,128]{1,0:T(8,128)} %param.9) | copy-start | bytes 196612
  6.5 19.9 %collective-permute-start.1 = (f32[1,128]{1,0:T(1,128)S(1)}, f32[1,128]{1,0:T(1,128)S(1)}, u32[]{:S(2)}, u32[]{:S(2)}) collective-permute-start(f32[1,128]{1,0:T(1,128)S(1)} %slice.206), channel_id=1, source_target_pairs={{0,8},{8,16},{16,24},{24,32},{32,40},{40,48},{48,56},{56,64},{64,7... | collective-permute-start | bytes 1544 | tf_op jit(solution)/shard_map/ppermute | solution.py:19
  15.6 10.9 %collective-permute-start.2 = (f32[256,1,128]{0,2,1:T(8,128)S(1)}, f32[256,1,128]{0,2,1:T(8,128)S(1)}, u32[]{:S(2)}, u32[]{:S(2)}) collective-permute-start(f32[256,1,128]{0,2,1:T(8,128)S(1)} %get-tuple-element.42), channel_id=1, source_target_pairs={{0,8},{8,16},{16,24},{24,32},{32,40},{40,48},{48,56},{56,64},{64,7... | collective-permute-start | bytes 393224 | tf_op jit(solution)/shard_map/ppermute | solution.py:30
  19.2 7.4 %collective-permute-start.3 = (f32[256,1,128]{0,2,1:T(8,128)S(1)}, f32[256,1,128]{0,2,1:T(8,128)S(1)}, u32[]{:S(2)}, u32[]{:S(2)}) collective-permute-start(f32[256,1,128]{0,2,1:T(8,128)S(1)} %get-tuple-element.41), channel_id=1, source_target_pairs={{8,0},{16,8},{24,16},{32,24},{40,32},{48,40},{56,48},{64,56},{72,6... | collective-permute-start | bytes 393224 | tf_op jit(solution)/shard_map/ppermute | solution.py:31
  20.7 6.3 %collective-permute-start.4 = (f32[256,128,1]{0,2,1:T(1,128)S(1)}, f32[256,128,1]{0,2,1:T(1,128)S(1)}, u32[]{:S(2)}, u32[]{:S(2)}) collective-permute-start(f32[256,128,1]{0,2,1:T(1,128)S(1)} %get-tuple-element.39), channel_id=1, source_target_pairs={{1,0},{2,1},{3,2},{4,3},{5,4},{6,5},{7,6},{9,8},{10,9},{11,10},{12... | collective-permute-start | bytes 393224 | tf_op jit(solution)/shard_map/ppermute | solution.py:31
  22.8 5.6 %collective-permute-start.5 = (f32[256,128,1]{0,2,1:T(1,128)S(1)}, f32[256,128,1]{0,2,1:T(1,128)S(1)}, u32[]{:S(2)}, u32[]{:S(2)}) collective-permute-start(f32[256,128,1]{0,2,1:T(1,128)S(1)} %get-tuple-element.40), channel_id=1, source_target_pairs={{0,1},{1,2},{2,3},{3,4},{4,5},{5,6},{6,7},{8,9},{9,10},{10,11},{11... | collective-permute-start | bytes 393224 | tf_op jit(solution)/shard_map/ppermute | solution.py:30
  61.3 32.6 %copy-start.11 = (f32[32,128,128]{2,1,0:T(8,128)S(1)}, f32[32,128,128]{2,1,0:T(8,128)}, u32[]{:S(2)}) copy-start(f32[32,128,128]{2,1,0:T(8,128)} %param.8) | copy-start | bytes 6291460
  81.5 30.5 %all-to-all-start.3 = ((f32[64,2,256]{2,1,0:T(2,128)}), f32[64,2,256]{2,1,0:T(2,128)S(1)}, u32[]{:S(2)}, u32[]{:S(2)}) async-start(f32[64,2,256]{2,1,0:T(2,128)} %copy.83), calls=%async_computation.3 | async-start | bytes 262144 | tf_op jit(solution)/shard_map/all_to_all | solution.py:83
  112.7 11.5 %all-to-all-start = ((f32[8,32,256]{2,1,0:T(8,128)}), f32[8,32,256]{2,1,0:T(8,128)S(1)}, u32[]{:S(2)}, u32[]{:S(2)}) async-start(f32[8,32,256]{2,1,0:T(8,128)} %broadcast_in_dim.77), calls=%async_computation | async-start | bytes 524288 | tf_op jit(solution)/shard_map/all_to_all | solution.py:51
  124.9 17.0 %all-to-all-start.4 = ((f32[64,2,256]{2,1,0:T(2,128)}), f32[64,2,256]{2,1,0:T(2,128)S(1)}, u32[]{:S(2)}, u32[]{:S(2)}) async-start(f32[64,2,256]{2,1,0:T(2,128)} %broadcast_in_dim.86), calls=%async_computation.4 | async-start | bytes 262144 | tf_op jit(solution)/shard_map/all_to_all | solution.py:51
  148.8 65.9 %all-to-all-start.1 = ((f32[16,32,256]{2,1,0:T(8,128)}), f32[16,32,256]{2,1,0:T(8,128)S(1)}, u32[]{:S(2)}, u32[]{:S(2)}) async-start(f32[16,32,256]{2,1,0:T(8,128)} %broadcast_in_dim.78), calls=%async_computation.1 | async-start | bytes 1048576 | tf_op jit(solution)/shard_map/all_to_all | solution.py:51
  238.8 12.8 %collective-permute-start.8 = (f32[32,128,1]{1,0,2:T(8,128)S(1)}, f32[32,128,1]{1,0,2:T(8,128)S(1)}, u32[]{:S(2)}, u32[]{:S(2)}) collective-permute-start(f32[32,128,1]{1,0,2:T(8,128)S(1)} %copy.87), channel_id=1, source_target_pairs={{1,0},{2,1},{3,2},{4,3},{5,4},{6,5},{7,6},{9,8},{10,9},{11,10},{12... | collective-permute-start | bytes 49160 | tf_op jit(solution)/shard_map/ppermute | solution.py:31
  243.8 10.8 %collective-permute-start.9 = (f32[32,128,1]{1,0,2:T(8,128)S(1)}, f32[32,128,1]{1,0,2:T(8,128)S(1)}, u32[]{:S(2)}, u32[]{:S(2)}) collective-permute-start(f32[32,128,1]{1,0,2:T(8,128)S(1)} %copy.89), channel_id=1, source_target_pairs={{0,1},{1,2},{2,3},{3,4},{4,5},{5,6},{6,7},{8,9},{9,10},{10,11},{11... | collective-permute-start | bytes 49160 | tf_op jit(solution)/shard_map/ppermute | solution.py:30
  247.0 10.4 %collective-permute-start.6 = (f32[32,1,128]{2,0,1:T(8,128)S(1)}, f32[32,1,128]{2,0,1:T(8,128)S(1)}, u32[]{:S(2)}, u32[]{:S(2)}) collective-permute-start(f32[32,1,128]{2,0,1:T(8,128)S(1)} %get-tuple-element.52), channel_id=1, source_target_pairs={{0,8},{8,16},{16,24},{24,32},{32,40},{40,48},{48,56},{56,64},{64,7... | collective-permute-start | bytes 49160 | tf_op jit(solution)/shard_map/ppermute | solution.py:30
  250.2 7.2 %collective-permute-start.7 = (f32[32,1,128]{2,0,1:T(8,128)S(1)}, f32[32,1,128]{2,0,1:T(8,128)S(1)}, u32[]{:S(2)}, u32[]{:S(2)}) collective-permute-start(f32[32,1,128]{2,0,1:T(8,128)S(1)} %get-tuple-element.51), channel_id=1, source_target_pairs={{8,0},{16,8},{24,16},{32,24},{40,32},{48,40},{56,48},{64,56},{72,6... | collective-permute-start | bytes 49160 | tf_op jit(solution)/shard_map/ppermute | solution.py:31
  326.1 38.3 %copy-start.2 = (f32[32,128,128]{2,0,1:T(8,128)}, f32[32,128,128]{2,0,1:T(8,128)S(1)}, u32[]{:S(2)}) copy-start(f32[32,128,128]{2,0,1:T(8,128)S(1)} %fusion.84) | copy-start | bytes 6291460
  373.8 12.0 %collective-permute-start.12 = (f32[32,128,1]{1,0,2:T(8,128)S(1)}, f32[32,128,1]{1,0,2:T(8,128)S(1)}, u32[]{:S(2)}, u32[]{:S(2)}) collective-permute-start(f32[32,128,1]{1,0,2:T(8,128)S(1)} %copy.96), channel_id=1, source_target_pairs={{1,0},{2,1},{3,2},{4,3},{5,4},{6,5},{7,6},{9,8},{10,9},{11,10},{12... | collective-permute-start | bytes 49160 | tf_op jit(solution)/shard_map/ppermute | solution.py:31
  380.1 8.5 %collective-permute-start.13 = (f32[32,128,1]{1,0,2:T(8,128)S(1)}, f32[32,128,1]{1,0,2:T(8,128)S(1)}, u32[]{:S(2)}, u32[]{:S(2)}) collective-permute-start(f32[32,128,1]{1,0,2:T(8,128)S(1)} %copy.98), channel_id=1, source_target_pairs={{0,1},{1,2},{2,3},{3,4},{4,5},{5,6},{6,7},{8,9},{9,10},{10,11},{11... | collective-permute-start | bytes 49160 | tf_op jit(solution)/shard_map/ppermute | solution.py:30
  382.2 9.3 %collective-permute-start.10 = (f32[32,1,128]{2,0,1:T(8,128)S(1)}, f32[32,1,128]{2,0,1:T(8,128)S(1)}, u32[]{:S(2)}, u32[]{:S(2)}) collective-permute-start(f32[32,1,128]{2,0,1:T(8,128)S(1)} %get-tuple-element.48), channel_id=1, source_target_pairs={{0,8},{8,16},{16,24},{24,32},{32,40},{40,48},{48,56},{56,64},{64,7... | collective-permute-start | bytes 49160 | tf_op jit(solution)/shard_map/ppermute | solution.py:30
  384.5 7.0 %collective-permute-start.11 = (f32[32,1,128]{2,0,1:T(8,128)S(1)}, f32[32,1,128]{2,0,1:T(8,128)S(1)}, u32[]{:S(2)}, u32[]{:S(2)}) collective-permute-start(f32[32,1,128]{2,0,1:T(8,128)S(1)} %get-tuple-element.47), channel_id=1, source_target_pairs={{8,0},{16,8},{24,16},{32,24},{40,32},{48,40},{56,48},{64,56},{72,6... | collective-permute-start | bytes 49160 | tf_op jit(solution)/shard_map/ppermute | solution.py:31
  412.7 29.5 %copy-start.3 = (f32[32,128,128]{2,0,1:T(8,128)S(1)}, f32[32,128,128]{2,0,1:T(8,128)}, u32[]{:S(2)}) copy-start(f32[32,128,128]{2,0,1:T(8,128)} %copy-done.2) | copy-start | bytes 6291460
  460.1 37.2 %copy-start.6 = (f32[32,128,128]{2,0,1:T(8,128)S(1)}, f32[32,128,128]{2,0,1:T(8,128)}, u32[]{:S(2)}) copy-start(f32[32,128,128]{2,0,1:T(8,128)} %copy-done.4) | copy-start | bytes 6291460
  (13 other events, 173.0 us)
where the time goes:
time: 533 us; the launch traced here: 522 us
  matrix products  180 us (34%)
  other arithmetic  110 us (21%)
  blocking collectives  102 us (19%)
  starting transfers between devices  67.4 us (13%)
  local copies, waits for them, and re-layouts  42.9 us (8%)
  waiting for transfers between devices  17 us (3%)
    all_to_all x9, blocking collectives, from_everyone(): lax.all_to_all(jnp.broadcast_to(value[None], (length, *value.shape)), axi...  98.4 us
    dot_general x3, matrix products, expand(): jnp.dot(coarse, basis_flat, precision=precise)  56.2 us
    dot_general x3, matrix products, correction_image(): jnp.dot(coarse, image_flat, precision=precise)  54.2 us
    dot_general x3, matrix products, project(): lax.dot_general(field.reshape(load_count, tile_cells), basis_flat, contra...  51.1 us
    sub x3, other arithmetic, stencil(): diagonal * centre - right_link * padded[:, 1:-1, 2:]  42.3 us
    another operation x6, other arithmetic, invert(): factor = jnp.linalg.cholesky(matrix)  34 us
    another operation x3, other arithmetic, invert(): lax.linalg.triangular_solve(factor, lower_solved, left_side=True, lower=T...  20.1 us
    ppermute x6, starting transfers between devices, extended(): lax.ppermute(last, axis, up)  17.9 us
  transfers between devices with their start and end apart: 18, of which 4 were waited for; matrix products, arithmetic and copies ran while one was open for 19% of the time, Pallas kernels for 0%

commit v1 on v0

v1 whole, which is shorter than its diff:
```python
import jax
import jax.numpy as jnp
from jax import lax
from jax.experimental import pallas as pl
from jax.experimental.pallas import tpu as pltpu
from jax.sharding import Mesh
from jax.sharding import PartitionSpec as P

REG = 16
ROW = ("row_0", "row_1")
COL = ("col_0", "col_1")
F32 = jnp.float32
precise = lax.Precision.HIGHEST

LAB, BUMP, RIGHT, DOWN, PAD = 32, 33, 34, 35, 36
SUB = 40
HALO = 3
EXT = 134
GROUPS = 9
ORDER = (1, 3, 5, 7, 9, 11, 13, 15, 2, 6, 10, 14, 4, 12, 8, 0)
POS = tuple(ORDER.index(p) for p in range(16))
NT = (((1,), (1,)), ((), ()))
NN = (((1,), (0,)), ((), ()))
TN = (((0,), (0,)), ((), ()))
whole = pl.BlockSpec(memory_space=pltpu.VMEM)
scalars = pl.BlockSpec(memory_space=pltpu.SMEM)


def dot(a, b, dims=NN):
    return lax.dot_general(a, b, dims, precision=precise, preferred_element_type=F32)


def lanes(shape):
    return lax.broadcasted_iota(jnp.int32, shape, len(shape) - 1)


def roll(x, shift, axis=1):
    return pltpu.roll(x, shift, axis)


def pack_kernel(x_ref, top_ref, bottom_ref, out_ref):
    lane = lanes((SUB, 128))
    for g in range(GROUPS):
        acc = jnp.zeros((SUB, 128), F32)
        for s in range(16):
            r = 16 * g - 8 + s
            if r < -HALO or r >= 128 + HALO:
                continue
            if r < 0:
                row = top_ref[r + HALO]
            elif r < 128:
                row = x_ref[r]
            else:
                row = bottom_ref[r - 128]
            acc = jnp.where(lane // 8 == s, roll(row, (8 * s + 3) % 128), acc)
        out_ref[g] = acc


def fields_kernel(
    place_ref, x_ref, top_ref, bottom_ref, own_ref, left_ref, right_ref,
    first_ref, second_ref, basis_ref, coef_ref, out_ref,
    xe, sz_o, sz_s, y0_o, y0_s, y1_s, sc, zs, y0, y1, gram,
):
    pr, pc = place_ref[0], place_ref[1]
    lane1 = lanes((1, 128))
    lane16 = lanes((16, 128))
    lane48 = lanes((48, 128))

    for i in range(HALO):
        xe[i] = top_ref[i]
        xe[EXT - HALO + i] = bottom_ref[i]

    def copy_rows(i, _):
        xe[i + HALO] = x_ref[i]
        return 0

    lax.fori_loop(0, 128, copy_rows, 0, unroll=4)

    slot = lax.broadcasted_iota(jnp.int32, (16, 128), 0)
    region_row = pr - 1 + slot // 4
    region_col = 2 * pc - 1 + slot % 4
    inside = (slot < 12) & (region_row >= 0) & (region_row < REG) & (region_col >= 0) & (region_col < REG)
    window = jnp.where(inside, region_row * REG + region_col, -1).astype(F32)

    def mixed(g):
        j = lanes((SUB, 128)) % 8
        return jnp.where(j < 3, left_ref[g], right_ref[g])

    def pair_left(o, s, lane):
        j = lane % 8
        return roll(jnp.where(j == 2, s, o), 1), roll(jnp.where(j == 2, o, s), 1)

    def pair_right(o, s, lane):
        j = lane % 8
        return roll(jnp.where(j == 3, s, o), 127), roll(jnp.where(j == 3, o, s), 127)

    def above(before, here, lane):
        return roll(jnp.where(lane >= 120, before, here), 8)

    def below(here, after, lane):
        return roll(jnp.where(lane < 8, after, here), 120)

    for g in range(GROUPS):
        o_row, s_row = own_ref[g], mixed(g)
        o_before = own_ref[g - 1] if g else jnp.zeros((SUB, 128), F32)
        s_before = mixed(g - 1) if g else jnp.zeros((SUB, 128), F32)
        lefts = pair_left(o_row[RIGHT : RIGHT + 1], s_row[RIGHT : RIGHT + 1], lane1)
        for side, (row, before, ll) in enumerate(
            ((o_row, o_before, lefts[0]), (s_row, s_before, lefts[1]))
        ):
            rl, dl = row[RIGHT : RIGHT + 1], row[DOWN : DOWN + 1]
            ul = above(before[DOWN : DOWN + 1], dl, lane1)
            diag = row[PAD : PAD + 1] + rl + ll + dl + ul
            inv = jnp.where(diag > 0, 1.0 / diag, 0.0)
            for n, value in enumerate((diag, rl, ll, dl, ul, inv)):
                sc[side, g, n : n + 1] = value
            z = jnp.where(row[LAB : LAB + 1] == window, row[BUMP : BUMP + 1], 0.0)
            (sz_s if side else sz_o)[g] = z

    def strip_image(ref_o, ref_s, g, lane, sides):
        shape = lane.shape
        o, s = ref_o[g], ref_s[g]
        lefts, rights = pair_left(o, s, lane), pair_right(o, s, lane)
        done = []
        for side in sides:
            ref, here = (ref_s, s) if side else (ref_o, o)
            zero = jnp.zeros(shape, F32)
            up = above(ref[g - 1] if g else zero, here, lane)
            down = below(here, ref[g + 1] if g + 1 < GROUPS else zero, lane)
            c = [sc[side, g, n : n + 1] for n in range(5)]
            done.append(c[0] * here - c[1] * rights[side] - c[2] * lefts[side] - c[3] * down - c[4] * up)
        return done

    for g in range(GROUPS):
        w = strip_image(sz_o, sz_s, g, lane16, (0, 1))
        loads = (own_ref[g], mixed(g))
        for side, ref in ((0, y0_o), (1, y0_s)):
            inv = sc[side, g, 5:6]
            ref[g, 0:32] = inv * loads[side][0:32]
            ref[g, 32:48] = inv * w[side]
    for g in range(GROUPS):
        (u,) = strip_image(y0_o, y0_s, g, lane48, (1,))
        y1_s[g] = sc[1, g, 5:6] * u

    def beside(i):
        k = i + 5
        return k // 16, 125 - 8 * (k % 16)

    def coefficients(i, _):
        g, shift = beside(i)
        row = xe[i, 32:40]
        other = jnp.where(lanes((8, 128)) % 8 < 3, left_ref[g, 32:40], right_ref[g, 32:40])
        other = roll(other, shift)
        rl, dl = row[2:3], row[3:4]
        ll = roll(jnp.where(lane1 == 127, other[2:3], rl), 1)
        ul = xe[jnp.maximum(i - 1, 0), DOWN : DOWN + 1]
        diag = row[4:5] + rl + ll + dl + ul
        inv = jnp.where(diag > 0, 1.0 / diag, 0.0)
        coef_ref[i] = jnp.concatenate([diag, rl, ll, dl, ul, inv, inv, inv], axis=0)
        zs[i] = jnp.where(row[0:1] == window, row[1:2], 0.0)
        return 0

    lax.fori_loop(0, EXT, coefficients, 0, unroll=2)

    def image(ref, strip, i, lane):
        g, shift = beside(i)
        here = ref[i]
        other = roll(strip[g], shift)
        left = roll(jnp.where(lane == 127, other, here), 1)
        right = roll(jnp.where(lane == 0, other, here), 127)
        c = coef_ref[i]
        return (
            c[0:1] * here
            - c[1:2] * right
            - c[2:3] * left
            - c[3:4] * ref[i + 1]
            - c[4:5] * ref[i - 1]
        ), c[5:6]

    def first_image(i, _):
        w, inv = image(zs, sz_s, i, lane16)
        basis_ref[i, 0:16] = zs[i]
        basis_ref[i, 16:32] = w
        y0[i, 0:32] = inv * xe[i, 0:32]
        y0[i, 32:48] = inv * w
        return 0

    lax.fori_loop(1, EXT - 1, first_image, 0, unroll=2)

    def second_image(i, _):
        f1, inv = image(y0, y0_s, i, lane48)
        first_ref[i] = f1
        y1[i] = inv * f1
        return 0

    lax.fori_loop(2, EXT - 2, second_image, 0, unroll=2)

    gram[...] = jnp.zeros((48, 256), F32)

    def third_image(i, sums):
        f2, _ = image(y1, y1_s, i, lane48)
        second_ref[i - HALO] = f2
        b, f1, w = xe[i, 0:32], first_ref[i], basis_ref[i, 16:32]
        y0b, y1u = y0[i, 0:32], y1[i, 0:32]
        left = jnp.concatenate([zs[i], y0[i, 32:48], y1[i, 32:48]], axis=0)
        every = jnp.concatenate([b, w, f1, f2], axis=0)
        gram[:, 0:144] += dot(left, every, NT)
        u, uu = f1[0:32], f2[0:32]
        return (sums[0] + y0b * b, sums[1] + y0b * u, sums[2] + y1u * u, sums[3] + y1u * uu)

    zero = jnp.zeros((32, 128), F32)
    sums = lax.fori_loop(HALO, EXT - HALO, third_image, (zero, zero, zero, zero))

    a0, a1 = gram[:, 0:128], gram[:, 128:256]
    half0 = a0[16:32]
    half1 = jnp.where(lane16 < 16, a1[16:32], 0.0)
    half1 = jnp.where((lane16 >= 16) & (lane16 < 64), roll(a0[0:16], 16), half1)
    half1 = jnp.where((lane16 >= 64) & (lane16 < 96), roll(a0[32:48], 96), half1)
    half1 = jnp.where((lane16 >= 96) & (lane16 < 112), roll(a1[32:48], 96), half1)

    def relative(x, zones):
        zone = jnp.zeros((16, 128), jnp.bool_)
        for z in zones:
            zone = zone | ((lane16 >= z) & (lane16 < z + 16))
        kept = jnp.where(zone, x, 0.0)
        moved = jnp.zeros((16, 128), F32)
        for s in range(12):
            moved = jnp.where(slot == s, roll(kept, (5 - s) % 128), moved)
        return jnp.where(zone, moved, x)

    half0 = relative(half0, (32, 80))
    half1 = relative(half1, (0, 48, 96))
    eye = lax.broadcasted_iota(jnp.int32, (32, 128), 0)
    for n, total in enumerate(sums):
        column = jnp.sum(total, axis=1, keepdims=True)
        for part in range(2):
            spread = jnp.where(lanes((32, 128)) - 112 == eye - 16 * part, column, 0.0)
            line = jnp.sum(spread, axis=0, keepdims=True)
            half1 = jnp.where((slot == 2 * n + part) & (lane16 >= 112), line, half1)
    out_ref[0:12] = half0[0:12]
    out_ref[12:24] = half1[0:12]


def combine_kernel(in_ref, out_ref):
    c = lax.broadcasted_iota(jnp.int32, (8, 128), 0)
    lane = lanes((8, 128))
    for half in range(2):
        for dr in range(3):
            at = [in_ref[pl.ds(half * 12 + dr * 4 + dq, 8, stride=24), :] for dq in range(4)]
            even = at[1] + jnp.where(c >= 1, roll(at[3], 1, 0), 0.0)
            odd = at[2] + jnp.where(c < 7, roll(at[0], 7, 0), 0.0)
            if half:
                even = jnp.where(lane < 112, even, 0.0)
                odd = jnp.where(lane < 112, odd, 0.0)
                if dr == 1:
                    for s in range(8):
                        line = jnp.sum(in_ref[pl.ds(12 + s, 8, stride=24), :], axis=0, keepdims=True)
                        even = jnp.where((c == s) & (lane >= 112), line, even)
            base = half * 48 + dr * 8
            out_ref[base : base + 8] = even
            out_ref[base + 24 : base + 32] = odd


def batched_inverse(a, lane, row):
    base = lane - lane % 16
    for k in range(16):
        at_k = lane % 16 == k
        column = jnp.take_along_axis(a, base + k, axis=1)
        pivot = column[k : k + 1]
        line = jnp.where(at_k[0:1], 1.0, a[k : k + 1]) / pivot
        a = jnp.where(row == k, line, jnp.where(at_k, 0.0, a) - column * line)
    return a


def block_inverse(matrix, low, high):
    lane = lanes((16, 128))
    row = lax.broadcasted_iota(jnp.int32, (16, 128), 0)
    compact = jnp.where(lane % 16 == row, 1.0, 0.0)
    for n in range(low // 16, high // 16):
        compact = jnp.where(lane // 16 == n, matrix[16 * n : 16 * n + 16], compact)
    compact = batched_inverse(compact, lane, row)
    parts = []
    for n in range(8):
        active = low <= 16 * n < high
        parts.append(jnp.where(lane // 16 == n, compact, 0.0) if active else jnp.zeros((16, 128), F32))
    return jnp.concatenate(parts, axis=0)


def coarse_kernel(place_ref, in_ref, out_ref, g0, g1, e, ei, va, vb, mw, mt, ms, mz):
    pr, pc = place_ref[0], place_ref[1]
    lane8 = lanes((8, 128))
    sub8 = lax.broadcasted_iota(jnp.int32, (8, 128), 0)

    def at(p, par):
        return POS[p] * 16 + par * 8

    for half, ref in ((0, g0), (1, g1)):
        for par in range(2):
            for p in range(16):
                total = None
                for dr in range(3):
                    r = p + 1 - dr
                    if 0 <= r < 16:
                        base = half * 48 + par * 24 + dr * 8
                        piece = in_ref[r, base : base + 8]
                        total = piece if total is None else total + piece
                ref[at(p, par) : at(p, par) + 8] = total

    tally = g1[at(0, 0) : at(0, 0) + 8]
    for p in range(1, 16):
        tally = tally + g1[at(p, 0) : at(p, 0) + 8]

    def total_of(n):
        low = roll(tally[2 * n : 2 * n + 1], 16)
        high = roll(tally[2 * n + 1 : 2 * n + 2], 32)
        return jnp.where(lanes((1, 128)) < 16, low, high)

    bb, bu, uu, uuu = (total_of(n) for n in range(4))

    for p in range(16):
        for par in range(2):
            tile = g1[at(p, par) : at(p, par) + 8]
            halves = [jnp.zeros((8, 128), F32), jnp.zeros((8, 128), F32)]
            for dp in (-1, 0, 1):
                if not 0 <= p + dp < 16:
                    continue
                for dq in (-1, 0, 1):
                    l = 48 + 5 + 4 * dp + dq
                    other = par if dq == 0 else 1 - par
                    step = 0 if dq == 0 else ((dq - 1) // 2 if par == 0 else (dq + 1) // 2)
                    target = at(p + dp, other)
                    h, off = target // 128, target % 128
                    hit = (lane8 - off == sub8 + step) & (sub8 + step >= 0) & (sub8 + step < 8)
                    value = jnp.broadcast_to(tile[:, l : l + 1], (8, 128))
                    halves[h] = jnp.where(hit, value, halves[h])
            e[at(p, par) : at(p, par) + 8, 0:128] = halves[0]
            e[at(p, par) : at(p, par) + 8, 128:256] = halves[1]

    lane = lanes((128, 128))
    row = lax.broadcasted_iota(jnp.int32, (128, 128), 0)
    outer = block_inverse(e[0:128, 0:128], 0, 128)
    across = dot(outer, e[0:128, 128:256])
    schur = e[128:256, 128:256] - dot(e[128:256, 0:128], across)
    steps = []
    for low, high in ((0, 64), (64, 96), (96, 112)):
        inv = block_inverse(schur, low, high)
        link = jnp.where((row >= low) & (row < high) & (lane >= high), schur, 0.0)
        x = dot(inv, link)
        keep = jnp.where((row >= high) & (lane >= high), schur, 0.0)
        schur = keep - dot(link, x, TN)
        steps.append((inv, jnp.where((row == lane) & (row >= high), 1.0, 0.0) - x))
    inner = block_inverse(schur, 112, 128)
    for inv, y in reversed(steps):
        inner = inv + dot(dot(y, inner), y, NT)
    half = dot(across, inner)
    ei[0:128, 0:128] = outer + dot(half, across, NT)
    ei[0:128, 128:256] = -half
    ei[128:256, 0:128] = -half.T
    ei[128:256, 128:256] = inner

    def solve(z):
        return dot(ei[...], z)

    def apply(ref, zone, v_ref):
        sides = {}
        for p in range(16):
            even, odd = v_ref[at(p, 0) : at(p, 0) + 8], v_ref[at(p, 1) : at(p, 1) + 8]
            sides[p, 0] = (roll(odd, 1, 0), even, odd)
            sides[p, 1] = (even, odd, roll(even, 7, 0))
        tiles = {}
        for p in range(16):
            for par in range(2):
                tile = ref[at(p, par) : at(p, par) + 8]
                total = None
                for dp in (-1, 0, 1):
                    if not 0 <= p + dp < 16:
                        continue
                    for n in range(3):
                        l = zone + 5 + 4 * dp + n - 1
                        term = tile[:, l : l + 1] * sides[p + dp, par][n]
                        total = term if total is None else total + term
                tiles[POS[p] * 2 + par] = total
        return jnp.concatenate([tiles[n] for n in range(32)], axis=0)

    def inner_product(a, b):
        return jnp.sum(a * b, axis=0, keepdims=True)

    wb = g0[...]
    wu = roll(g0[...], 80)
    wuu = roll(g0[...], 32)
    zb = roll(g1[...], 112)
    tuu = roll(g1[...], 64)
    c0 = solve(zb)
    va[...] = c0
    f_c = apply(g0, 32, va)
    g_c = apply(g0, 80, va)
    h_c = apply(g1, 0, va)
    k_c = apply(g1, 96, va)
    grad0 = wb - f_c
    k0 = solve(grad0)
    vb[...] = k0
    f_k = apply(g0, 32, vb)
    g_k = apply(g0, 80, vb)
    rho0 = bb - 2.0 * inner_product(c0, wb) + inner_product(c0, f_c)
    energy0 = bu - 2.0 * inner_product(c0, wu) + inner_product(c0, g_c)
    curve0 = energy0 - inner_product(k0, grad0)
    a0 = rho0 / curve0
    e1 = c0 - a0 * k0
    f_e = f_c - a0 * f_k
    g_e = g_c - a0 * g_k
    grad1 = wb - f_e + a0 * (g_c - wu)
    k1 = solve(grad1)

    def second_norm(m0, m1, m2, v0, v1, v2, e_image, c_image, last):
        own = m0 - 2.0 * inner_product(e1, v0) + inner_product(e1, e_image)
        mixed = m1 - inner_product(c0, v1) - inner_product(e1, v1) + inner_product(e1, c_image)
        far = m2 - 2.0 * inner_product(c0, v2) + inner_product(c0, last)
        return own - 2.0 * a0 * mixed + a0 * a0 * far

    rho1 = second_norm(bb, bu, uu, wb, wu, wuu, f_e, g_c, h_c)
    energy1 = second_norm(bu, uu, uuu, wu, wuu, tuu, g_e, h_c, k_c)
    beta = rho1 / rho0
    cross = inner_product(e1, wu)
    s1q0 = (
        bu
        - inner_product(c0, wu)
        - cross
        + inner_product(e1, g_c)
        - a0 * (uu - 2.0 * inner_product(c0, wuu) + inner_product(c0, h_c))
        - inner_product(k0, grad1)
    )
    curve1 = energy1 - inner_product(k1, grad1) + 2.0 * beta * s1q0 + beta * beta * curve0
    a1 = rho1 / curve1

    ab = a1 * beta
    w_res = a1 * k1 + ab * k0 - e1
    t_res = (a0 + ab) * c0 + a1 * e1
    s_res = -(a1 * a0) * c0
    w_sol = -(a0 + ab) * c0 - a1 * e1
    t_sol = (a1 * a0) * c0
    z_sol = c0 - (a0 + ab) * k0 - a1 * k1
    big = lanes((256, 128))

    def joined(first, second):
        return jnp.where(big < 32, first, jnp.where(big < 64, roll(second, 32), 0.0))

    found = (
        (mz, jnp.where((big >= 64) & (big < 96), roll(z_sol, 64), 0.0)),
        (mw, joined(w_res, w_sol)),
        (mt, joined(t_res, t_sol)),
        (ms, jnp.where(big < 32, s_res, 0.0)),
    )
    for ref, value in found:
        for p in range(16):
            ref[16 * p : 16 * p + 16] = value[16 * POS[p] : 16 * POS[p] + 16]
    for n, (ref, _) in enumerate(found):
        for dr in range(3):
            p = jnp.clip(pr - 1 + dr, 0, 15)
            for dq in range(4):
                par = (dq + 1) % 2
                c = jnp.clip(pc - 1 + (dq + 1) // 2, 0, 7)
                k = 16 * n + 4 * dr + dq
                out_ref[k : k + 1] = ref[pl.ds(p * 16 + par * 8 + c, 1), :]
        out_ref[16 * n + 12 : 16 * n + 16] = jnp.zeros((4, 128), F32)
    out_ref[64:65] = -a0 - a1 - ab
    out_ref[65:66] = a1 * a0
    out_ref[66:67] = a0 + ab + a1
    out_ref[67:68] = -(a1 * a0)
    out_ref[68:72] = jnp.zeros((4, 128), F32)


def outputs_kernel(x_ref, first_ref, second_ref, basis_ref, coef_ref, m_ref, sol_ref, res_ref):
    m = jnp.concatenate([m_ref[...], jnp.zeros((56, 128), F32)], axis=0).T
    left = m[0:96, 0:64]
    shape = (32, 128)
    p1, p2, p3, p4 = (jnp.broadcast_to(m[0:32, 64 + n : 65 + n], shape) for n in range(4))

    def step(r, _):
        i = r + HALO
        b, f1, f2 = x_ref[r, 0:32], first_ref[i], second_ref[r]
        u, uu = f1[0:32], f2[0:32]
        rows = jnp.concatenate([basis_ref[i], f1[32:48], f2[32:48]], axis=0)
        d = dot(left, rows)
        inv = coef_ref[i, 5:6]
        res_ref[r] = b + p1 * u + p2 * uu + d[0:32]
        sol_ref[r] = inv * (p3 * b + p4 * u + d[32:64]) + d[64:96]
        return 0

    lax.fori_loop(0, 128, step, 0, unroll=2)


def from_everyone(value, axis):
    count = lax.axis_size(axis)
    return lax.all_to_all(jnp.broadcast_to(value[None], (count, *value.shape)), axis, 0, 0, tiled=True)


def lookup(entries, classes):
    levels = lax.broadcasted_iota(jnp.int32, (entries.shape[0],) + classes.shape, 0)
    return jnp.sum(jnp.where(classes[None] == levels, entries[:, None, None], 0.0), axis=0)


def shape_of(*dims):
    return jax.ShapeDtypeStruct(dims, F32)


def vmem(*dims):
    return pltpu.VMEM(dims, F32)


def body(load_currents, labels, bump_height, horizontal_class, vertical_class, pad_class, edge_table, pad_table):
    pr, pc = lax.axis_index(ROW), lax.axis_index(COL)
    rows, cols = lax.axis_size(ROW), lax.axis_size(COL)
    place = jnp.stack([pr, pc]).astype(jnp.int32)
    row_ids = lax.broadcasted_iota(jnp.int32, labels.shape, 0)
    col_ids = lax.broadcasted_iota(jnp.int32, labels.shape, 1)
    right_link = jnp.where((col_ids == 127) & (pc == cols - 1), 0.0, lookup(edge_table, horizontal_class))
    down_link = jnp.where((row_ids == 127) & (pr == rows - 1), 0.0, lookup(edge_table, vertical_class))
    pad = lookup(pad_table, pad_class)
    zero = jnp.zeros_like(pad)
    params = jnp.stack(
        [labels.astype(F32), bump_height, right_link, down_link, pad, zero, zero, zero], axis=1
    )
    x = jnp.concatenate([jnp.transpose(load_currents, (1, 0, 2)), params], axis=1)
    down = [(i, i + 1) for i in range(rows - 1)]
    top = lax.ppermute(x[-HALO:], ROW, down)
    bottom = lax.ppermute(x[:HALO], ROW, [(b, a) for a, b in down])
    own = pl.pallas_call(
        pack_kernel, out_shape=shape_of(GROUPS, SUB, 128), in_specs=[whole] * 3, out_specs=whole
    )(x, top, bottom)
    right = [(i, i + 1) for i in range(cols - 1)]
    beside_left = lax.ppermute(own, COL, right)
    beside_right = lax.ppermute(own, COL, [(b, a) for a, b in right])
    first, second, basis, coef, payload = pl.pallas_call(
        fields_kernel,
        out_shape=(
            shape_of(EXT, 48, 128),
            shape_of(128, 48, 128),
            shape_of(EXT, 32, 128),
            shape_of(EXT, 8, 128),
            shape_of(24, 128),
        ),
        in_specs=[scalars] + [whole] * 6,
        out_specs=(whole,) * 5,
        scratch_shapes=[
            vmem(EXT, SUB, 128),
            vmem(GROUPS, 16, 128),
            vmem(GROUPS, 16, 128),
            vmem(GROUPS, 48, 128),
            vmem(GROUPS, 48, 128),
            vmem(GROUPS, 48, 128),
            vmem(2, GROUPS, 8, 128),
            vmem(EXT, 16, 128),
            vmem(EXT, 48, 128),
            vmem(EXT, 48, 128),
            vmem(48, 256),
        ],
    )(place, x, top, bottom, own, beside_left, beside_right)
    in_row = from_everyone(payload, COL).reshape(-1, 128)
    combined = pl.pallas_call(
        combine_kernel, out_shape=shape_of(96, 128), in_specs=[whole], out_specs=whole
    )(in_row)
    everything = from_everyone(combined, ROW)
    matrix = pl.pallas_call(
        coarse_kernel,
        out_shape=shape_of(72, 128),
        in_specs=[scalars, whole],
        out_specs=whole,
        scratch_shapes=[vmem(256, 128), vmem(256, 128), vmem(256, 256), vmem(256, 256)]
        + [vmem(256, 128)] * 6,
    )(place, everything)
    solution, residual = pl.pallas_call(
        outputs_kernel,
        out_shape=(shape_of(128, 32, 128), shape_of(128, 32, 128)),
        in_specs=[whole] * 6,
        out_specs=(whole, whole),
    )(x, first, second, basis, coef, matrix)
    return jnp.transpose(solution, (1, 0, 2)), jnp.transpose(residual, (1, 0, 2))


def solution(mesh):
    finer = Mesh(mesh.devices.reshape(4, 4, 4, 2), ("row_0", "row_1", "col_0", "col_1"))
    grid = P(ROW, COL)
    return jax.shard_map(
        body,
        mesh=finer,
        in_specs=(P(None, ROW, COL), grid, grid, grid, grid, grid, P(), P()),
        out_specs=(P(None, ROW, COL), P(None, ROW, COL)),
        check_vma=False,
    )
```

time: 533 us -> 201 us (0.38); the launches traced: 522 us -> 200 us
  matrix products: 180 us -> 0 us
  Pallas kernels: 0 us -> 127 us
  other arithmetic: 110 us -> 2.01 us
  blocking collectives: 102 us -> 34.4 us
  starting transfers between devices: 67.4 us -> 12.8 us
  local copies, waits for them, and re-layouts: 42.9 us -> 18.8 us
  waiting for transfers between devices: 17 us -> 3.37 us
    dot_general x13 -> x0, matrix products: 178 us -> none  [the longest x3 56.2 us: expand(): jnp.dot(coarse, basis_flat, precision=precise)]
    pallas_call x0 -> x5, Pallas kernels: none -> 127 us  [the longest x1 87.1 us: body(): pl.pallas_call(fields_kernel, out_shape=(shape_of(EXT, 48, 128), shape_of...]
    all_to_all x10 -> x2, blocking collectives: 102 us -> 34.4 us  [from_everyone(): lax.all_to_all(jnp.broadcast_to(value[None], (count, *value.shape)), axis...]
    another operation x9 -> x1, other arithmetic: 54.1 us -> 0.65 us  [body(): place = jnp.stack([pr, pc]).astype(jnp.int32)]
    sub x4 -> x0, other arithmetic: 44.4 us -> none  [the longest x3 42.3 us: stencil(): diagonal * centre - right_link * padded[:, 1:-1, 2:]]
    all_to_all x4 -> x0, starting transfers between devices: 29.4 us -> none  [the longest x3 16.9 us: from_everyone(): lax.all_to_all(jnp.broadcast_to(value[None], (length, *value.shape)), axi...]
    ppermute x14 -> x4, starting transfers between devices: 38 us -> 12.8 us  [the longest x1 4.99 us: body(): top = lax.ppermute(x[-HALO:], ROW, down)]
    slice x14 -> x1, local copies, waits for them, and re-layouts: 16.6 us -> 0.01 us  [body(): bottom = lax.ppermute(x[:HALO], ROW, [(b, a) for a, b in down])]
  transfers between devices with their start and end apart: 18 -> 4, of which waited for: 4 -> 3; matrix products, arithmetic and copies ran while one was open for 19% -> 0% of each run, Pallas kernels for 0% -> 0%
where the time goes in v1:
time: 201 us; the launch traced here: 200 us
  Pallas kernels  127 us (63%)
  blocking collectives  34.4 us (17%)
  local copies, waits for them, and re-layouts  18.8 us (9%)
  starting transfers between devices  12.8 us (6%)
  waiting for transfers between devices  3.37 us (2%)
    pallas_call x1, Pallas kernels, body(): pl.pallas_call(fields_kernel, out_shape=(shape_of(EXT, 48, 128), shape_of...  87.1 us
    all_to_all x2, blocking collectives, from_everyone(): lax.all_to_all(jnp.broadcast_to(value[None], (count, *value.shape)), axis...  34.4 us
    pallas_call x1, Pallas kernels, body(): pl.pallas_call(outputs_kernel, out_shape=(shape_of(128, 32, 128), shape_o...  21.4 us
    pallas_call x1, Pallas kernels, body(): pl.pallas_call(coarse_kernel, out_shape=shape_of(72, 128), in_specs=[scal...  14.3 us
    unnamed x27, local copies, waits for them, and re-layouts  12.4 us
    ppermute x1, starting transfers between devices, body(): top = lax.ppermute(x[-HALO:], ROW, down)  4.99 us
    concatenate x2, local copies, waits for them, and re-layouts, body(): jnp.concatenate([jnp.transpose(load_currents, (1, 0, 2)), params], axis=1)  4.81 us
  transfers between devices with their start and end apart: 4, of which 3 were waited for; matrix products, arithmetic and copies ran while one was open for 0% of the time, Pallas kernels for 0%

profile of v1, /device:TPU:1, one launch (start us, length us, event | category | flops | bytes accessed | tf_op | source)
XLA Modules:
  0.0 199.8 jit_solution(3303671714301097952)
XLA Ops:
  0.7 0.8 convert_element_type.3
  1.6 4.2 %copy.17 = f32[32,128,128]{2,0,1:T(8,128)} copy(f32[32,128,128]{2,1,0:T(8,128)} %param.8) | data formatting | bytes 4194304 | tf_op args[0]
  6.5 4.8 %concatenate.7.x_ref = f32[128,40,128]{2,1,0:T(8,128)S(1)} concatenate(f32[128,32,128]{2,1,0:T(8,128)} %bitcast.13, f32[128,1,128]{2,1,0:T(1,128)S(1)} %bitcast.17, f32[128,1,128]{2,1,0:T(1,128)S(1)} %bitcast.21, f32[128,1,128]{2,1,0:T(1,128)S(1)} %get-tuple-element.25, f32[128,1,128]{2,1,0:T(1,128)S(1)} %get-tuple-element.24, f32[128,1,128]{2,1,0:T(1,128)S(1)} %bitcast.18, ...), dimensions={1} | concatenate | bytes 5242880 | tf_op jit(solution)/shard_map/concatenate | solution.py:523
  11.3 1.3 collective-permute-start.1
  12.6 5.0 %collective-permute-start = (f32[3,40,128]{2,1,0:T(8,128)S(1)}, f32[3,40,128]{2,1,0:T(8,128)S(1)}, u32[]{:S(2)}, u32[]{:S(2)}) collective-permute-start(f32[3,40,128]{2,1,0:T(8,128)S(1)} %get-tuple-element.23), channel_id=1, source_target_pairs={{0,8},{8,16},{16,24},{24,32},{32,40},{40,48},{48,56},{56,64},{64,7... | collective-permute-start | bytes 184328 | tf_op jit(solution)/shard_map/ppermute | solution.py:525
  17.6 1.3 collective-permute-done.top_ref
  18.8 0.6 copy-done.3
  19.5 3.2 %shard_map.95.own_ref = f32[9,40,128]{2,1,0:T(8,128)} custom-call(f32[128,40,128]{2,1,0:T(8,128)} %copy-done, f32[3,40,128]{2,1,0:T(8,128)} %copy-done.3, f32[3,40,128]{2,1,0:T(8,128)} %copy-done.2), custom_call_target="tpu_custom_call" | custom-call | tf_op jit(solution)/shard_map/pallas_call | solution.py:527
  22.7 3.4 %collective-permute-start.3 = (f32[9,40,128]{2,1,0:T(8,128)}, f32[9,40,128]{2,1,0:T(8,128)S(1)}, u32[]{:S(2)}, u32[]{:S(2)}) collective-permute-start(f32[9,40,128]{2,1,0:T(8,128)} %shard_map.95.own_ref), channel_id=1, source_target_pairs={{1,0},{2,1},{3,2},{4,3},{5,4},{6,5},{7,6},{9,8},{10,9},{11,10},{12... | collective-permute-start | bytes 552968 | tf_op jit(solution)/shard_map/ppermute | solution.py:532
  26.1 3.1 %collective-permute-start.2 = (f32[9,40,128]{2,1,0:T(8,128)}, f32[9,40,128]{2,1,0:T(8,128)S(1)}, u32[]{:S(2)}, u32[]{:S(2)}) collective-permute-start(f32[9,40,128]{2,1,0:T(8,128)} %shard_map.95.own_ref), channel_id=1, source_target_pairs={{0,1},{1,2},{2,3},{3,4},{4,5},{5,6},{6,7},{8,9},{9,10},{10,11},{11... | collective-permute-start | bytes 552968 | tf_op jit(solution)/shard_map/ppermute | solution.py:531
  29.2 0.7 pad_add_fusion.place_ref
  29.9 0.8 collective-permute-done.3.right_ref
  30.7 1.3 collective-permute-done.2.left_ref
  32.0 0.7 copy-done.5
  32.7 87.1 %shard_map.96 = (f32[134,48,128]{2,1,0:T(8,128)}, f32[128,48,128]{2,1,0:T(8,128)}, f32[134,32,128]{2,1,0:T(8,128)}, f32[134,8,128]{2,1,0:T(8,128)}, f32[24,128]{1,0:T(8,128)}) custom-call(s32[2]{0:T(128)} %pad_add_fusion.place_ref, f32[128,40,128]{2,1,0:T(8,128)} %copy-done, f32[3,40,128]{2,1,0:T(8,128)} %copy-done.3, f32[3,40,128]{2,1,0:T(8,128)} %copy-done.2, ...), custom_call_target="tpu_custom_call" | custom-call | tf_op jit(solution)/shard_map/pallas_call | solution.py:533
  119.7 0.7 broadcast_in_dim.49
  120.5 10.4 %all_to_all.10 = f32[8,24,128]{2,1,0:T(8,128)} all-to-all(f32[8,24,128]{2,1,0:T(8,128)S(1)} %broadcast_in_dim.49), channel_id=1, replica_groups=mesh['row_0'=4,'row_1'=4,'col_0'=4,'col_1'=2] {'col_0','col_1'}, dimensions={0} | all-to-all | bytes 196608 | tf_op jit(solution)/shard_map/all_to_all | solution.py:494
  130.9 1.5 shard_map.97
  132.4 0.9 broadcast_in_dim.50
  133.3 24.0 %all_to_all.11.in_ref = f32[16,96,128]{2,1,0:T(8,128)} all-to-all(f32[16,96,128]{2,1,0:T(8,128)S(1)} %broadcast_in_dim.50), channel_id=1, replica_groups=mesh['row_0'=4,'row_1'=4,'col_0'=4,'col_1'=2] {'row_0','row_1'}, dimensions={0} | all-to-all | bytes 1572864 | tf_op jit(solution)/shard_map/all_to_all | solution.py:494
  157.3 14.3 %shard_map.98.m_ref = f32[72,128]{1,0:T(8,128)} custom-call(s32[2]{0:T(128)} %pad_add_fusion.place_ref, f32[16,96,128]{2,1,0:T(8,128)} %all_to_all.11.in_ref), custom_call_target="tpu_custom_call" | custom-call | tf_op jit(solution)/shard_map/pallas_call | solution.py:563
  171.6 21.4 %shard_map.99 = (f32[128,32,128]{2,1,0:T(8,128)}, f32[128,32,128]{2,1,0:T(8,128)}) custom-call(f32[128,40,128]{2,1,0:T(8,128)} %copy-done, f32[134,48,128]{2,1,0:T(8,128)} %get-tuple-element.9.first_ref, f32[128,48,128]{2,1,0:T(8,128)} %get-tuple-element.10.second_ref, f32[134,32,128]{2,1,0:T(8,128)} %get-tuple-element.11.basis_ref, ...), custom_call_target="tpu_custom_call" | custom-call | tf_op jit(solution)/shard_map/pallas_call | solution.py:571
  192.9 4.3 %copy.14 = f32[32,128,128]{2,1,0:T(8,128)} copy(f32[32,128,128]{2,0,1:T(8,128)} %bitcast.15) | data formatting | bytes 4194304
  197.2 2.5 %copy.15 = f32[32,128,128]{2,1,0:T(8,128)} copy(f32[32,128,128]{2,0,1:T(8,128)S(1)} %bitcast.14) | data formatting | bytes 4194304
  (31 shorter events, 0.6 us)
Async XLA Ops:
  1.5 4.3 %copy-start.7 = (s32[128,128]{1,0:T(8,128)S(1)}, s32[128,128]{1,0:T(8,128)}, u32[]{:S(2)}) copy-start(s32[128,128]{1,0:T(8,128)} %param.13) | copy-start | bytes 196612
  1.5 4.3 %copy-start.10 = (f32[8]{0:T(128)S(1)}, f32[8]{0:T(128)}, u32[]{:S(2)}) copy-start(f32[8]{0:T(128)} %param.15) | copy-start | bytes 100
  1.5 4.4 %copy-start.8 = (s32[128,128]{1,0:T(8,128)S(1)}, s32[128,128]{1,0:T(8,128)}, u32[]{:S(2)}) copy-start(s32[128,128]{1,0:T(8,128)} %param.12) | copy-start | bytes 196612
  1.5 4.4 %copy-start.9 = (s32[128,128]{1,0:T(8,128)S(1)}, s32[128,128]{1,0:T(8,128)}, u32[]{:S(2)}) copy-start(s32[128,128]{1,0:T(8,128)} %param.11) | copy-start | bytes 196612
  1.6 4.4 %copy-start.11 = (f32[8]{0:T(128)S(1)}, f32[8]{0:T(128)}, u32[]{:S(2)}) copy-start(f32[8]{0:T(128)} %param.14) | copy-start | bytes 100
  1.6 4.9 %copy-start.6 = (f32[128,128]{1,0:T(8,128)S(1)}, f32[128,128]{1,0:T(8,128)}, u32[]{:S(2)}) copy-start(f32[128,128]{1,0:T(8,128)} %param.10) | copy-start | bytes 196612
  11.2 7.6 %copy-start = (f32[128,40,128]{2,1,0:T(8,128)}, f32[128,40,128]{2,1,0:T(8,128)S(1)}, u32[]{:S(2)}) copy-start(f32[128,40,128]{2,1,0:T(8,128)S(1)} %concatenate.7.x_ref) | copy-start | bytes 7864324
  11.3 6.3 %collective-permute-start.1 = (f32[3,40,128]{2,1,0:T(8,128)S(1)}, f32[3,40,128]{2,1,0:T(8,128)S(1)}, u32[]{:S(2)}, u32[]{:S(2)}) collective-permute-start(f32[3,40,128]{2,1,0:T(8,128)S(1)} %get-tuple-element.22), channel_id=1, source_target_pairs={{8,0},{16,8},{24,16},{32,24},{40,32},{48,40},{56,48},{64,56},{72,6... | collective-permute-start | bytes 184328 | tf_op jit(solution)/shard_map/ppermute | solution.py:526
  12.6 6.3 %collective-permute-start = (f32[3,40,128]{2,1,0:T(8,128)S(1)}, f32[3,40,128]{2,1,0:T(8,128)S(1)}, u32[]{:S(2)}, u32[]{:S(2)}) collective-permute-start(f32[3,40,128]{2,1,0:T(8,128)S(1)} %get-tuple-element.23), channel_id=1, source_target_pairs={{0,8},{8,16},{16,24},{24,32},{32,40},{40,48},{48,56},{56,64},{64,7... | collective-permute-start | bytes 184328 | tf_op jit(solution)/shard_map/ppermute | solution.py:525
  17.6 1.3 copy-start.2
  18.8 0.6 copy-start.3
  22.7 8.0 %collective-permute-start.3 = (f32[9,40,128]{2,1,0:T(8,128)}, f32[9,40,128]{2,1,0:T(8,128)S(1)}, u32[]{:S(2)}, u32[]{:S(2)}) collective-permute-start(f32[9,40,128]{2,1,0:T(8,128)} %shard_map.95.own_ref), channel_id=1, source_target_pairs={{1,0},{2,1},{3,2},{4,3},{5,4},{6,5},{7,6},{9,8},{10,9},{11,10},{12... | collective-permute-start | bytes 552968 | tf_op jit(solution)/shard_map/ppermute | solution.py:532
  26.1 5.9 %collective-permute-start.2 = (f32[9,40,128]{2,1,0:T(8,128)}, f32[9,40,128]{2,1,0:T(8,128)S(1)}, u32[]{:S(2)}, u32[]{:S(2)}) collective-permute-start(f32[9,40,128]{2,1,0:T(8,128)} %shard_map.95.own_ref), channel_id=1, source_target_pairs={{0,1},{1,2},{2,3},{3,4},{4,5},{5,6},{6,7},{8,9},{9,10},{10,11},{11... | collective-permute-start | bytes 552968 | tf_op jit(solution)/shard_map/ppermute | solution.py:531
  30.7 1.3 copy-start.4
  32.0 0.7 copy-start.5
  192.9 4.3 %copy-start.1 = (f32[128,32,128]{2,1,0:T(8,128)S(1)}, f32[128,32,128]{2,1,0:T(8,128)}, u32[]{:S(2)}) copy-start(f32[128,32,128]{2,1,0:T(8,128)} %get-tuple-element.15) | copy-start | bytes 6291460

commit v2 on v1

--- a/solution.py
+++ b/solution.py
@@ -15,7 +15,6 @@
 LAB, BUMP, RIGHT, DOWN, PAD = 32, 33, 34, 35, 36
 SUB = 40
 HALO = 3
-EXT = 134
 GROUPS = 9
 ORDER = (1, 3, 5, 7, 9, 11, 13, 15, 2, 6, 10, 14, 4, 12, 8, 0)
 POS = tuple(ORDER.index(p) for p in range(16))
@@ -30,6 +29,19 @@
     return lax.dot_general(a, b, dims, precision=precise, preferred_element_type=F32)
 
 
+def parts_of(x, count):
+    parts = []
+    for n in range(count):
+        parts.append(x.astype(jnp.bfloat16))
+        if n + 1 < count:
+            x = x - parts[-1].astype(F32)
+    return parts
+
+
+def fast_dot(a, b, dims=NN):
+    return lax.dot_general(a, b, dims, preferred_element_type=F32)
+
+
 def lanes(shape):
     return lax.broadcasted_iota(jnp.int32, shape, len(shape) - 1)
 
@@ -38,43 +50,92 @@
     return pltpu.roll(x, shift, axis)
 
 
-def pack_kernel(x_ref, top_ref, bottom_ref, out_ref):
-    lane = lanes((SUB, 128))
+def prepare_kernel(
+    place_ref, edge_ref, pad_ref, load_ref, label_ref, bump_ref, across_ref, down_ref, pad_class_ref,
+    grid_ref, first_ref,
+):
+    pr, pc = place_ref[0], place_ref[1]
+    shape = (128, 128)
+    row, lane = lax.broadcasted_iota(jnp.int32, shape, 0), lanes(shape)
+
+    def lookup(table, classes):
+        found = jnp.zeros(shape, F32)
+        for n in range(8):
+            found = jnp.where(classes == n, table[n], found)
+        return found
+
+    right = lookup(edge_ref, across_ref[...])
+    down = lookup(edge_ref, down_ref[...])
+    grid_ref[0:128] = label_ref[...].astype(F32)
+    grid_ref[128:256] = bump_ref[...]
+    grid_ref[256:384] = jnp.where((lane == 127) & (pc == 7), 0.0, right)
+    grid_ref[384:512] = jnp.where((row == 127) & (pr == 15), 0.0, down)
+    grid_ref[512:640] = lookup(pad_ref, pad_class_ref[...])
+    grid_ref[640:1024] = jnp.zeros((384, 128), F32)
+    for n in range(HALO):
+        first_ref[n, 0:32] = load_ref[pl.ds(n, 32, stride=128), :]
+        first_ref[n, 32:40] = grid_ref[pl.ds(n, 8, stride=128), :]
+
+
+def pack_kernel(load_ref, grid_ref, rows_ref, own_ref, last_ref):
+    lane = lanes((32, 128)) // 8
+
+    def group(g, slots):
+        loads, rest = jnp.zeros((32, 128), F32), jnp.zeros((8, 128), F32)
+        for s in slots:
+            r = 16 * g - 8 + s
+            b = load_ref[pl.ds(r, 32, stride=128), :]
+            rows_ref[r] = b
+            loads = jnp.where(lane == s, roll(b, (8 * s + 3) % 128), loads)
+            rest = jnp.where(lane[0:8] == s, roll(grid_ref[pl.ds(r, 8, stride=128), :], (8 * s + 3) % 128), rest)
+        own_ref[g, 0:32] = loads
+        own_ref[g, 32:40] = rest
+
+    group(0, range(8, 16))
+    group(8, range(8))
+
+    def step(g, _):
+        group(g, range(16))
+        return 0
+
+    lax.fori_loop(1, 8, step, 0)
+    for n in range(HALO):
+        r = 128 - HALO + n
+        last_ref[n, 0:32] = rows_ref[r]
+        last_ref[n, 32:40] = grid_ref[pl.ds(r, 8, stride=128), :]
+
+
+def corner_kernel(own_ref, top_ref, bottom_ref, out_ref):
+    lane = lanes((SUB, 128)) // 8
     for g in range(GROUPS):
-        acc = jnp.zeros((SUB, 128), F32)
-        for s in range(16):
-            r = 16 * g - 8 + s
-            if r < -HALO or r >= 128 + HALO:
-                continue
-            if r < 0:
-                row = top_ref[r + HALO]
-            elif r < 128:
-                row = x_ref[r]
-            else:
-                row = bottom_ref[r - 128]
-            acc = jnp.where(lane // 8 == s, roll(row, (8 * s + 3) % 128), acc)
-        out_ref[g] = acc
+        out_ref[g] = own_ref[g]
+    start, end = own_ref[0], own_ref[8]
+    for n in range(HALO):
+        s = 8 - HALO + n
+        start = jnp.where(lane == s, roll(top_ref[n], (8 * s + 3) % 128), start)
+        s = 8 + n
+        end = jnp.where(lane == s, roll(bottom_ref[n], (8 * s + 3) % 128), end)
+    out_ref[0] = start
+    out_ref[8] = end
 
 
 def fields_kernel(
-    place_ref, x_ref, top_ref, bottom_ref, own_ref, left_ref, right_ref,
-    first_ref, second_ref, basis_ref, coef_ref, out_ref,
-    xe, sz_o, sz_s, y0_o, y0_s, y1_s, sc, zs, y0, y1, gram,
+    place_ref, rows_ref, grid_ref, top_ref, bottom_ref, own_ref, left_ref, right_ref,
+    first_ref, second_ref, w_ref, coef_ref, out_ref,
+    ext, sz_o, sz_s, y0_o, y0_s, y1_s, sc, y0, y1, gram,
 ):
     pr, pc = place_ref[0], place_ref[1]
     lane1 = lanes((1, 128))
     lane16 = lanes((16, 128))
     lane48 = lanes((48, 128))
 
-    for i in range(HALO):
-        xe[i] = top_ref[i]
-        xe[EXT - HALO + i] = bottom_ref[i]
-
-    def copy_rows(i, _):
-        xe[i + HALO] = x_ref[i]
-        return 0
-
-    lax.fori_loop(0, 128, copy_rows, 0, unroll=4)
+    for n in range(5):
+        ext[n, 0:16] = jnp.zeros((16, 128), F32)
+        ext[n, 16:144] = grid_ref[128 * n : 128 * n + 128]
+        ext[n, 144:160] = jnp.zeros((16, 128), F32)
+        for k in range(HALO):
+            ext[n, 16 - HALO + k : 17 - HALO + k] = top_ref[k, 32 + n : 33 + n]
+            ext[n, 144 + k : 145 + k] = bottom_ref[k, 32 + n : 33 + n]
 
     slot = lax.broadcasted_iota(jnp.int32, (16, 128), 0)
     region_row = pr - 1 + slot // 4
@@ -117,6 +178,18 @@
             z = jnp.where(row[LAB : LAB + 1] == window, row[BUMP : BUMP + 1], 0.0)
             (sz_s if side else sz_o)[g] = z
 
+        at = 16 * g + 8
+        beside = jnp.zeros((16, 128), F32)
+        for s in range(16):
+            beside = jnp.where(slot == s, roll(s_row[RIGHT : RIGHT + 1], 125 - 8 * s), beside)
+        rl, dl = ext[2, at : at + 16], ext[3, at : at + 16]
+        ll = roll(jnp.where(lane16 == 127, beside, rl), 1)
+        ul = ext[3, at - 1 : at + 15]
+        diag = ext[4, at : at + 16] + rl + ll + dl + ul
+        inv = jnp.where(diag > 0, 1.0 / diag, 0.0)
+        for n, value in enumerate((diag, rl, ll, dl, ul, inv)):
+            coef_ref[n, at : at + 16] = value
+
     def strip_image(ref_o, ref_s, g, lane, sides):
         shape = lane.shape
         o, s = ref_o[g], ref_s[g]
@@ -142,76 +215,92 @@
         (u,) = strip_image(y0_o, y0_s, g, lane48, (1,))
         y1_s[g] = sc[1, g, 5:6] * u
 
-    def beside(i):
-        k = i + 5
-        return k // 16, 125 - 8 * (k % 16)
-
-    def coefficients(i, _):
-        g, shift = beside(i)
-        row = xe[i, 32:40]
-        other = jnp.where(lanes((8, 128)) % 8 < 3, left_ref[g, 32:40], right_ref[g, 32:40])
-        other = roll(other, shift)
-        rl, dl = row[2:3], row[3:4]
-        ll = roll(jnp.where(lane1 == 127, other[2:3], rl), 1)
-        ul = xe[jnp.maximum(i - 1, 0), DOWN : DOWN + 1]
-        diag = row[4:5] + rl + ll + dl + ul
-        inv = jnp.where(diag > 0, 1.0 / diag, 0.0)
-        coef_ref[i] = jnp.concatenate([diag, rl, ll, dl, ul, inv, inv, inv], axis=0)
-        zs[i] = jnp.where(row[0:1] == window, row[1:2], 0.0)
-        return 0
-
-    lax.fori_loop(0, EXT, coefficients, 0, unroll=2)
-
-    def image(ref, strip, i, lane):
-        g, shift = beside(i)
-        here = ref[i]
-        other = roll(strip[g], shift)
+    def passes(work, low, high):
+        for s in range(16):
+            if s - 8 >= low:
+                work(0, s)
+
+        def step(g, _):
+            for s in range(16):
+                work(g, s)
+            return 0
+
+        lax.fori_loop(1, 8, step, 0)
+        for s in range(16):
+            if 120 + s < high:
+                work(8, s)
+
+    def owned(g, s):
+        return not isinstance(g, int) or 0 <= 16 * g - 8 + s < 128
+
+    def coef(n, g, s):
+        return coef_ref[n, pl.ds(16 * g + 8 + s, 1), :]
+
+    def image(here, up, down, strip, g, s, lane):
+        other = roll(strip[g], 125 - 8 * s)
         left = roll(jnp.where(lane == 127, other, here), 1)
         right = roll(jnp.where(lane == 0, other, here), 127)
-        c = coef_ref[i]
         return (
-            c[0:1] * here
-            - c[1:2] * right
-            - c[2:3] * left
-            - c[3:4] * ref[i + 1]
-            - c[4:5] * ref[i - 1]
-        ), c[5:6]
-
-    def first_image(i, _):
-        w, inv = image(zs, sz_s, i, lane16)
-        basis_ref[i, 0:16] = zs[i]
-        basis_ref[i, 16:32] = w
-        y0[i, 0:32] = inv * xe[i, 0:32]
-        y0[i, 32:48] = inv * w
-        return 0
-
-    lax.fori_loop(1, EXT - 1, first_image, 0, unroll=2)
-
-    def second_image(i, _):
-        f1, inv = image(y0, y0_s, i, lane48)
-        first_ref[i] = f1
-        y1[i] = inv * f1
-        return 0
-
-    lax.fori_loop(2, EXT - 2, second_image, 0, unroll=2)
-
-    gram[...] = jnp.zeros((48, 256), F32)
-
-    def third_image(i, sums):
-        f2, _ = image(y1, y1_s, i, lane48)
-        second_ref[i - HALO] = f2
-        b, f1, w = xe[i, 0:32], first_ref[i], basis_ref[i, 16:32]
-        y0b, y1u = y0[i, 0:32], y1[i, 0:32]
-        left = jnp.concatenate([zs[i], y0[i, 32:48], y1[i, 32:48]], axis=0)
-        every = jnp.concatenate([b, w, f1, f2], axis=0)
-        gram[:, 0:144] += dot(left, every, NT)
-        u, uu = f1[0:32], f2[0:32]
-        return (sums[0] + y0b * b, sums[1] + y0b * u, sums[2] + y1u * u, sums[3] + y1u * uu)
+            coef(0, g, s) * here
+            - coef(1, g, s) * right
+            - coef(2, g, s) * left
+            - coef(3, g, s) * down
+            - coef(4, g, s) * up
+        )
+
+    def basis(j):
+        return jnp.where(ext[0, pl.ds(j, 1), :] == window, ext[1, pl.ds(j, 1), :], 0.0)
+
+    def first_image(g, s):
+        r, j = 16 * g - 8 + s, 16 * g + 8 + s
+        w = image(basis(j), basis(j - 1), basis(j + 1), sz_s, g, s, lane16)
+        if owned(g, s):
+            b = rows_ref[r]
+            w_ref[r] = w
+        else:
+            b = top_ref[r + HALO, 0:32] if r < 0 else bottom_ref[r - 128, 0:32]
+        inv = coef(5, g, s)
+        y0[16 * g + s, 0:32] = inv * b
+        y0[16 * g + s, 32:48] = inv * w
+
+    passes(first_image, -2, 130)
+
+    def second_image(g, s):
+        i = 16 * g + s
+        f1 = image(y0[i], y0[i - 1], y0[i + 1], y0_s, g, s, lane48)
+        if owned(g, s):
+            first_ref[16 * g - 8 + s] = f1
+        y1[i] = coef(5, g, s) * f1
+
+    passes(second_image, -1, 129)
+
+    def third_image(g, s):
+        i = 16 * g + s
+        second_ref[16 * g - 8 + s] = image(y1[i], y1[i - 1], y1[i + 1], y1_s, g, s, lane48)
+
+    passes(third_image, 0, 128)
+
+    gram[...] = jnp.zeros((96, 256), F32)
+
+    def products(k, sums):
+        left, every = [], []
+        sums = list(sums)
+        for n in range(16):
+            r = 16 * k + n
+            b, f1, f2, y0r, y1r = rows_ref[r], first_ref[r], second_ref[r], y0[r + 8], y1[r + 8]
+            left.append(jnp.concatenate([basis(r + 16), y0r[32:48], y1r[32:48]], axis=0))
+            every.append(jnp.concatenate([b, w_ref[r], f1, f2], axis=0))
+            pairs = ((y0r, b), (y0r, f1), (y1r, f1), (y1r, f2))
+            sums = [t + p[0:32] * q[0:32] for t, (p, q) in zip(sums, pairs)]
+        left = jnp.concatenate(parts_of(jnp.concatenate(left, axis=1), 2), axis=0)
+        high, low = parts_of(jnp.concatenate(every, axis=1), 2)
+        gram[:, 0:144] += fast_dot(left, high, NT) + fast_dot(left, low, NT)
+        return tuple(sums)
 
     zero = jnp.zeros((32, 128), F32)
-    sums = lax.fori_loop(HALO, EXT - HALO, third_image, (zero, zero, zero, zero))
-
-    a0, a1 = gram[:, 0:128], gram[:, 128:256]
+    sums = lax.fori_loop(0, 8, products, (zero, zero, zero, zero))
+
+    a0, a1 = gram[0:48, 0:128] + gram[48:96, 0:128], gram[0:48, 128:256] + gram[48:96, 128:256]
     half0 = a0[16:32]
     half1 = jnp.where(lane16 < 16, a1[16:32], 0.0)
     half1 = jnp.where((lane16 >= 16) & (lane16 < 64), roll(a0[0:16], 16), half1)
@@ -469,34 +558,42 @@
     out_ref[68:72] = jnp.zeros((4, 128), F32)
 
 
-def outputs_kernel(x_ref, first_ref, second_ref, basis_ref, coef_ref, m_ref, sol_ref, res_ref):
+def outputs_kernel(rows_ref, first_ref, second_ref, w_ref, grid_ref, coef_ref, place_ref, m_ref, sol_ref, res_ref):
+    pr, pc = place_ref[0], place_ref[1]
+    slot = lax.broadcasted_iota(jnp.int32, (16, 128), 0)
+    region_row = pr - 1 + slot // 4
+    region_col = 2 * pc - 1 + slot % 4
+    inside = (slot < 12) & (region_row >= 0) & (region_row < REG) & (region_col >= 0) & (region_col < REG)
+    window = jnp.where(inside, region_row * REG + region_col, -1).astype(F32)
     m = jnp.concatenate([m_ref[...], jnp.zeros((56, 128), F32)], axis=0).T
-    left = m[0:96, 0:64]
+    c1, c2, c3 = parts_of(m[0:96, 0:64], 3)
+    left = jnp.concatenate([c1, c1, c2, c2, c1, c3], axis=1)
     shape = (32, 128)
     p1, p2, p3, p4 = (jnp.broadcast_to(m[0:32, 64 + n : 65 + n], shape) for n in range(4))
 
-    def step(r, _):
-        i = r + HALO
-        b, f1, f2 = x_ref[r, 0:32], first_ref[i], second_ref[r]
-        u, uu = f1[0:32], f2[0:32]
-        rows = jnp.concatenate([basis_ref[i], f1[32:48], f2[32:48]], axis=0)
-        d = dot(left, rows)
-        inv = coef_ref[i, 5:6]
-        res_ref[r] = b + p1 * u + p2 * uu + d[0:32]
-        sol_ref[r] = inv * (p3 * b + p4 * u + d[32:64]) + d[64:96]
+    def step(k, _):
+        rows = []
+        for n in range(8):
+            r = 8 * k + n
+            z = jnp.where(grid_ref[pl.ds(r, 1), :] == window, grid_ref[pl.ds(128 + r, 1), :], 0.0)
+            rows.append(jnp.concatenate([z, w_ref[r], first_ref[r, 32:48], second_ref[r, 32:48]], axis=0))
+        r1, r2, r3 = parts_of(jnp.concatenate(rows, axis=1), 3)
+        d = fast_dot(left, jnp.concatenate([r1, r2, r1, r2, r3, r1], axis=0))
+        for n in range(8):
+            r = 8 * k + n
+            b, u, uu = rows_ref[r], first_ref[r, 0:32], second_ref[r, 0:32]
+            e = d[:, 128 * n : 128 * n + 128]
+            inv = coef_ref[5, pl.ds(r + 16, 1), :]
+            res_ref[pl.ds(r, 32, stride=128), :] = b + p1 * u + p2 * uu + e[0:32]
+            sol_ref[pl.ds(r, 32, stride=128), :] = inv * (p3 * b + p4 * u + e[32:64]) + e[64:96]
         return 0
 
-    lax.fori_loop(0, 128, step, 0, unroll=2)
+    lax.fori_loop(0, 16, step, 0)
 
 
 def from_everyone(value, axis):
     count = lax.axis_size(axis)
     return lax.all_to_all(jnp.broadcast_to(value[None], (count, *value.shape)), axis, 0, 0, tiled=True)
-
-
-def lookup(entries, classes):
-    levels = lax.broadcasted_iota(jnp.int32, (entries.shape[0],) + classes.shape, 0)
-    return jnp.sum(jnp.where(classes[None] == levels, entries[:, None, None], 0.0), axis=0)
 
 
 def shape_of(*dims):
@@ -511,50 +608,52 @@
     pr, pc = lax.axis_index(ROW), lax.axis_index(COL)
     rows, cols = lax.axis_size(ROW), lax.axis_size(COL)
     place = jnp.stack([pr, pc]).astype(jnp.int32)
-    row_ids = lax.broadcasted_iota(jnp.int32, labels.shape, 0)
-    col_ids = lax.broadcasted_iota(jnp.int32, labels.shape, 1)
-    right_link = jnp.where((col_ids == 127) & (pc == cols - 1), 0.0, lookup(edge_table, horizontal_class))
-    down_link = jnp.where((row_ids == 127) & (pr == rows - 1), 0.0, lookup(edge_table, vertical_class))
-    pad = lookup(pad_table, pad_class)
-    zero = jnp.zeros_like(pad)
-    params = jnp.stack(
-        [labels.astype(F32), bump_height, right_link, down_link, pad, zero, zero, zero], axis=1
-    )
-    x = jnp.concatenate([jnp.transpose(load_currents, (1, 0, 2)), params], axis=1)
+    loads = load_currents.reshape(-1, 128)
+    grid, first_rows = pl.pallas_call(
+        prepare_kernel,
+        out_shape=(shape_of(1024, 128), shape_of(HALO, SUB, 128)),
+        in_specs=[scalars] * 3 + [whole] * 6,
+        out_specs=(whole, whole),
+    )(place, edge_table, pad_table, loads, labels, bump_height, horizontal_class, vertical_class, pad_class)
     down = [(i, i + 1) for i in range(rows - 1)]
-    top = lax.ppermute(x[-HALO:], ROW, down)
-    bottom = lax.ppermute(x[:HALO], ROW, [(b, a) for a, b in down])
+    bottom = lax.ppermute(first_rows, ROW, [(b, a) for a, b in down])
+    by_rows, own, last_rows = pl.pallas_call(
+        pack_kernel,
+        out_shape=(shape_of(128, 32, 128), shape_of(GROUPS, SUB, 128), shape_of(HALO, SUB, 128)),
+        in_specs=[whole] * 2,
+        out_specs=(whole,) * 3,
+    )(loads, grid)
+    top = lax.ppermute(last_rows, ROW, down)
     own = pl.pallas_call(
-        pack_kernel, out_shape=shape_of(GROUPS, SUB, 128), in_specs=[whole] * 3, out_specs=whole
-    )(x, top, bottom)
+        corner_kernel, out_shape=shape_of(GROUPS, SUB, 128), in_specs=[whole] * 3, out_specs=whole
+    )(own, top, bottom)
     right = [(i, i + 1) for i in range(cols - 1)]
     beside_left = lax.ppermute(own, COL, right)
     beside_right = lax.ppermute(own, COL, [(b, a) for a, b in right])
-    first, second, basis, coef, payload = pl.pallas_call(
+    first, second, w, coef, payload = pl.pallas_call(
         fields_kernel,
         out_shape=(
-            shape_of(EXT, 48, 128),
             shape_of(128, 48, 128),
-            shape_of(EXT, 32, 128),
-            shape_of(EXT, 8, 128),
+            shape_of(128, 48, 128),
+            shape_of(128, 16, 128),
+            shape_of(6, 160, 128),
             shape_of(24, 128),
         ),
-        in_specs=[scalars] + [whole] * 6,
+        in_specs=[scalars] + [whole] * 7,
         out_specs=(whole,) * 5,
         scratch_shapes=[
-            vmem(EXT, SUB, 128),
+            vmem(5, 160, 128),
             vmem(GROUPS, 16, 128),
             vmem(GROUPS, 16, 128),
             vmem(GROUPS, 48, 128),
             vmem(GROUPS, 48, 128),
             vmem(GROUPS, 48, 128),
             vmem(2, GROUPS, 8, 128),
-            vmem(EXT, 16, 128),
-            vmem(EXT, 48, 128),
-            vmem(EXT, 48, 128),
-            vmem(48, 256),
+            vmem(144, 48, 128),
+            vmem(144, 48, 128),
+            vmem(96, 256),
         ],
-    )(place, x, top, bottom, own, beside_left, beside_right)
+    )(place, by_rows, grid, top, bottom, own, beside_left, beside_right)
     in_row = from_everyone(payload, COL).reshape(-1, 128)
     combined = pl.pallas_call(
         combine_kernel, out_shape=shape_of(96, 128), in_specs=[whole], out_specs=whole
@@ -570,11 +669,11 @@
     )(place, everything)
     solution, residual = pl.pallas_call(
         outputs_kernel,
-        out_shape=(shape_of(128, 32, 128), shape_of(128, 32, 128)),
-        in_specs=[whole] * 6,
+        out_shape=(shape_of(4096, 128), shape_of(4096, 128)),
+        in_specs=[whole] * 6 + [scalars, whole],
         out_specs=(whole, whole),
-    )(x, first, second, basis, coef, matrix)
-    return jnp.transpose(solution, (1, 0, 2)), jnp.transpose(residual, (1, 0, 2))
+    )(by_rows, first, second, w, grid, coef, place, matrix)
+    return solution.reshape(load_currents.shape), residual.reshape(load_currents.shape)
 
 
 def solution(mesh):

time: 201 us -> 121 us (0.60)
  Pallas kernels: 127 us -> 64.7 us
  local copies, waits for them, and re-layouts: 18.8 us -> 2.87 us
    pallas_call x3 -> x5, Pallas kernels: 112 us -> 48.9 us  [the longest x1 27.5 us: body(): pl.pallas_call(fields_kernel, out_shape=(shape_of(128, 48, 128), shape_of...]
    unnamed x27 -> x8, local copies, waits for them, and re-layouts: 12.4 us -> 1.29 us
    concatenate x2 -> x0, local copies, waits for them, and re-layouts: 4.81 us -> none  [body(): jnp.concatenate([jnp.transpose(load_currents, (1, 0, 2)), params], axis=1)]
  transfers between devices with their start and end apart: 4 -> 4, of which waited for: 3 -> 3; matrix products, arithmetic and copies ran while one was open for 0% -> 0% of each run, Pallas kernels for 0% -> 4%
where the time goes in v2:
time: 121 us; the launch traced here: 120 us
  Pallas kernels  64.7 us (53%)
  blocking collectives  34.3 us (28%)
  starting transfers between devices  12.8 us (11%)
  waiting for transfers between devices  4.34 us (4%)
  local copies, waits for them, and re-layouts  2.87 us (2%)
    all_to_all x2, blocking collectives, from_everyone(): lax.all_to_all(jnp.broadcast_to(value[None], (count, *value.shape)), axis...  34.3 us
    pallas_call x1, Pallas kernels, body(): pl.pallas_call(fields_kernel, out_shape=(shape_of(128, 48, 128), shape_of...  27.5 us
    pallas_call x1, Pallas kernels, body(): pl.pallas_call(coarse_kernel, out_shape=shape_of(72, 128), in_specs=[scal...  14.3 us
    pallas_call x1, Pallas kernels, body(): pl.pallas_call(outputs_kernel, out_shape=(shape_of(4096, 128), shape_of(4...  12 us
    pallas_call x1, Pallas kernels, body(): pl.pallas_call(pack_kernel, out_shape=(shape_of(128, 32, 128), shape_of(G...  5.06 us
    ppermute x1, starting transfers between devices, body(): top = lax.ppermute(last_rows, ROW, down)  4.98 us
    ppermute x1, starting transfers between devices, body(): beside_right = lax.ppermute(own, COL, [(b, a) for a, b in right])  3.42 us
    ppermute x1, starting transfers between devices, body(): beside_left = lax.ppermute(own, COL, right)  3.11 us
  transfers between devices with their start and end apart: 4, of which 3 were waited for; matrix products, arithmetic and copies ran while one was open for 0% of the time, Pallas kernels for 4%

profile of v2, /device:TPU:1, one launch (start us, length us, event | category | flops | bytes accessed | tf_op | source)
XLA Modules:
  0.0 120.4 jit_solution(7786733326289355811)
XLA Ops:
  0.6 0.7 pad_add_fusion.place_ref
  1.3 2.6 %shard_map.95 = (f32[1024,128]{1,0:T(8,128)}, f32[3,40,128]{2,1,0:T(8,128)}) custom-call(s32[2]{0:T(128)} %pad_add_fusion.place_ref, f32[8]{0:T(128)} %edge_ref.1, f32[8]{0:T(128)} %pad_ref.1, f32[4096,128]{1,0:T(8,128)} %bitcast.6, s32[128,128]{1,0:T(8,128)} %label_ref.1, f32[128,128]{1,0:T(8,128)} %bump_ref.1, s32[128,128]{1,0:T(8,128)} %across_ref.1, ...), custom_call_target="tpu_custom_call" | custom-call | tf_op jit(solution)/shard_map/pallas_call | solution.py:612
  3.9 1.3 %collective-permute-start.1 = (f32[3,40,128]{2,1,0:T(8,128)}, f32[3,40,128]{2,1,0:T(8,128)S(1)}, u32[]{:S(2)}, u32[]{:S(2)}) collective-permute-start(f32[3,40,128]{2,1,0:T(8,128)} %get-tuple-element.17), channel_id=1, source_target_pairs={{8,0},{16,8},{24,16},{32,24},{40,32},{48,40},{56,48},{64,56},{72,6... | collective-permute-start | bytes 184328 | tf_op jit(solution)/shard_map/ppermute | solution.py:619
  5.2 5.1 %shard_map.96 = (f32[128,32,128]{2,1,0:T(8,128)}, f32[9,40,128]{2,1,0:T(8,128)}, f32[3,40,128]{2,1,0:T(8,128)}) custom-call(f32[4096,128]{1,0:T(8,128)} %bitcast.7, f32[1024,128]{1,0:T(8,128)} %get-tuple-element.14.grid_ref), custom_call_target="tpu_custom_call" | custom-call | tf_op jit(solution)/shard_map/pallas_call | solution.py:620
  10.3 5.0 %collective-permute-start = (f32[3,40,128]{2,1,0:T(8,128)}, f32[3,40,128]{2,1,0:T(8,128)S(1)}, u32[]{:S(2)}, u32[]{:S(2)}) collective-permute-start(f32[3,40,128]{2,1,0:T(8,128)} %get-tuple-element.16), channel_id=1, source_target_pairs={{0,8},{8,16},{16,24},{24,32},{32,40},{40,48},{48,56},{56,64},{64,7... | collective-permute-start | bytes 184328 | tf_op jit(solution)/shard_map/ppermute | solution.py:626
  15.3 0.0 collective-permute-done.1.bottom_ref
  15.3 1.6 %collective-permute-done.top_ref = f32[3,40,128]{2,1,0:T(8,128)S(1)} collective-permute-done((f32[3,40,128]{2,1,0:T(8,128)}, f32[3,40,128]{2,1,0:T(8,128)S(1)}, u32[]{:S(2)}, u32[]{:S(2)}) %collective-permute-start) | collective-permute-done | bytes 61472 | tf_op jit(solution)/shard_map/ppermute | solution.py:626
  16.9 0.0 copy-done
  16.9 0.6 copy-done.1
  17.5 1.7 %shard_map.97.own_ref = f32[9,40,128]{2,1,0:T(8,128)} custom-call(f32[9,40,128]{2,1,0:T(8,128)} %get-tuple-element.18.own_ref, f32[3,40,128]{2,1,0:T(8,128)} %copy-done.1, f32[3,40,128]{2,1,0:T(8,128)} %copy-done), custom_call_target="tpu_custom_call" | custom-call | tf_op jit(solution)/shard_map/pallas_call | solution.py:627
  19.2 3.4 %collective-permute-start.3 = (f32[9,40,128]{2,1,0:T(8,128)}, f32[9,40,128]{2,1,0:T(8,128)S(1)}, u32[]{:S(2)}, u32[]{:S(2)}) collective-permute-start(f32[9,40,128]{2,1,0:T(8,128)} %shard_map.97.own_ref), channel_id=1, source_target_pairs={{1,0},{2,1},{3,2},{4,3},{5,4},{6,5},{7,6},{9,8},{10,9},{11,10},{12... | collective-permute-start | bytes 552968 | tf_op jit(solution)/shard_map/ppermute | solution.py:632
  22.6 3.1 %collective-permute-start.2 = (f32[9,40,128]{2,1,0:T(8,128)}, f32[9,40,128]{2,1,0:T(8,128)S(1)}, u32[]{:S(2)}, u32[]{:S(2)}) collective-permute-start(f32[9,40,128]{2,1,0:T(8,128)} %shard_map.97.own_ref), channel_id=1, source_target_pairs={{0,1},{1,2},{2,3},{3,4},{4,5},{5,6},{6,7},{8,9},{9,10},{10,11},{11... | collective-permute-start | bytes 552968 | tf_op jit(solution)/shard_map/ppermute | solution.py:631
  25.8 1.5 %collective-permute-done.3.right_ref = f32[9,40,128]{2,1,0:T(8,128)S(1)} collective-permute-done((f32[9,40,128]{2,1,0:T(8,128)}, f32[9,40,128]{2,1,0:T(8,128)S(1)}, u32[]{:S(2)}, u32[]{:S(2)}) %collective-permute-start.3) | collective-permute-done | bytes 184352 | tf_op jit(solution)/shard_map/ppermute | solution.py:632
  27.3 1.3 %collective-permute-done.2.left_ref = f32[9,40,128]{2,1,0:T(8,128)S(1)} collective-permute-done((f32[9,40,128]{2,1,0:T(8,128)}, f32[9,40,128]{2,1,0:T(8,128)S(1)}, u32[]{:S(2)}, u32[]{:S(2)}) %collective-permute-start.2) | collective-permute-done | bytes 184352 | tf_op jit(solution)/shard_map/ppermute | solution.py:631
  28.5 0.0 copy-done.2
  28.5 0.7 copy-done.3
  29.2 27.5 %shard_map.98 = (f32[128,48,128]{2,1,0:T(8,128)}, f32[128,48,128]{2,1,0:T(8,128)}, f32[128,16,128]{2,1,0:T(8,128)}, f32[6,160,128]{2,1,0:T(8,128)}, f32[24,128]{1,0:T(8,128)}) custom-call(s32[2]{0:T(128)} %pad_add_fusion.place_ref, f32[128,32,128]{2,1,0:T(8,128)} %get-tuple-element.15.rows_ref, f32[1024,128]{1,0:T(8,128)} %get-tuple-element.14.grid_ref, ...), custom_call_target="tpu_custom_call" | custom-call | tf_op jit(solution)/shard_map/pallas_call | solution.py:633
  56.7 0.7 broadcast_in_dim.4
  57.4 10.4 %all_to_all.10 = f32[8,24,128]{2,1,0:T(8,128)} all-to-all(f32[8,24,128]{2,1,0:T(8,128)S(1)} %broadcast_in_dim.4), channel_id=1, replica_groups=mesh['row_0'=4,'row_1'=4,'col_0'=4,'col_1'=2] {'col_0','col_1'}, dimensions={0} | all-to-all | bytes 196608 | tf_op jit(solution)/shard_map/all_to_all | solution.py:596
  67.9 1.5 %shard_map.99 = f32[96,128]{1,0:T(8,128)} custom-call(f32[192,128]{1,0:T(8,128)} %bitcast.8), custom_call_target="tpu_custom_call" | custom-call | tf_op jit(solution)/shard_map/pallas_call | solution.py:658
  69.4 0.9 broadcast_in_dim.5
  70.3 23.9 %all_to_all.11.in_ref = f32[16,96,128]{2,1,0:T(8,128)} all-to-all(f32[16,96,128]{2,1,0:T(8,128)S(1)} %broadcast_in_dim.5), channel_id=1, replica_groups=mesh['row_0'=4,'row_1'=4,'col_0'=4,'col_1'=2] {'row_0','row_1'}, dimensions={0} | all-to-all | bytes 1572864 | tf_op jit(solution)/shard_map/all_to_all | solution.py:596
  94.2 14.3 %shard_map.100.m_ref = f32[72,128]{1,0:T(8,128)} custom-call(s32[2]{0:T(128)} %pad_add_fusion.place_ref, f32[16,96,128]{2,1,0:T(8,128)} %all_to_all.11.in_ref), custom_call_target="tpu_custom_call" | custom-call | tf_op jit(solution)/shard_map/pallas_call | solution.py:662
  108.4 12.0 %shard_map.101 = (f32[4096,128]{1,0:T(8,128)}, f32[4096,128]{1,0:T(8,128)}) custom-call(f32[128,32,128]{2,1,0:T(8,128)} %get-tuple-element.15.rows_ref, f32[128,48,128]{2,1,0:T(8,128)} %get-tuple-element.19.first_ref, f32[128,48,128]{2,1,0:T(8,128)} %get-tuple-element.20.second_ref, f32[128,16,128]{2,1,0:T(8,128)} %get-tuple-element.21.w_ref, ...), custom_call_target="tpu_custom_call" | custom-call | tf_op jit(solution)/shard_map/pallas_call | solution.py:670
  (4 shorter events, 0.0 us)
Async XLA Ops:
  3.9 11.3 %collective-permute-start.1 = (f32[3,40,128]{2,1,0:T(8,128)}, f32[3,40,128]{2,1,0:T(8,128)S(1)}, u32[]{:S(2)}, u32[]{:S(2)}) collective-permute-start(f32[3,40,128]{2,1,0:T(8,128)} %get-tuple-element.17), channel_id=1, source_target_pairs={{8,0},{16,8},{24,16},{32,24},{40,32},{48,40},{56,48},{64,56},{72,6... | collective-permute-start | bytes 184328 | tf_op jit(solution)/shard_map/ppermute | solution.py:619
  10.3 6.6 %collective-permute-start = (f32[3,40,128]{2,1,0:T(8,128)}, f32[3,40,128]{2,1,0:T(8,128)S(1)}, u32[]{:S(2)}, u32[]{:S(2)}) collective-permute-start(f32[3,40,128]{2,1,0:T(8,128)} %get-tuple-element.16), channel_id=1, source_target_pairs={{0,8},{8,16},{16,24},{24,32},{32,40},{40,48},{48,56},{56,64},{64,7... | collective-permute-start | bytes 184328 | tf_op jit(solution)/shard_map/ppermute | solution.py:626
  15.3 1.6 %copy-start = (f32[3,40,128]{2,1,0:T(8,128)}, f32[3,40,128]{2,1,0:T(8,128)S(1)}, u32[]{:S(2)}) copy-start(f32[3,40,128]{2,1,0:T(8,128)S(1)} %collective-permute-done.1.bottom_ref) | copy-start | bytes 184324
  16.9 0.6 copy-start.1
  19.2 8.0 %collective-permute-start.3 = (f32[9,40,128]{2,1,0:T(8,128)}, f32[9,40,128]{2,1,0:T(8,128)S(1)}, u32[]{:S(2)}, u32[]{:S(2)}) collective-permute-start(f32[9,40,128]{2,1,0:T(8,128)} %shard_map.97.own_ref), channel_id=1, source_target_pairs={{1,0},{2,1},{3,2},{4,3},{5,4},{6,5},{7,6},{9,8},{10,9},{11,10},{12... | collective-permute-start | bytes 552968 | tf_op jit(solution)/shard_map/ppermute | solution.py:632
  22.6 5.9 %collective-permute-start.2 = (f32[9,40,128]{2,1,0:T(8,128)}, f32[9,40,128]{2,1,0:T(8,128)S(1)}, u32[]{:S(2)}, u32[]{:S(2)}) collective-permute-start(f32[9,40,128]{2,1,0:T(8,128)} %shard_map.97.own_ref), channel_id=1, source_target_pairs={{0,1},{1,2},{2,3},{3,4},{4,5},{5,6},{6,7},{8,9},{9,10},{10,11},{11... | collective-permute-start | bytes 552968 | tf_op jit(solution)/shard_map/ppermute | solution.py:631
  27.2 1.3 %copy-start.2 = (f32[9,40,128]{2,1,0:T(8,128)}, f32[9,40,128]{2,1,0:T(8,128)S(1)}, u32[]{:S(2)}) copy-start(f32[9,40,128]{2,1,0:T(8,128)S(1)} %collective-permute-done.3.right_ref) | copy-start | bytes 552964
  28.5 0.7 copy-start.3

commit v3 on v2

v3 whole, which is shorter than its diff:
```python
import jax
import jax.numpy as jnp
from jax import lax
from jax.experimental import pallas as pl
from jax.experimental.pallas import tpu as pltpu
from jax.sharding import Mesh
from jax.sharding import PartitionSpec as P

REG = 16
ROW = ("row_0", "row_1")
COL = ("col_0", "col_1")
F32 = jnp.float32
precise = lax.Precision.HIGHEST

LAB, BUMP, RIGHT, DOWN, PAD = 32, 33, 34, 35, 36
SUB = 40
HALO = 3
GROUPS = 9
ORDER = (1, 3, 5, 7, 9, 11, 13, 15, 2, 6, 10, 14, 4, 12, 8, 0)
POS = tuple(ORDER.index(p) for p in range(16))
NT = (((1,), (1,)), ((), ()))
NN = (((1,), (0,)), ((), ()))
TN = (((0,), (0,)), ((), ()))
whole = pl.BlockSpec(memory_space=pltpu.VMEM)
outside = pl.BlockSpec(memory_space=pltpu.HBM)
limited = pltpu.CompilerParams(vmem_limit_bytes=32 * 2**20)
scalars = pl.BlockSpec(memory_space=pltpu.SMEM)


def dot(a, b, dims=NN):
    return lax.dot_general(a, b, dims, precision=precise, preferred_element_type=F32)


def parts_of(x, count):
    parts = []
    for n in range(count):
        parts.append(x.astype(jnp.bfloat16))
        if n + 1 < count:
            x = x - parts[-1].astype(F32)
    return parts


def fast_dot(a, b, dims=NN):
    return lax.dot_general(a, b, dims, preferred_element_type=F32)


def lanes(shape):
    return lax.broadcasted_iota(jnp.int32, shape, len(shape) - 1)


def roll(x, shift, axis=1):
    return pltpu.roll(x, shift, axis)


def prepare_kernel(
    place_ref, edge_hbm, pad_hbm, load_hbm, label_hbm, bump_hbm, across_hbm, down_hbm, pad_class_hbm,
    grid_ref, first_ref, edge_ref, pad_ref, load_ref, label_ref, across_ref, down_ref, pad_class_ref, done,
):
    copies = [
        pltpu.make_async_copy(source, target, done.at[n])
        for n, (source, target) in enumerate(
            (
                (edge_hbm, edge_ref),
                (pad_hbm, pad_ref),
                (across_hbm, across_ref),
                (down_hbm, down_ref),
                (pad_class_hbm, pad_class_ref),
                (label_hbm, label_ref),
                (bump_hbm, grid_ref.at[pl.ds(128, 128)]),
                (load_hbm.at[:, pl.ds(0, 8)], load_ref),
            )
        )
    ]
    for copy in copies:
        copy.start()
    for copy in copies:
        copy.wait()
    pr, pc = place_ref[0], place_ref[1]
    shape = (128, 128)
    row, lane = lax.broadcasted_iota(jnp.int32, shape, 0), lanes(shape)

    def lookup(table, classes):
        found = jnp.zeros(shape, F32)
        for n in range(8):
            found = jnp.where(classes == n, table[n], found)
        return found

    right = lookup(edge_ref, across_ref[...])
    down = lookup(edge_ref, down_ref[...])
    grid_ref[0:128] = label_ref[...].astype(F32)
    grid_ref[256:384] = jnp.where((lane == 127) & (pc == 7), 0.0, right)
    grid_ref[384:512] = jnp.where((row == 127) & (pr == 15), 0.0, down)
    grid_ref[512:640] = lookup(pad_ref, pad_class_ref[...])
    grid_ref[640:1024] = jnp.zeros((384, 128), F32)
    for n in range(HALO):
        first_ref[n, 0:32] = load_ref[:, n]
        first_ref[n, 32:40] = grid_ref[pl.ds(n, 8, stride=128), :]


def pack_kernel(load_ref, grid_ref, rows_ref, own_ref, last_ref):
    lane = lanes((32, 128)) // 8

    def group(g, slots):
        loads, rest = jnp.zeros((32, 128), F32), jnp.zeros((8, 128), F32)
        for s in slots:
            r = 16 * g - 8 + s
            b = load_ref[pl.ds(r, 32, stride=128), :]
            rows_ref[r] = b
            loads = jnp.where(lane == s, roll(b, (8 * s + 3) % 128), loads)
            rest = jnp.where(lane[0:8] == s, roll(grid_ref[pl.ds(r, 8, stride=128), :], (8 * s + 3) % 128), rest)
        own_ref[g, 0:32] = loads
        own_ref[g, 32:40] = rest

    group(0, range(8, 16))
    group(8, range(8))

    def step(g, _):
        group(g, range(16))
        return 0

    lax.fori_loop(1, 8, step, 0)
    for n in range(HALO):
        r = 128 - HALO + n
        last_ref[n, 0:32] = rows_ref[r]
        last_ref[n, 32:40] = grid_ref[pl.ds(r, 8, stride=128), :]


def corner_kernel(own_ref, top_ref, bottom_ref, out_ref):
    lane = lanes((SUB, 128)) // 8
    for g in range(GROUPS):
        out_ref[g] = own_ref[g]
    start, end = own_ref[0], own_ref[8]
    for n in range(HALO):
        s = 8 - HALO + n
        start = jnp.where(lane == s, roll(top_ref[n], (8 * s + 3) % 128), start)
        s = 8 + n
        end = jnp.where(lane == s, roll(bottom_ref[n], (8 * s + 3) % 128), end)
    out_ref[0] = start
    out_ref[8] = end


def fields_kernel(
    place_ref, rows_ref, grid_ref, top_ref, bottom_ref, own_ref, left_ref, right_ref,
    first_ref, second_ref, w_ref, coef_ref, out_ref,
    ext, so, ss, sz_o, sz_s, y0_o, y0_s, qz, q0, q1, sc, y0, y1, gram,
):
    pr, pc = place_ref[0], place_ref[1]
    lane1 = lanes((1, 128))
    lane16 = lanes((16, 128))
    lane48 = lanes((48, 128))

    for n in range(5):
        ext[n, 0:16] = jnp.zeros((16, 128), F32)
        ext[n, 16:144] = grid_ref[128 * n : 128 * n + 128]
        ext[n, 144:160] = jnp.zeros((16, 128), F32)
        for k in range(HALO):
            ext[n, 16 - HALO + k : 17 - HALO + k] = top_ref[k, 32 + n : 33 + n]
            ext[n, 144 + k : 145 + k] = bottom_ref[k, 32 + n : 33 + n]

    slot = lax.broadcasted_iota(jnp.int32, (16, 128), 0)
    region_row = pr - 1 + slot // 4
    region_col = 2 * pc - 1 + slot % 4
    inside = (slot < 12) & (region_row >= 0) & (region_row < REG) & (region_col >= 0) & (region_col < REG)
    window = jnp.where(inside, region_row * REG + region_col, -1).astype(F32)

    for ref in (so, ss, sz_o, sz_s, y0_o, y0_s):
        ref[0] = jnp.zeros(ref.shape[1:], F32)
        ref[GROUPS + 1] = jnp.zeros(ref.shape[1:], F32)

    def pair_left(o, s, lane):
        j = lane % 8
        return roll(jnp.where(j == 2, s, o), 1), roll(jnp.where(j == 2, o, s), 1)

    def pair_right(o, s, lane):
        j = lane % 8
        return roll(jnp.where(j == 3, s, o), 127), roll(jnp.where(j == 3, o, s), 127)

    def above(before, here, lane):
        return roll(jnp.where(lane >= 120, before, here), 8)

    def below(here, after, lane):
        return roll(jnp.where(lane < 8, after, here), 120)

    def strips(g, _):
        o_row = own_ref[g]
        s_row = jnp.where(lanes((SUB, 128)) % 8 < 3, left_ref[g], right_ref[g])
        so[g + 1], ss[g + 1] = o_row, s_row
        lefts = pair_left(o_row[RIGHT : RIGHT + 1], s_row[RIGHT : RIGHT + 1], lane1)
        for side, (row, ref, ll) in enumerate(((o_row, so, lefts[0]), (s_row, ss, lefts[1]))):
            rl, dl = row[RIGHT : RIGHT + 1], row[DOWN : DOWN + 1]
            ul = above(ref[g, DOWN : DOWN + 1], dl, lane1)
            diag = row[PAD : PAD + 1] + rl + ll + dl + ul
            inv = jnp.where(diag > 0, 1.0 / diag, 0.0)
            for n, value in enumerate((diag, rl, ll, dl, ul, inv)):
                sc[side, g, n : n + 1] = value
            z = jnp.where(row[LAB : LAB + 1] == window, row[BUMP : BUMP + 1], 0.0)
            (sz_s if side else sz_o)[g + 1] = z
            if side:
                qz[2 * g] = z
                qz[2 * g + 1] = roll(z, 64)

        at = pl.multiple_of(16 * g + 8, 8)
        beside = jnp.zeros((16, 128), F32)
        for s in range(16):
            beside = jnp.where(slot == s, roll(s_row[RIGHT : RIGHT + 1], 125 - 8 * s), beside)
        rl, dl = ext[2, pl.ds(at, 16)], ext[3, pl.ds(at, 16)]
        ll = roll(jnp.where(lane16 == 127, beside, rl), 1)
        last = ext[3, pl.ds(pl.multiple_of(at - 8, 8), 8)]
        ul = jnp.where(slot == 0, last[7:8], roll(dl, 1, 0))
        diag = ext[4, pl.ds(at, 16)] + rl + ll + dl + ul
        inv = jnp.where(diag > 0, 1.0 / diag, 0.0)
        for n, value in enumerate((diag, rl, ll, dl, ul, inv)):
            coef_ref[n, pl.ds(at, 16)] = value
        return 0

    lax.fori_loop(0, GROUPS, strips, 0)

    def strip_image(ref_o, ref_s, g, lane, sides):
        o, s = ref_o[g + 1], ref_s[g + 1]
        lefts, rights = pair_left(o, s, lane), pair_right(o, s, lane)
        done = []
        for side in sides:
            ref, here = (ref_s, s) if side else (ref_o, o)
            up = above(ref[g], here, lane)
            down = below(here, ref[g + 2], lane)
            c = [sc[side, g, n : n + 1] for n in range(5)]
            done.append(c[0] * here - c[1] * rights[side] - c[2] * lefts[side] - c[3] * down - c[4] * up)
        return done

    def strip_first(g, _):
        w = strip_image(sz_o, sz_s, g, lane16, (0, 1))
        for side, (source, ref) in enumerate(((so, y0_o), (ss, y0_s))):
            inv = sc[side, g, 5:6]
            ref[g + 1, 0:32] = inv * source[g + 1, 0:32]
            ref[g + 1, 32:48] = inv * w[side]
        y = y0_s[g + 1]
        q0[2 * g] = y
        q0[2 * g + 1] = roll(y, 64)
        return 0

    lax.fori_loop(0, GROUPS, strip_first, 0)

    def strip_second(g, _):
        (u,) = strip_image(y0_o, y0_s, g, lane48, (1,))
        y = sc[1, g, 5:6] * u
        q1[2 * g] = y
        q1[2 * g + 1] = roll(y, 64)
        return 0

    lax.fori_loop(0, GROUPS, strip_second, 0)

    def passes(work, low, high):
        for s in range(8):
            if s - 8 >= low:
                work(0, s)

        def step(g, _):
            for s in range(8):
                work(g, s)
            return 0

        lax.fori_loop(1, 17, step, 0)
        for s in range(8):
            if 128 + s < high:
                work(17, s)

    def owned(g):
        return not isinstance(g, int)

    def coef(n, g, s):
        return coef_ref[n, pl.ds(8 * g + 8 + s, 1), :]

    def image(here, up, down, strip, g, s, lane):
        other = roll(strip[g], 125 - 8 * s)
        left = roll(jnp.where(lane == 127, other, here), 1)
        right = roll(jnp.where(lane == 0, other, here), 127)
        return (
            coef(0, g, s) * here
            - coef(1, g, s) * right
            - coef(2, g, s) * left
            - coef(3, g, s) * down
            - coef(4, g, s) * up
        )

    def basis(j):
        return jnp.where(ext[0, pl.ds(j, 1), :] == window, ext[1, pl.ds(j, 1), :], 0.0)

    def first_image(g, s):
        r, j = 8 * g - 8 + s, 8 * g + 8 + s
        w = image(basis(j), basis(j - 1), basis(j + 1), qz, g, s, lane16)
        if owned(g):
            b = rows_ref[r]
            w_ref[r] = w
        else:
            b = top_ref[r + HALO, 0:32] if r < 0 else bottom_ref[r - 128, 0:32]
        inv = coef(5, g, s)
        y0[8 * g + s, 0:32] = inv * b
        y0[8 * g + s, 32:48] = inv * w

    passes(first_image, -2, 130)

    def second_image(g, s):
        i = 8 * g + s
        f1 = image(y0[i], y0[i - 1], y0[i + 1], q0, g, s, lane48)
        if owned(g):
            first_ref[8 * g - 8 + s] = f1
        y1[i] = coef(5, g, s) * f1

    passes(second_image, -1, 129)

    def third_image(g, s):
        i = 8 * g + s
        second_ref[8 * g - 8 + s] = image(y1[i], y1[i - 1], y1[i + 1], q1, g, s, lane48)

    passes(third_image, 0, 128)

    gram[...] = jnp.zeros((96, 256), F32)

    def products(k, sums):
        left, every = [], []
        sums = list(sums)
        for n in range(16):
            r = 16 * k + n
            b, f1, f2, y0r, y1r = rows_ref[r], first_ref[r], second_ref[r], y0[r + 8], y1[r + 8]
            left.append(jnp.concatenate([basis(r + 16), y0r[32:48], y1r[32:48]], axis=0))
            every.append(jnp.concatenate([b, w_ref[r], f1, f2], axis=0))
            pairs = ((y0r, b), (y0r, f1), (y1r, f1), (y1r, f2))
            sums = [t + p[0:32] * q[0:32] for t, (p, q) in zip(sums, pairs)]
        left = jnp.concatenate(parts_of(jnp.concatenate(left, axis=1), 2), axis=0)
        high, low = parts_of(jnp.concatenate(every, axis=1), 2)
        gram[:, 0:144] += fast_dot(left, high, NT) + fast_dot(left, low, NT)
        return tuple(sums)

    zero = jnp.zeros((32, 128), F32)
    sums = lax.fori_loop(0, 8, products, (zero, zero, zero, zero))

    a0, a1 = gram[0:48, 0:128] + gram[48:96, 0:128], gram[0:48, 128:256] + gram[48:96, 128:256]
    zr, w0, t0, w1, t1 = a0[0:16], a0[16:32], a0[32:48], a1[16:32], a1[32:48]
    matrices = jnp.zeros((16, 128), F32)
    for n, (x, z) in enumerate(((w0, 32), (w0, 80), (w1, 0), (zr, 32), (t1, 0))):
        start = 24 * n
        matrices = jnp.where((lane16 >= start) & (lane16 < start + 16), roll(x, (start - z) % 128), matrices)
    moved = jnp.zeros((16, 128), F32)
    for k in range(12):
        moved = jnp.where(slot == k, roll(matrices, (128 - k) % 128), moved)
    common = jnp.zeros((16, 128), F32)
    for n in range(5):
        start = 20 + 6 * n
        common = jnp.where((lane16 >= start) & (lane16 < start + 6), roll(moved, (start - 24 * n) % 128), common)
    lines = []
    diagonal = lanes((32, 128)) == lax.broadcasted_iota(jnp.int32, (32, 128), 0)
    for total in sums:
        column = jnp.sum(total, axis=1, keepdims=True)
        lines.append(jnp.sum(jnp.where(diagonal, column, 0.0), axis=0, keepdims=True))
    lane8, row8 = lanes((8, 128)), lax.broadcasted_iota(jnp.int32, (8, 128), 0)
    for d in range(8):
        message = common
        for n, (x, z) in enumerate(((w0, 0), (w0, 48), (w0, 96), (zr, 0), (t0, 96))):
            hit = (lane16 >= 4 * n) & (lane16 < 4 * n + 4)
            message = jnp.where(hit, roll(x, (4 * n - z - 4 * d) % 128), message)
        upper = roll(roll(message, 10, 0), 64)
        sent = jnp.where(lane8 < 64, message[0:8], upper[0:8])
        line = jnp.zeros((1, 128), F32)
        for n in range(4):
            line = jnp.where((lane1 >= 4 * n) & (lane1 < 4 * n + 4), roll(lines[n], (4 * n - 4 * d) % 128), line)
        out_ref[8 * d : 8 * d + 8] = jnp.where(row8 < 6, sent, jnp.where(row8 == 6, line, 0.0))


def batched_inverse(a, lane, row):
    base = lane - lane % 16
    for k in range(16):
        at_k = lane % 16 == k
        column = jnp.take_along_axis(a, base + k, axis=1)
        pivot = column[k : k + 1]
        line = jnp.where(at_k[0:1], 1.0, a[k : k + 1]) / pivot
        a = jnp.where(row == k, line, jnp.where(at_k, 0.0, a) - column * line)
    return a


def block_inverse(matrix, low, high):
    lane = lanes((16, 128))
    row = lax.broadcasted_iota(jnp.int32, (16, 128), 0)
    compact = jnp.where(lane % 16 == row, 1.0, 0.0)
    for n in range(low // 16, high // 16):
        compact = jnp.where(lane // 16 == n, matrix[16 * n : 16 * n + 16], compact)
    compact = batched_inverse(compact, lane, row)
    parts = []
    for n in range(8):
        active = low <= 16 * n < high
        parts.append(jnp.where(lane // 16 == n, compact, 0.0) if active else jnp.zeros((16, 128), F32))
    return jnp.concatenate(parts, axis=0)


def coarse_kernel(place_ref, in_ref, out_ref, g, e, ei, first, second, near):
    pr, pc = place_ref[0], place_ref[1]
    sub8 = lax.broadcasted_iota(jnp.int32, (8, 128), 0)

    for p in range(16):
        sums = {}
        for dr in range(3):
            r = p + 1 - dr
            if not 0 <= r < 16:
                continue
            for dq in range(4):
                k = 4 * dr + dq
                piece = in_ref[pl.ds(64 * r + k % 6, 8, stride=8), :]
                if dq == 0:
                    piece = jnp.where(sub8 < 7, roll(piece, 7, 0), 0.0)
                elif dq == 3:
                    piece = jnp.where(sub8 >= 1, roll(piece, 1, 0), 0.0)
                key = ((dq + 1) % 2, k >= 6)
                sums[key] = sums[key] + piece if key in sums else piece
        for par in range(2):
            total = jnp.zeros((8, 128), F32)
            if (par, False) in sums:
                total = total + sums[par, False]
            if (par, True) in sums:
                total = total + roll(sums[par, True], 64)
            g[pl.ds(16 * p + par, 8, stride=2), :] = total
    tally = jnp.sum(in_ref[pl.ds(6, 128, stride=8), :], axis=0, keepdims=True)
    tally = jnp.broadcast_to(tally, (128, 128)).T
    bb, bu, uu, uuu = (tally[4 * n : 4 * n + 4, 0:1] for n in range(4))
    by_lane = jnp.concatenate([g[0:128].T, g[128:256].T], axis=1)

    lane16, row16 = lanes((16, 128)), lax.broadcasted_iota(jnp.int32, (16, 128), 0)
    base = 20 + 6 * 3
    for p in range(16):
        own = g[16 * p : 16 * p + 16]
        terms = [(own, d, dp, dq) for d, dp, dq in ((0, 0, 0), (1, 0, 1))]
        terms.append((roll(own, 1, 0), 1, 0, -1))
        if p < 15:
            terms += [(own, d, 1, dq) for d, dq in ((3, -1), (4, 0), (5, 1))]
        if p > 0:
            last = g[16 * p - 16 : 16 * p]
            terms += [(roll(last, 15, 0), 3, -1, 1), (last, 4, -1, 0), (roll(last, 1, 0), 5, -1, -1)]
        halves = [jnp.zeros((16, 128), F32), jnp.zeros((16, 128), F32)]
        for x, d, dp, dq in terms:
            target = POS[p + dp] * 16
            h, off = target // 128, target % 128
            q = row16 + dq
            hit = (lane16 == off + q) & (q >= 0) & (q < 16)
            value = jnp.broadcast_to(x[:, base + d : base + d + 1], (16, 128))
            halves[h] = jnp.where(hit, value, halves[h])
        at = POS[p] * 16
        e[at : at + 16, 0:128] = halves[0]
        e[at : at + 16, 128:256] = halves[1]

    lane = lanes((128, 128))
    row = lax.broadcasted_iota(jnp.int32, (128, 128), 0)
    outer = block_inverse(e[0:128, 0:128], 0, 128)
    across = dot(outer, e[0:128, 128:256])
    schur = e[128:256, 128:256] - dot(e[128:256, 0:128], across)
    steps = []
    for low, high in ((0, 64), (64, 96), (96, 112)):
        inv = block_inverse(schur, low, high)
        link = jnp.where((row >= low) & (row < high) & (lane >= high), schur, 0.0)
        x = dot(inv, link)
        keep = jnp.where((row >= high) & (lane >= high), schur, 0.0)
        schur = keep - dot(link, x, TN)
        steps.append((inv, jnp.where((row == lane) & (row >= high), 1.0, 0.0) - x))
    inner = block_inverse(schur, 112, 128)
    for inv, y in reversed(steps):
        inner = inv + dot(dot(y, inner), y, NT)
    half = dot(across, inner)
    near_diag = outer + dot(half, across, NT)

    def ordered(top_half, bottom_half):
        blocks = [top_half[16 * n : 16 * n + 16] for n in range(8)]
        blocks += [bottom_half[16 * n : 16 * n + 16] for n in range(8)]
        blocks = [blocks[POS[p]] for p in range(16)]
        return jnp.concatenate(blocks[:8], axis=0), jnp.concatenate(blocks[8:], axis=0)

    left_top, left_bottom = ordered(near_diag, -half.T)
    right_top, right_bottom = ordered(-half, inner)
    top_left, bottom_left = ordered(left_top.T, right_top.T)
    top_right, bottom_right = ordered(left_bottom.T, right_bottom.T)
    ei[0:128, 0:128] = top_left
    ei[0:128, 128:256] = top_right
    ei[128:256, 0:128] = bottom_left
    ei[128:256, 128:256] = bottom_right

    def solve(z):
        return dot(z, ei[...])

    def apply(n, v):
        c = [by_lane[20 + 6 * n + d : 21 + 6 * n + d] for d in range(6)]
        total = c[0] * v
        for d, step in ((1, 1), (3, 15), (4, 16), (5, 17)):
            total = total + c[d] * roll(v, 256 - step) + roll(c[d] * v, step)
        return total

    def inner_product(a, b):
        return jnp.sum(a * b, axis=1, keepdims=True)

    wb, wu, wuu, zb, tuu = (by_lane[4 * n : 4 * n + 4] for n in range(5))
    c0 = solve(zb)
    f_c, g_c, h_c, k_c = apply(0, c0), apply(1, c0), apply(2, c0), apply(4, c0)
    grad0 = wb - f_c
    k0 = solve(grad0)
    f_k, g_k = apply(0, k0), apply(1, k0)
    rho0 = bb - 2.0 * inner_product(c0, wb) + inner_product(c0, f_c)
    energy0 = bu - 2.0 * inner_product(c0, wu) + inner_product(c0, g_c)
    curve0 = energy0 - inner_product(k0, grad0)
    a0 = rho0 / curve0
    e1 = c0 - a0 * k0
    f_e = f_c - a0 * f_k
    g_e = g_c - a0 * g_k
    grad1 = wb - f_e + a0 * (g_c - wu)
    k1 = solve(grad1)

    def second_norm(m0, m1, m2, v0, v1, v2, e_image, c_image, last):
        own = m0 - 2.0 * inner_product(e1, v0) + inner_product(e1, e_image)
        mixed = m1 - inner_product(c0, v1) - inner_product(e1, v1) + inner_product(e1, c_image)
        far = m2 - 2.0 * inner_product(c0, v2) + inner_product(c0, last)
        return own - 2.0 * a0 * mixed + a0 * a0 * far

    rho1 = second_norm(bb, bu, uu, wb, wu, wuu, f_e, g_c, h_c)
    energy1 = second_norm(bu, uu, uuu, wu, wuu, tuu, g_e, h_c, k_c)
    beta = rho1 / rho0
    cross = (
        bu
        - inner_product(c0, wu)
        - inner_product(e1, wu)
        + inner_product(e1, g_c)
        - a0 * (uu - 2.0 * inner_product(c0, wuu) + inner_product(c0, h_c))
        - inner_product(k0, grad1)
    )
    curve1 = energy1 - inner_product(k1, grad1) + 2.0 * beta * cross + beta * beta * curve0
    a1 = rho1 / curve1

    mine = lax.broadcasted_iota(jnp.int32, (32, 256), 0) // 4 == pc

    def zone(value):
        value = jnp.broadcast_to(value, (4, 256))
        return jnp.where(mine, jnp.concatenate([value] * 8, axis=0), 0.0)

    ab = a1 * beta
    stacks = (
        (
            zone(a1 * k1 + ab * k0 - e1),
            zone(-(a0 + ab) * c0 - a1 * e1),
            zone((a0 + ab) * c0 + a1 * e1),
            zone((a1 * a0) * c0),
        ),
        (
            zone(-(a1 * a0) * c0),
            zone(c0 - (a0 + ab) * k0 - a1 * k1),
            zone(-a0 - a1 - ab),
            zone(a1 * a0),
        ),
    )
    out_ref[...] = jnp.zeros((256, 128), F32)
    for n, (ref, stack) in enumerate(((first, stacks[0]), (second, stacks[1]))):
        stack = jnp.concatenate(stack, axis=0)
        ref[0:8] = jnp.zeros((8, 128), F32)
        ref[8:136] = stack[:, 0:128].T
        ref[136:264] = stack[:, 128:256].T
        ref[264:272] = jnp.zeros((8, 128), F32)
        for dr in range(3):
            p = jnp.clip(pr - 1 + dr, 0, 15)
            near[...] = ref[pl.ds(pl.multiple_of(16 * p, 16), 32), :]
            for dq in range(4):
                out_ref[pl.ds(16 * n + 4 * dr + dq, 8, stride=32), :] = near[pl.ds(7 + dq, 8, stride=2), :]


def outputs_kernel(rows_ref, first_ref, second_ref, w_ref, grid_ref, coef_ref, place_ref, m_ref, sol_ref, res_ref):
    pr, pc = place_ref[0], place_ref[1]
    slot = lax.broadcasted_iota(jnp.int32, (16, 128), 0)
    region_row = pr - 1 + slot // 4
    region_col = 2 * pc - 1 + slot % 4
    inside = (slot < 12) & (region_row >= 0) & (region_row < REG) & (region_col >= 0) & (region_col < REG)
    window = jnp.where(inside, region_row * REG + region_col, -1).astype(F32)
    total = m_ref[0:32]
    for n in range(1, 8):
        total = total + m_ref[32 * n : 32 * n + 32]
    top, bottom = total[0:16], total[16:32]
    lane = lanes((16, 128))
    steps = jnp.where(slot == 0, roll(bottom[5:6], 64), jnp.where(slot == 1, roll(bottom[5:6], 32), 0.0))
    m = jnp.concatenate(
        [
            jnp.where((lane >= 64) & (lane < 96), roll(bottom, 32), 0.0),
            jnp.where(lane < 64, top, 0.0),
            jnp.where(lane < 64, roll(top, 64), 0.0),
            jnp.where(lane < 32, bottom, 0.0),
            steps,
            jnp.zeros((48, 128), F32),
        ],
        axis=0,
    ).T
    c1, c2, c3 = parts_of(m[0:96, 0:64], 3)
    left = jnp.concatenate([c1, c1, c2, c2, c1, c3], axis=1)
    shape = (32, 128)
    p1, p2 = (jnp.broadcast_to(m[0:32, 64 + n : 65 + n], shape) for n in range(2))

    def step(k, _):
        rows = []
        for n in range(8):
            r = 8 * k + n
            z = jnp.where(grid_ref[pl.ds(r, 1), :] == window, grid_ref[pl.ds(128 + r, 1), :], 0.0)
            rows.append(jnp.concatenate([z, w_ref[r], first_ref[r, 32:48], second_ref[r, 32:48]], axis=0))
        r1, r2, r3 = parts_of(jnp.concatenate(rows, axis=1), 3)
        d = fast_dot(left, jnp.concatenate([r1, r2, r1, r2, r3, r1], axis=0))
        for n in range(8):
            r = 8 * k + n
            b, u, uu = rows_ref[r], first_ref[r, 0:32], second_ref[r, 0:32]
            e = d[:, 128 * n : 128 * n + 128]
            inv = coef_ref[5, pl.ds(r + 16, 1), :]
            res_ref[pl.ds(r, 32, stride=128), :] = b + p1 * u + p2 * uu + e[0:32]
            sol_ref[pl.ds(r, 32, stride=128), :] = inv * (e[32:64] - p1 * b - p2 * u) + e[64:96]
        return 0

    lax.fori_loop(0, 16, step, 0)


def shape_of(*dims):
    return jax.ShapeDtypeStruct(dims, F32)


def kept(*dims):
    return pltpu.VMEM(dims, F32)


def vmem(*dims):
    return pltpu.VMEM(dims, F32)


def body(load_currents, labels, bump_height, horizontal_class, vertical_class, pad_class, edge_table, pad_table):
    pr, pc = lax.axis_index(ROW), lax.axis_index(COL)
    rows, cols = lax.axis_size(ROW), lax.axis_size(COL)
    place = jnp.stack([pr, pc]).astype(jnp.int32)
    loads = load_currents.reshape(-1, 128)
    grid, first_rows = pl.pallas_call(
        prepare_kernel,
        out_shape=(kept(1024, 128), shape_of(HALO, SUB, 128)),
        compiler_params=limited,
        in_specs=[scalars] + [outside] * 8,
        out_specs=(whole, whole),
        scratch_shapes=[pltpu.SMEM((8,), F32), pltpu.SMEM((8,), F32), vmem(32, 8, 128)]
        + [pltpu.VMEM((128, 128), jnp.int32)] * 4
        + [pltpu.SemaphoreType.DMA((8,))],
    )(
        place,
        *(
            pltpu.with_memory_space_constraint(x, pltpu.HBM)
            for x in (
                edge_table, pad_table, load_currents, labels, bump_height,
                horizontal_class, vertical_class, pad_class,
            )
        ),
    )
    down = [(i, i + 1) for i in range(rows - 1)]
    bottom = lax.ppermute(first_rows, ROW, [(b, a) for a, b in down])
    by_rows, own, last_rows = pl.pallas_call(
        pack_kernel,
        out_shape=(kept(128, 32, 128), kept(GROUPS, SUB, 128), shape_of(HALO, SUB, 128)),
        compiler_params=limited,
        in_specs=[whole] * 2,
        out_specs=(whole,) * 3,
    )(loads, grid)
    top = lax.ppermute(last_rows, ROW, down)
    own = pl.pallas_call(
        corner_kernel, out_shape=shape_of(GROUPS, SUB, 128), in_specs=[whole] * 3, out_specs=whole, compiler_params=limited
    )(own, top, bottom)
    right = [(i, i + 1) for i in range(cols - 1)]
    beside_left = lax.ppermute(own, COL, right)
    beside_right = lax.ppermute(own, COL, [(b, a) for a, b in right])
    first, second, w, coef, payload = pl.pallas_call(
        fields_kernel,
        out_shape=(
            kept(128, 48, 128),
            kept(128, 48, 128),
            kept(128, 16, 128),
            kept(6, 160, 128),
            shape_of(64, 128),
        ),
        compiler_params=limited,
        in_specs=[scalars] + [whole] * 7,
        out_specs=(whole,) * 5,
        scratch_shapes=[
            vmem(5, 160, 128),
            vmem(GROUPS + 2, SUB, 128),
            vmem(GROUPS + 2, SUB, 128),
            vmem(GROUPS + 2, 16, 128),
            vmem(GROUPS + 2, 16, 128),
            vmem(GROUPS + 2, 48, 128),
            vmem(GROUPS + 2, 48, 128),
            vmem(2 * GROUPS, 16, 128),
            vmem(2 * GROUPS, 48, 128),
            vmem(2 * GROUPS, 48, 128),
            vmem(2, GROUPS, 8, 128),
            vmem(144, 48, 128),
            vmem(144, 48, 128),
            vmem(96, 256),
        ],
    )(place, by_rows, grid, top, bottom, own, beside_left, beside_right)
    sent = jnp.broadcast_to(payload.reshape(1, cols, 8, 128), (rows, cols, 8, 128)).reshape(-1, 8, 128)
    everything = lax.all_to_all(sent, ROW + COL, 0, 0, tiled=True).reshape(-1, 128)
    found = pl.pallas_call(
        coarse_kernel,
        out_shape=shape_of(256, 128),
        compiler_params=limited,
        in_specs=[scalars, whole],
        out_specs=whole,
        scratch_shapes=[
            vmem(256, 128),
            vmem(256, 256),
            vmem(256, 256),
            vmem(272, 128),
            vmem(272, 128),
            vmem(32, 128),
        ],
    )(place, everything)
    matrix = lax.all_to_all(found.reshape(cols, 32, 128), COL, 0, 0, tiled=True).reshape(-1, 128)
    solution, residual = pl.pallas_call(
        outputs_kernel,
        out_shape=(shape_of(4096, 128), shape_of(4096, 128)),
        compiler_params=limited,
        in_specs=[whole] * 6 + [scalars, whole],
        out_specs=(whole, whole),
    )(by_rows, first, second, w, grid, coef, place, matrix)
    return solution.reshape(load_currents.shape), residual.reshape(load_currents.shape)


def solution(mesh):
    finer = Mesh(mesh.devices.reshape(4, 4, 4, 2), ("row_0", "row_1", "col_0", "col_1"))
    grid = P(ROW, COL)
    return jax.shard_map(
        body,
        mesh=finer,
        in_specs=(P(None, ROW, COL), grid, grid, grid, grid, grid, P(), P()),
        out_specs=(P(None, ROW, COL), P(None, ROW, COL)),
        check_vma=False,
    )
```

time: 121 us -> 102 us (0.84)
  Pallas kernels: 64.7 us -> 47.9 us
  local copies, waits for them, and re-layouts: 2.87 us -> 0.05 us
  blocking collectives: 34.3 us -> 36.4 us
    pallas_call x5 -> x4, Pallas kernels: 51 us -> 39.2 us  [the longest x1 22.7 us: body(): pl.pallas_call(fields_kernel, out_shape=(kept(128, 48, 128), kept(128, 48...]
    pallas_call x1, Pallas kernels: 12 us -> 8.67 us  [body(): pl.pallas_call(outputs_kernel, out_shape=(shape_of(4096, 128), shape_of(4...]
    all_to_all x2, blocking collectives: 34.3 us -> 36.4 us  [the longest x1 27.8 us: body(): lax.all_to_all(sent, ROW + COL, 0, 0, tiled=True).reshape(-1, 128)]
    pallas_call x1, Pallas kernels: 1.73 us -> 0.09 us  [body(): pl.pallas_call(corner_kernel, out_shape=shape_of(GROUPS, SUB, 128), in_sp...]
    broadcast_in_dim x2 -> x1, local copies, waits for them, and re-layouts: 1.58 us -> 0.04 us  [body(): jnp.broadcast_to(payload.reshape(1, cols, 8, 128), (rows, cols, 8, 128))]
    unnamed x8 -> x2, local copies, waits for them, and re-layouts: 1.29 us -> 0.01 us
  transfers between devices with their start and end apart: 4 -> 4, of which waited for: 3 -> 3; matrix products, arithmetic and copies ran while one was open for 0% -> 0% of each run, Pallas kernels for 4% -> 2%
where the time goes in v3:
time: 102 us
  Pallas kernels  47.9 us (47%)
  blocking collectives  36.4 us (36%)
  starting transfers between devices  12.8 us (13%)
  waiting for transfers between devices  3.73 us (4%)
    all_to_all x1, blocking collectives, body(): lax.all_to_all(sent, ROW + COL, 0, 0, tiled=True).reshape(-1, 128)  27.8 us
    pallas_call x1, Pallas kernels, body(): pl.pallas_call(fields_kernel, out_shape=(kept(128, 48, 128), kept(128, 48...  22.7 us
    pallas_call x1, Pallas kernels, body(): pl.pallas_call(coarse_kernel, out_shape=shape_of(256, 128), compiler_para...  12.6 us
    pallas_call x1, Pallas kernels, body(): pl.pallas_call(outputs_kernel, out_shape=(shape_of(4096, 128), shape_of(4...  8.67 us
    all_to_all x1, blocking collectives, body(): lax.all_to_all(found.reshape(cols, 32, 128), COL, 0, 0, tiled=True)  8.58 us
    ppermute x1, starting transfers between devices, body(): top = lax.ppermute(last_rows, ROW, down)  4.99 us
    ppermute x1, starting transfers between devices, body(): beside_right = lax.ppermute(own, COL, [(b, a) for a, b in right])  3.44 us
    ppermute x1, starting transfers between devices, body(): beside_left = lax.ppermute(own, COL, right)  3.11 us
  transfers between devices with their start and end apart: 4, of which 3 were waited for; matrix products, arithmetic and copies ran while one was open for 0% of the time, Pallas kernels for 2%

profile of v3, /device:TPU:1, one launch (start us, length us, event | category | flops | bytes accessed | tf_op | source)
XLA Modules:
  0.0 101.7 jit_solution(1001873717808880460)
XLA Ops:
  0.6 0.0 copy-start
  0.7 0.1 pad_add_fusion.place_ref
  0.7 1.8 %shard_map.95 = (f32[1024,128]{1,0:T(8,128)S(1)}, f32[3,40,128]{2,1,0:T(8,128)S(1)}) custom-call(s32[2]{0:T(128)S(1)} %pad_add_fusion.place_ref, f32[8]{0:T(128)} %edge_hbm.1, f32[8]{0:T(128)} %pad_hbm.1, f32[32,128,128]{2,1,0:T(8,128)} %load_hbm.1, s32[128,128]{1,0:T(8,128)} %label_hbm.1, f32[128,128]{1,0:T(8,128)} %bump_hbm.1, s32[128,128]{1,0:T(8,128)} %across_hbm.1, ...), custom_call_target="tpu_custom_call" | custom-call | tf_op jit(solution)/shard_map/pallas_call | solution.py:632
  2.6 1.3 %collective-permute-start.1 = (f32[3,40,128]{2,1,0:T(8,128)S(1)}, f32[3,40,128]{2,1,0:T(8,128)S(1)}, u32[]{:S(2)}, u32[]{:S(2)}) collective-permute-start(f32[3,40,128]{2,1,0:T(8,128)S(1)} %get-tuple-element.17), channel_id=1, source_target_pairs={{8,0},{16,8},{24,16},{32,24},{40,32},{48,40},{56,48},{64,56},{72,6... | collective-permute-start | bytes 184328 | tf_op jit(solution)/shard_map/ppermute | solution.py:652
  3.9 0.0 copy-done
  3.9 2.1 %shard_map.96 = (f32[128,32,128]{2,1,0:T(8,128)S(1)}, f32[9,40,128]{2,1,0:T(8,128)S(1)}, f32[3,40,128]{2,1,0:T(8,128)S(1)}) custom-call(f32[4096,128]{1,0:T(8,128)S(1)} %bitcast.10, f32[1024,128]{1,0:T(8,128)S(1)} %get-tuple-element.14.grid_ref), custom_call_target="tpu_custom_call" | custom-call | tf_op jit(solution)/shard_map/pallas_call | solution.py:653
  6.0 5.0 %collective-permute-start = (f32[3,40,128]{2,1,0:T(8,128)S(1)}, f32[3,40,128]{2,1,0:T(8,128)S(1)}, u32[]{:S(2)}, u32[]{:S(2)}) collective-permute-start(f32[3,40,128]{2,1,0:T(8,128)S(1)} %get-tuple-element.16), channel_id=1, source_target_pairs={{0,8},{8,16},{16,24},{24,32},{32,40},{40,48},{48,56},{56,64},{64,7... | collective-permute-start | bytes 184328 | tf_op jit(solution)/shard_map/ppermute | solution.py:660
  11.0 0.0 collective-permute-done.1.bottom_ref
  11.0 1.3 %collective-permute-done.top_ref = f32[3,40,128]{2,1,0:T(8,128)S(1)} collective-permute-done((f32[3,40,128]{2,1,0:T(8,128)S(1)}, f32[3,40,128]{2,1,0:T(8,128)S(1)}, u32[]{:S(2)}, u32[]{:S(2)}) %collective-permute-start) | collective-permute-done | bytes 61472 | tf_op jit(solution)/shard_map/ppermute | solution.py:660
  12.2 0.1 shard_map.97.own_ref
  12.3 3.4 %collective-permute-start.3 = (f32[9,40,128]{2,1,0:T(8,128)S(1)}, f32[9,40,128]{2,1,0:T(8,128)S(1)}, u32[]{:S(2)}, u32[]{:S(2)}) collective-permute-start(f32[9,40,128]{2,1,0:T(8,128)S(1)} %shard_map.97.own_ref), channel_id=1, source_target_pairs={{1,0},{2,1},{3,2},{4,3},{5,4},{6,5},{7,6},{9,8},{10,9},{11,10},{12... | collective-permute-start | bytes 552968 | tf_op jit(solution)/shard_map/ppermute | solution.py:666
  15.8 3.1 %collective-permute-start.2 = (f32[9,40,128]{2,1,0:T(8,128)S(1)}, f32[9,40,128]{2,1,0:T(8,128)S(1)}, u32[]{:S(2)}, u32[]{:S(2)}) collective-permute-start(f32[9,40,128]{2,1,0:T(8,128)S(1)} %shard_map.97.own_ref), channel_id=1, source_target_pairs={{0,1},{1,2},{2,3},{3,4},{4,5},{5,6},{6,7},{8,9},{9,10},{10,11},{11... | collective-permute-start | bytes 552968 | tf_op jit(solution)/shard_map/ppermute | solution.py:665
  18.9 1.3 %collective-permute-done.3.right_ref = f32[9,40,128]{2,1,0:T(8,128)S(1)} collective-permute-done((f32[9,40,128]{2,1,0:T(8,128)S(1)}, f32[9,40,128]{2,1,0:T(8,128)S(1)}, u32[]{:S(2)}, u32[]{:S(2)}) %collective-permute-start.3) | collective-permute-done | bytes 184352 | tf_op jit(solution)/shard_map/ppermute | solution.py:666
  20.2 1.2 %collective-permute-done.2.left_ref = f32[9,40,128]{2,1,0:T(8,128)S(1)} collective-permute-done((f32[9,40,128]{2,1,0:T(8,128)S(1)}, f32[9,40,128]{2,1,0:T(8,128)S(1)}, u32[]{:S(2)}, u32[]{:S(2)}) %collective-permute-start.2) | collective-permute-done | bytes 184352 | tf_op jit(solution)/shard_map/ppermute | solution.py:665
  21.4 22.7 %shard_map.98 = (f32[128,48,128]{2,1,0:T(8,128)S(1)}, f32[128,48,128]{2,1,0:T(8,128)S(1)}, f32[128,16,128]{2,1,0:T(8,128)S(1)}, f32[6,160,128]{2,1,0:T(8,128)S(1)}, f32[64,128]{1,0:T(8,128)S(1)}) custom-call(s32[2]{0:T(128)S(1)} %pad_add_fusion.place_ref, f32[128,32,128]{2,1,0:T(8,128)S(1)} %get-tuple-element.15.rows_ref, ...), custom_call_target="tpu_custom_call" | custom-call | tf_op jit(solution)/shard_map/pallas_call | solution.py:667
  44.1 27.8 %all_to_all.10 = f32[128,8,128]{2,1,0:T(8,128)S(1)} all-to-all(f32[128,8,128]{2,1,0:T(8,128)S(1)} %bitcast.15), channel_id=1, replica_groups=mesh['row_0'=4,'row_1'=4,'col_0'=4,'col_1'=2] {'row_0','row_1','col_0','..., dimensions={0} | all-to-all | bytes 1048576 | tf_op jit(solution)/shard_map/all_to_all | solution.py:697
  71.9 12.6 %shard_map.99 = f32[256,128]{1,0:T(8,128)S(1)} custom-call(s32[2]{0:T(128)S(1)} %pad_add_fusion.place_ref, f32[1024,128]{1,0:T(8,128)S(1)} %bitcast.11), custom_call_target="tpu_custom_call" | custom-call | tf_op jit(solution)/shard_map/pallas_call | solution.py:698
  84.5 8.6 %all_to_all.11 = f32[8,32,128]{2,1,0:T(8,128)S(1)} all-to-all(f32[8,32,128]{2,1,0:T(8,128)S(1)} %bitcast.13), channel_id=1, replica_groups=mesh['row_0'=4,'row_1'=4,'col_0'=4,'col_1'=2] {'col_0','col_1'}, dimensions={0} | all-to-all | bytes 262144 | tf_op jit(solution)/shard_map/all_to_all | solution.py:713
  93.1 8.7 %shard_map.100 = (f32[4096,128]{1,0:T(8,128)}, f32[4096,128]{1,0:T(8,128)}) custom-call(f32[128,32,128]{2,1,0:T(8,128)S(1)} %get-tuple-element.15.rows_ref, f32[128,48,128]{2,1,0:T(8,128)S(1)} %get-tuple-element.19.first_ref, f32[128,48,128]{2,1,0:T(8,128)S(1)} %get-tuple-element.20.second_ref, f32[128,16,128]{2,1,0:T(8,128)S(1)} %get-tuple-element.21.w_ref, ...), custom_call_target="tpu_custom_call" | custom-call | tf_op jit(solution)/shard_map/pallas_call | solution.py:714
  (1 shorter events, 0.0 us)
Async XLA Ops:
  0.6 3.2 %copy-start = (f32[32,128,128]{2,1,0:T(8,128)S(1)}, f32[32,128,128]{2,1,0:T(8,128)}, u32[]{:S(2)}) copy-start(f32[32,128,128]{2,1,0:T(8,128)} %load_hbm.1) | copy-start | bytes 6291460
  2.6 8.4 %collective-permute-start.1 = (f32[3,40,128]{2,1,0:T(8,128)S(1)}, f32[3,40,128]{2,1,0:T(8,128)S(1)}, u32[]{:S(2)}, u32[]{:S(2)}) collective-permute-start(f32[3,40,128]{2,1,0:T(8,128)S(1)} %get-tuple-element.17), channel_id=1, source_target_pairs={{8,0},{16,8},{24,16},{32,24},{40,32},{48,40},{56,48},{64,56},{72,6... | collective-permute-start | bytes 184328 | tf_op jit(solution)/shard_map/ppermute | solution.py:652
  6.0 6.3 %collective-permute-start = (f32[3,40,128]{2,1,0:T(8,128)S(1)}, f32[3,40,128]{2,1,0:T(8,128)S(1)}, u32[]{:S(2)}, u32[]{:S(2)}) collective-permute-start(f32[3,40,128]{2,1,0:T(8,128)S(1)} %get-tuple-element.16), channel_id=1, source_target_pairs={{0,8},{8,16},{16,24},{24,32},{32,40},{40,48},{48,56},{56,64},{64,7... | collective-permute-start | bytes 184328 | tf_op jit(solution)/shard_map/ppermute | solution.py:660
  12.3 7.8 %collective-permute-start.3 = (f32[9,40,128]{2,1,0:T(8,128)S(1)}, f32[9,40,128]{2,1,0:T(8,128)S(1)}, u32[]{:S(2)}, u32[]{:S(2)}) collective-permute-start(f32[9,40,128]{2,1,0:T(8,128)S(1)} %shard_map.97.own_ref), channel_id=1, source_target_pairs={{1,0},{2,1},{3,2},{4,3},{5,4},{6,5},{7,6},{9,8},{10,9},{11,10},{12... | collective-permute-start | bytes 552968 | tf_op jit(solution)/shard_map/ppermute | solution.py:666
  15.8 5.6 %collective-permute-start.2 = (f32[9,40,128]{2,1,0:T(8,128)S(1)}, f32[9,40,128]{2,1,0:T(8,128)S(1)}, u32[]{:S(2)}, u32[]{:S(2)}) collective-permute-start(f32[9,40,128]{2,1,0:T(8,128)S(1)} %shard_map.97.own_ref), channel_id=1, source_target_pairs={{0,1},{1,2},{2,3},{3,4},{4,5},{5,6},{6,7},{8,9},{9,10},{10,11},{11... | collective-permute-start | bytes 552968 | tf_op jit(solution)/shard_map/ppermute | solution.py:665

commit v4 on v3

--- a/solution.py
+++ b/solution.py
@@ -54,7 +54,7 @@
 
 def prepare_kernel(
     place_ref, edge_hbm, pad_hbm, load_hbm, label_hbm, bump_hbm, across_hbm, down_hbm, pad_class_hbm,
-    grid_ref, first_ref, edge_ref, pad_ref, load_ref, label_ref, across_ref, down_ref, pad_class_ref, done,
+    grid_ref, first_ref, last_ref, edge_ref, pad_ref, load_ref, load_end_ref, label_ref, across_ref, down_ref, pad_class_ref, done,
 ):
     copies = [
         pltpu.make_async_copy(source, target, done.at[n])
@@ -68,6 +68,7 @@
                 (label_hbm, label_ref),
                 (bump_hbm, grid_ref.at[pl.ds(128, 128)]),
                 (load_hbm.at[:, pl.ds(0, 8)], load_ref),
+                (load_hbm.at[:, pl.ds(120, 8)], load_end_ref),
             )
         )
     ]
@@ -95,9 +96,11 @@
     for n in range(HALO):
         first_ref[n, 0:32] = load_ref[:, n]
         first_ref[n, 32:40] = grid_ref[pl.ds(n, 8, stride=128), :]
-
-
-def pack_kernel(load_ref, grid_ref, rows_ref, own_ref, last_ref):
+        last_ref[n, 0:32] = load_end_ref[:, 8 - HALO + n]
+        last_ref[n, 32:40] = grid_ref[pl.ds(128 - HALO + n, 8, stride=128), :]
+
+
+def pack_kernel(load_ref, grid_ref, rows_ref, own_ref):
     lane = lanes((32, 128)) // 8
 
     def group(g, slots):
@@ -119,10 +122,6 @@
         return 0
 
     lax.fori_loop(1, 8, step, 0)
-    for n in range(HALO):
-        r = 128 - HALO + n
-        last_ref[n, 0:32] = rows_ref[r]
-        last_ref[n, 32:40] = grid_ref[pl.ds(r, 8, stride=128), :]
 
 
 def corner_kernel(own_ref, top_ref, bottom_ref, out_ref):
@@ -308,21 +307,19 @@
 
     passes(second_image, -1, 129)
 
-    def third_image(g, s):
-        i = 8 * g + s
-        second_ref[8 * g - 8 + s] = image(y1[i], y1[i - 1], y1[i + 1], q1, g, s, lane48)
-
-    passes(third_image, 0, 128)
-
     gram[...] = jnp.zeros((96, 256), F32)
 
-    def products(k, sums):
+    def third_image(g, sums):
         left, every = [], []
         sums = list(sums)
-        for n in range(16):
-            r = 16 * k + n
-            b, f1, f2, y0r, y1r = rows_ref[r], first_ref[r], second_ref[r], y0[r + 8], y1[r + 8]
-            left.append(jnp.concatenate([basis(r + 16), y0r[32:48], y1r[32:48]], axis=0))
+        for s in range(8):
+            i = 8 * g + s
+            r = i - 8
+            y0r, y1r = y0[i], y1[i]
+            f2 = image(y1r, y1[i - 1], y1[i + 1], q1, g, s, lane48)
+            second_ref[r] = f2
+            b, f1 = rows_ref[r], first_ref[r]
+            left.append(jnp.concatenate([basis(i + 8), y0r[32:48], y1r[32:48]], axis=0))
             every.append(jnp.concatenate([b, w_ref[r], f1, f2], axis=0))
             pairs = ((y0r, b), (y0r, f1), (y1r, f1), (y1r, f2))
             sums = [t + p[0:32] * q[0:32] for t, (p, q) in zip(sums, pairs)]
@@ -332,7 +329,7 @@
         return tuple(sums)
 
     zero = jnp.zeros((32, 128), F32)
-    sums = lax.fori_loop(0, 8, products, (zero, zero, zero, zero))
+    sums = lax.fori_loop(1, 17, third_image, (zero, zero, zero, zero))
 
     a0, a1 = gram[0:48, 0:128] + gram[48:96, 0:128], gram[0:48, 128:256] + gram[48:96, 128:256]
     zr, w0, t0, w1, t1 = a0[0:16], a0[16:32], a0[32:48], a1[16:32], a1[32:48]
@@ -368,12 +365,18 @@
 
 def batched_inverse(a, lane, row):
     base = lane - lane % 16
-    for k in range(16):
-        at_k = lane % 16 == k
-        column = jnp.take_along_axis(a, base + k, axis=1)
-        pivot = column[k : k + 1]
-        line = jnp.where(at_k[0:1], 1.0, a[k : k + 1]) / pivot
-        a = jnp.where(row == k, line, jnp.where(at_k, 0.0, a) - column * line)
+    for k in range(0, 16, 2):
+        at_k, at_n = lane % 16 == k, lane % 16 == k + 1
+        left = jnp.take_along_axis(a, base + k, axis=1)
+        right = jnp.take_along_axis(a, base + k + 1, axis=1)
+        p, q, r, t = left[k : k + 1], right[k : k + 1], left[k + 1 : k + 2], right[k + 1 : k + 2]
+        inverse = 1.0 / (p * t - q * r)
+        upper = jnp.where(at_k[0:1], 1.0, jnp.where(at_n[0:1], 0.0, a[k : k + 1]))
+        lower = jnp.where(at_n[0:1], 1.0, jnp.where(at_k[0:1], 0.0, a[k + 1 : k + 2]))
+        first = (t * upper - q * lower) * inverse
+        second = (p * lower - r * upper) * inverse
+        rest = jnp.where(at_k | at_n, 0.0, a) - left * first - right * second
+        a = jnp.where(row == k, first, jnp.where(row == k + 1, second, rest))
     return a
 
 
@@ -563,53 +566,59 @@
                 out_ref[pl.ds(16 * n + 4 * dr + dq, 8, stride=32), :] = near[pl.ds(7 + dq, 8, stride=2), :]
 
 
-def outputs_kernel(rows_ref, first_ref, second_ref, w_ref, grid_ref, coef_ref, place_ref, m_ref, sol_ref, res_ref):
-    pr, pc = place_ref[0], place_ref[1]
-    slot = lax.broadcasted_iota(jnp.int32, (16, 128), 0)
-    region_row = pr - 1 + slot // 4
-    region_col = 2 * pc - 1 + slot % 4
-    inside = (slot < 12) & (region_row >= 0) & (region_row < REG) & (region_col >= 0) & (region_col < REG)
-    window = jnp.where(inside, region_row * REG + region_col, -1).astype(F32)
-    total = m_ref[0:32]
-    for n in range(1, 8):
-        total = total + m_ref[32 * n : 32 * n + 32]
-    top, bottom = total[0:16], total[16:32]
-    lane = lanes((16, 128))
-    steps = jnp.where(slot == 0, roll(bottom[5:6], 64), jnp.where(slot == 1, roll(bottom[5:6], 32), 0.0))
-    m = jnp.concatenate(
-        [
-            jnp.where((lane >= 64) & (lane < 96), roll(bottom, 32), 0.0),
-            jnp.where(lane < 64, top, 0.0),
-            jnp.where(lane < 64, roll(top, 64), 0.0),
-            jnp.where(lane < 32, bottom, 0.0),
-            steps,
-            jnp.zeros((48, 128), F32),
-        ],
-        axis=0,
-    ).T
-    c1, c2, c3 = parts_of(m[0:96, 0:64], 3)
-    left = jnp.concatenate([c1, c1, c2, c2, c1, c3], axis=1)
-    shape = (32, 128)
-    p1, p2 = (jnp.broadcast_to(m[0:32, 64 + n : 65 + n], shape) for n in range(2))
-
-    def step(k, _):
+def outputs_kernel(
+    place_ref, rows_ref, first_ref, second_ref, w_ref, grid_ref, coef_ref, m_ref, sol_ref, res_ref,
+    left_ref, step_ref, window_ref,
+):
+    block = pl.program_id(0)
+
+    @pl.when(block == 0)
+    def _():
+        pr, pc = place_ref[0], place_ref[1]
+        slot = lax.broadcasted_iota(jnp.int32, (16, 128), 0)
+        region_row = pr - 1 + slot // 4
+        region_col = 2 * pc - 1 + slot % 4
+        inside = (slot < 12) & (region_row >= 0) & (region_row < REG) & (region_col >= 0) & (region_col < REG)
+        window_ref[...] = jnp.where(inside, region_row * REG + region_col, -1).astype(F32)
+        total = m_ref[0:32]
+        for n in range(1, 8):
+            total = total + m_ref[32 * n : 32 * n + 32]
+        top, bottom = total[0:16], total[16:32]
+        lane = lanes((16, 128))
+        steps = jnp.where(slot == 0, roll(bottom[5:6], 64), jnp.where(slot == 1, roll(bottom[5:6], 32), 0.0))
+        m = jnp.concatenate(
+            [
+                jnp.where((lane >= 64) & (lane < 96), roll(bottom, 32), 0.0),
+                jnp.where(lane < 64, top, 0.0),
+                jnp.where(lane < 64, roll(top, 64), 0.0),
+                jnp.where(lane < 32, bottom, 0.0),
+                steps,
+                jnp.zeros((48, 128), F32),
+            ],
+            axis=0,
+        ).T
+        c1, c2, c3 = parts_of(m[0:96, 0:64], 3)
+        left_ref[...] = jnp.concatenate([c1, c1, c2, c2, c1, c3], axis=1)
+        for n in range(2):
+            step_ref[n] = jnp.broadcast_to(m[0:32, 64 + n : 65 + n], (32, 128))
+
+    left, window = left_ref[...], window_ref[...]
+    for part in range(2):
         rows = []
         for n in range(8):
-            r = 8 * k + n
+            r = 16 * block + 8 * part + n
             z = jnp.where(grid_ref[pl.ds(r, 1), :] == window, grid_ref[pl.ds(128 + r, 1), :], 0.0)
             rows.append(jnp.concatenate([z, w_ref[r], first_ref[r, 32:48], second_ref[r, 32:48]], axis=0))
         r1, r2, r3 = parts_of(jnp.concatenate(rows, axis=1), 3)
         d = fast_dot(left, jnp.concatenate([r1, r2, r1, r2, r3, r1], axis=0))
         for n in range(8):
-            r = 8 * k + n
+            r = 16 * block + 8 * part + n
             b, u, uu = rows_ref[r], first_ref[r, 0:32], second_ref[r, 0:32]
             e = d[:, 128 * n : 128 * n + 128]
             inv = coef_ref[5, pl.ds(r + 16, 1), :]
-            res_ref[pl.ds(r, 32, stride=128), :] = b + p1 * u + p2 * uu + e[0:32]
-            sol_ref[pl.ds(r, 32, stride=128), :] = inv * (e[32:64] - p1 * b - p2 * u) + e[64:96]
-        return 0
-
-    lax.fori_loop(0, 16, step, 0)
+            p1, p2 = step_ref[0], step_ref[1]
+            res_ref[:, 8 * part + n] = b + p1 * u + p2 * uu + e[0:32]
+            sol_ref[:, 8 * part + n] = inv * (e[32:64] - p1 * b - p2 * u) + e[64:96]
 
 
 def shape_of(*dims):
@@ -629,15 +638,15 @@
     rows, cols = lax.axis_size(ROW), lax.axis_size(COL)
     place = jnp.stack([pr, pc]).astype(jnp.int32)
     loads = load_currents.reshape(-1, 128)
-    grid, first_rows = pl.pallas_call(
+    grid, first_rows, last_rows = pl.pallas_call(
         prepare_kernel,
-        out_shape=(kept(1024, 128), shape_of(HALO, SUB, 128)),
+        out_shape=(kept(1024, 128), shape_of(HALO, SUB, 128), shape_of(HALO, SUB, 128)),
         compiler_params=limited,
         in_specs=[scalars] + [outside] * 8,
-        out_specs=(whole, whole),
-        scratch_shapes=[pltpu.SMEM((8,), F32), pltpu.SMEM((8,), F32), vmem(32, 8, 128)]
+        out_specs=(whole,) * 3,
+        scratch_shapes=[pltpu.SMEM((8,), F32), pltpu.SMEM((8,), F32), vmem(32, 8, 128), vmem(32, 8, 128)]
         + [pltpu.VMEM((128, 128), jnp.int32)] * 4
-        + [pltpu.SemaphoreType.DMA((8,))],
+        + [pltpu.SemaphoreType.DMA((9,))],
     )(
         place,
         *(
@@ -650,14 +659,14 @@
     )
     down = [(i, i + 1) for i in range(rows - 1)]
     bottom = lax.ppermute(first_rows, ROW, [(b, a) for a, b in down])
-    by_rows, own, last_rows = pl.pallas_call(
+    top = lax.ppermute(last_rows, ROW, down)
+    by_rows, own = pl.pallas_call(
         pack_kernel,
-        out_shape=(kept(128, 32, 128), kept(GROUPS, SUB, 128), shape_of(HALO, SUB, 128)),
+        out_shape=(kept(128, 32, 128), kept(GROUPS, SUB, 128)),
         compiler_params=limited,
         in_specs=[whole] * 2,
-        out_specs=(whole,) * 3,
+        out_specs=(whole,) * 2,
     )(loads, grid)
-    top = lax.ppermute(last_rows, ROW, down)
     own = pl.pallas_call(
         corner_kernel, out_shape=shape_of(GROUPS, SUB, 128), in_specs=[whole] * 3, out_specs=whole, compiler_params=limited
     )(own, top, bottom)
@@ -711,14 +720,16 @@
         ],
     )(place, everything)
     matrix = lax.all_to_all(found.reshape(cols, 32, 128), COL, 0, 0, tiled=True).reshape(-1, 128)
-    solution, residual = pl.pallas_call(
+    by_block = pl.BlockSpec((32, 16, 128), lambda k: (0, k, 0))
+    return pl.pallas_call(
         outputs_kernel,
-        out_shape=(shape_of(4096, 128), shape_of(4096, 128)),
+        grid=(8,),
+        out_shape=(shape_of(32, 128, 128), shape_of(32, 128, 128)),
         compiler_params=limited,
-        in_specs=[whole] * 6 + [scalars, whole],
-        out_specs=(whole, whole),
-    )(by_rows, first, second, w, grid, coef, place, matrix)
-    return solution.reshape(load_currents.shape), residual.reshape(load_currents.shape)
+        in_specs=[scalars] + [whole] * 7,
+        out_specs=(by_block, by_block),
+        scratch_shapes=[pltpu.VMEM((96, 384), jnp.bfloat16), vmem(2, 32, 128), vmem(16, 128)],
+    )(place, by_rows, first, second, w, grid, coef, matrix)
 
 
 def solution(mesh):

time: 102 us -> 95.5 us (0.936)
  Pallas kernels: 47.9 us -> 44.1 us
  blocking collectives: 36.4 us -> 33.6 us
    all_to_all x1, blocking collectives: 27.8 us -> 25 us  [body(): lax.all_to_all(sent, ROW + COL, 0, 0, tiled=True).reshape(-1, 128)]
    pallas_call x1, Pallas kernels: 12.6 us -> 10.1 us  [body(): pl.pallas_call(coarse_kernel, out_shape=shape_of(256, 128), compiler_para...]
    ppermute x1, waiting for transfers between devices: 0.01 us -> 1.76 us  [body(): bottom = lax.ppermute(first_rows, ROW, [(b, a) for a, b in down])]
    ppermute x1, waiting for transfers between devices: 1.26 us -> 0.01 us  [body(): top = lax.ppermute(last_rows, ROW, down)]
    pallas_call x1, Pallas kernels: 8.67 us -> 7.42 us  [body(): pl.pallas_call(outputs_kernel, grid=(8,), out_shape=(shape_of(32, 128, 12...]
where the time goes in v4:
time: 95.5 us; the launch traced here: 95.3 us
  Pallas kernels  44.1 us (46%)
  blocking collectives  33.6 us (35%)
  starting transfers between devices  12.5 us (13%)
  waiting for transfers between devices  4.22 us (4%)
    all_to_all x1, blocking collectives, body(): lax.all_to_all(sent, ROW + COL, 0, 0, tiled=True).reshape(-1, 128)  25 us
    pallas_call x1, Pallas kernels, body(): pl.pallas_call(fields_kernel, out_shape=(kept(128, 48, 128), kept(128, 48...  22.5 us
    pallas_call x1, Pallas kernels, body(): pl.pallas_call(coarse_kernel, out_shape=shape_of(256, 128), compiler_para...  10.1 us
    all_to_all x1, blocking collectives, body(): lax.all_to_all(found.reshape(cols, 32, 128), COL, 0, 0, tiled=True)  8.59 us
    pallas_call x1, Pallas kernels, body(): pl.pallas_call(outputs_kernel, grid=(8,), out_shape=(shape_of(32, 128, 12...  7.42 us
    ppermute x1, starting transfers between devices, body(): top = lax.ppermute(last_rows, ROW, down)  4.36 us
    ppermute x1, starting transfers between devices, body(): beside_right = lax.ppermute(own, COL, [(b, a) for a, b in right])  3.83 us
    ppermute x1, starting transfers between devices, body(): beside_left = lax.ppermute(own, COL, right)  3.02 us
  transfers between devices with their start and end apart: 4, of which 3 were waited for; matrix products, arithmetic and copies ran while one was open for 0% of the time, Pallas kernels for 2%

profile of v4, /device:TPU:1, one launch (start us, length us, event | category | flops | bytes accessed | tf_op | source)
XLA Modules:
  0.0 95.3 jit_solution(5011726274021499951)
XLA Ops:
  0.6 0.0 copy-start
  0.7 0.1 pad_add_fusion.place_ref
  0.7 1.9 %shard_map.95 = (f32[1024,128]{1,0:T(8,128)S(1)}, f32[3,40,128]{2,1,0:T(8,128)S(1)}, f32[3,40,128]{2,1,0:T(8,128)S(1)}) custom-call(s32[2]{0:T(128)S(1)} %pad_add_fusion.place_ref, f32[8]{0:T(128)} %edge_hbm.1, f32[8]{0:T(128)} %pad_hbm.1, f32[32,128,128]{2,1,0:T(8,128)} %load_hbm.1, s32[128,128]{1,0:T(8,128)} %label_hbm.1, f32[128,128]{1,0:T(8,128)} %bump_hbm.1, ...), custom_call_target="tpu_custom_call" | custom-call | tf_op jit(solution)/shard_map/pallas_call | solution.py:641
  2.7 4.4 %collective-permute-start = (f32[3,40,128]{2,1,0:T(8,128)S(1)}, f32[3,40,128]{2,1,0:T(8,128)S(1)}, u32[]{:S(2)}, u32[]{:S(2)}) collective-permute-start(f32[3,40,128]{2,1,0:T(8,128)S(1)} %get-tuple-element.14), channel_id=1, source_target_pairs={{0,8},{8,16},{16,24},{24,32},{32,40},{40,48},{48,56},{56,64},{64,7... | collective-permute-start | bytes 184328 | tf_op jit(solution)/shard_map/ppermute | solution.py:662
  7.0 1.3 %collective-permute-start.1 = (f32[3,40,128]{2,1,0:T(8,128)S(1)}, f32[3,40,128]{2,1,0:T(8,128)S(1)}, u32[]{:S(2)}, u32[]{:S(2)}) collective-permute-start(f32[3,40,128]{2,1,0:T(8,128)S(1)} %get-tuple-element.15), channel_id=1, source_target_pairs={{8,0},{16,8},{24,16},{32,24},{40,32},{48,40},{56,48},{64,56},{72,6... | collective-permute-start | bytes 184328 | tf_op jit(solution)/shard_map/ppermute | solution.py:661
  8.3 0.0 copy-done
  8.4 2.1 %shard_map.96 = (f32[128,32,128]{2,1,0:T(8,128)S(1)}, f32[9,40,128]{2,1,0:T(8,128)S(1)}) custom-call(f32[4096,128]{1,0:T(8,128)S(1)} %bitcast.8, f32[1024,128]{1,0:T(8,128)S(1)} %get-tuple-element.12.grid_ref), custom_call_target="tpu_custom_call" | custom-call | tf_op jit(solution)/shard_map/pallas_call | solution.py:663
  10.4 0.0 collective-permute-done.top_ref
  10.4 1.8 %collective-permute-done.1.bottom_ref = f32[3,40,128]{2,1,0:T(8,128)S(1)} collective-permute-done((f32[3,40,128]{2,1,0:T(8,128)S(1)}, f32[3,40,128]{2,1,0:T(8,128)S(1)}, u32[]{:S(2)}, u32[]{:S(2)}) %collective-permute-start.1) | collective-permute-done | bytes 61472 | tf_op jit(solution)/shard_map/ppermute | solution.py:661
  12.2 0.1 shard_map.97.own_ref
  12.3 3.8 %collective-permute-start.3 = (f32[9,40,128]{2,1,0:T(8,128)S(1)}, f32[9,40,128]{2,1,0:T(8,128)S(1)}, u32[]{:S(2)}, u32[]{:S(2)}) collective-permute-start(f32[9,40,128]{2,1,0:T(8,128)S(1)} %shard_map.97.own_ref), channel_id=1, source_target_pairs={{1,0},{2,1},{3,2},{4,3},{5,4},{6,5},{7,6},{9,8},{10,9},{11,10},{12... | collective-permute-start | bytes 552968 | tf_op jit(solution)/shard_map/ppermute | solution.py:675
  16.1 3.0 %collective-permute-start.2 = (f32[9,40,128]{2,1,0:T(8,128)S(1)}, f32[9,40,128]{2,1,0:T(8,128)S(1)}, u32[]{:S(2)}, u32[]{:S(2)}) collective-permute-start(f32[9,40,128]{2,1,0:T(8,128)S(1)} %shard_map.97.own_ref), channel_id=1, source_target_pairs={{0,1},{1,2},{2,3},{3,4},{4,5},{5,6},{6,7},{8,9},{9,10},{10,11},{11... | collective-permute-start | bytes 552968 | tf_op jit(solution)/shard_map/ppermute | solution.py:674
  19.2 1.3 %collective-permute-done.3.right_ref = f32[9,40,128]{2,1,0:T(8,128)S(1)} collective-permute-done((f32[9,40,128]{2,1,0:T(8,128)S(1)}, f32[9,40,128]{2,1,0:T(8,128)S(1)}, u32[]{:S(2)}, u32[]{:S(2)}) %collective-permute-start.3) | collective-permute-done | bytes 184352 | tf_op jit(solution)/shard_map/ppermute | solution.py:675
  20.4 1.2 %collective-permute-done.2.left_ref = f32[9,40,128]{2,1,0:T(8,128)S(1)} collective-permute-done((f32[9,40,128]{2,1,0:T(8,128)S(1)}, f32[9,40,128]{2,1,0:T(8,128)S(1)}, u32[]{:S(2)}, u32[]{:S(2)}) %collective-permute-start.2) | collective-permute-done | bytes 184352 | tf_op jit(solution)/shard_map/ppermute | solution.py:674
  21.6 22.5 %shard_map.98 = (f32[128,48,128]{2,1,0:T(8,128)S(1)}, f32[128,48,128]{2,1,0:T(8,128)S(1)}, f32[128,16,128]{2,1,0:T(8,128)S(1)}, f32[6,160,128]{2,1,0:T(8,128)S(1)}, f32[64,128]{1,0:T(8,128)S(1)}) custom-call(s32[2]{0:T(128)S(1)} %pad_add_fusion.place_ref, f32[128,32,128]{2,1,0:T(8,128)S(1)} %get-tuple-element.13.rows_ref, ...), custom_call_target="tpu_custom_call" | custom-call | tf_op jit(solution)/shard_map/pallas_call | solution.py:676
  44.2 25.0 %all_to_all.10 = f32[128,8,128]{2,1,0:T(8,128)S(1)} all-to-all(f32[128,8,128]{2,1,0:T(8,128)S(1)} %bitcast.13), channel_id=1, replica_groups=mesh['row_0'=4,'row_1'=4,'col_0'=4,'col_1'=2] {'row_0','row_1','col_0','..., dimensions={0} | all-to-all | bytes 1048576 | tf_op jit(solution)/shard_map/all_to_all | solution.py:706
  69.2 10.1 %shard_map.99 = f32[256,128]{1,0:T(8,128)S(1)} custom-call(s32[2]{0:T(128)S(1)} %pad_add_fusion.place_ref, f32[1024,128]{1,0:T(8,128)S(1)} %bitcast.9), custom_call_target="tpu_custom_call" | custom-call | tf_op jit(solution)/shard_map/pallas_call | solution.py:707
  79.3 8.6 %all_to_all.11 = f32[8,32,128]{2,1,0:T(8,128)S(1)} all-to-all(f32[8,32,128]{2,1,0:T(8,128)S(1)} %bitcast.11), channel_id=1, replica_groups=mesh['row_0'=4,'row_1'=4,'col_0'=4,'col_1'=2] {'col_0','col_1'}, dimensions={0} | all-to-all | bytes 262144 | tf_op jit(solution)/shard_map/all_to_all | solution.py:722
  87.9 7.4 %shard_map.100 = (f32[32,128,128]{2,1,0:T(8,128)}, f32[32,128,128]{2,1,0:T(8,128)}) custom-call(s32[2]{0:T(128)S(1)} %pad_add_fusion.place_ref, f32[128,32,128]{2,1,0:T(8,128)S(1)} %get-tuple-element.13.rows_ref, f32[128,48,128]{2,1,0:T(8,128)S(1)} %get-tuple-element.17.first_ref, f32[128,48,128]{2,1,0:T(8,128)S(1)} %get-tuple-element.18.second_ref, ...), custom_call_target="tpu_custom_call" | custom-call | tf_op jit(solution)/shard_map/pallas_call | solution.py:724
  (1 shorter events, 0.0 us)
Async XLA Ops:
  0.6 7.7 %copy-start = (f32[32,128,128]{2,1,0:T(8,128)S(1)}, f32[32,128,128]{2,1,0:T(8,128)}, u32[]{:S(2)}) copy-start(f32[32,128,128]{2,1,0:T(8,128)} %load_hbm.1) | copy-start | bytes 6291460
  2.7 7.8 %collective-permute-start = (f32[3,40,128]{2,1,0:T(8,128)S(1)}, f32[3,40,128]{2,1,0:T(8,128)S(1)}, u32[]{:S(2)}, u32[]{:S(2)}) collective-permute-start(f32[3,40,128]{2,1,0:T(8,128)S(1)} %get-tuple-element.14), channel_id=1, source_target_pairs={{0,8},{8,16},{16,24},{24,32},{32,40},{40,48},{48,56},{56,64},{64,7... | collective-permute-start | bytes 184328 | tf_op jit(solution)/shard_map/ppermute | solution.py:662
  7.0 5.2 %collective-permute-start.1 = (f32[3,40,128]{2,1,0:T(8,128)S(1)}, f32[3,40,128]{2,1,0:T(8,128)S(1)}, u32[]{:S(2)}, u32[]{:S(2)}) collective-permute-start(f32[3,40,128]{2,1,0:T(8,128)S(1)} %get-tuple-element.15), channel_id=1, source_target_pairs={{8,0},{16,8},{24,16},{32,24},{40,32},{48,40},{56,48},{64,56},{72,6... | collective-permute-start | bytes 184328 | tf_op jit(solution)/shard_map/ppermute | solution.py:661
  12.3 8.1 %collective-permute-start.3 = (f32[9,40,128]{2,1,0:T(8,128)S(1)}, f32[9,40,128]{2,1,0:T(8,128)S(1)}, u32[]{:S(2)}, u32[]{:S(2)}) collective-permute-start(f32[9,40,128]{2,1,0:T(8,128)S(1)} %shard_map.97.own_ref), channel_id=1, source_target_pairs={{1,0},{2,1},{3,2},{4,3},{5,4},{6,5},{7,6},{9,8},{10,9},{11,10},{12... | collective-permute-start | bytes 552968 | tf_op jit(solution)/shard_map/ppermute | solution.py:675
  16.1 5.5 %collective-permute-start.2 = (f32[9,40,128]{2,1,0:T(8,128)S(1)}, f32[9,40,128]{2,1,0:T(8,128)S(1)}, u32[]{:S(2)}, u32[]{:S(2)}) collective-permute-start(f32[9,40,128]{2,1,0:T(8,128)S(1)} %shard_map.97.own_ref), channel_id=1, source_target_pairs={{0,1},{1,2},{2,3},{3,4},{4,5},{5,6},{6,7},{8,9},{9,10},{10,11},{11... | collective-permute-start | bytes 552968 | tf_op jit(solution)/shard_map/ppermute | solution.py:674

commit v5 on v4

--- a/solution.py
+++ b/solution.py
@@ -212,7 +212,7 @@
             coef_ref[n, pl.ds(at, 16)] = value
         return 0
 
-    lax.fori_loop(0, GROUPS, strips, 0)
+    lax.fori_loop(0, GROUPS, strips, 0, unroll=3)
 
     def strip_image(ref_o, ref_s, g, lane, sides):
         o, s = ref_o[g + 1], ref_s[g + 1]
@@ -237,7 +237,7 @@
         q0[2 * g + 1] = roll(y, 64)
         return 0
 
-    lax.fori_loop(0, GROUPS, strip_first, 0)
+    lax.fori_loop(0, GROUPS, strip_first, 0, unroll=3)
 
     def strip_second(g, _):
         (u,) = strip_image(y0_o, y0_s, g, lane48, (1,))
@@ -246,22 +246,7 @@
         q1[2 * g + 1] = roll(y, 64)
         return 0
 
-    lax.fori_loop(0, GROUPS, strip_second, 0)
-
-    def passes(work, low, high):
-        for s in range(8):
-            if s - 8 >= low:
-                work(0, s)
-
-        def step(g, _):
-            for s in range(8):
-                work(g, s)
-            return 0
-
-        lax.fori_loop(1, 17, step, 0)
-        for s in range(8):
-            if 128 + s < high:
-                work(17, s)
+    lax.fori_loop(0, GROUPS, strip_second, 0, unroll=3)
 
     def owned(g):
         return not isinstance(g, int)
@@ -296,8 +281,6 @@
         y0[8 * g + s, 0:32] = inv * b
         y0[8 * g + s, 32:48] = inv * w
 
-    passes(first_image, -2, 130)
-
     def second_image(g, s):
         i = 8 * g + s
         f1 = image(y0[i], y0[i - 1], y0[i + 1], q0, g, s, lane48)
@@ -305,20 +288,44 @@
             first_ref[8 * g - 8 + s] = f1
         y1[i] = coef(5, g, s) * f1
 
-    passes(second_image, -1, 129)
+    def both(g, _):
+        for s in range(8):
+            second_image(g - 2, s)
+        for s in range(8):
+            first_image(g, s)
+        return 0
+
+    def only(work):
+        def step(g, _):
+            for s in range(8):
+                work(g, s)
+            return 0
+
+        return step
+
+    for s in (6, 7):
+        first_image(0, s)
+    lax.fori_loop(1, 3, only(first_image), 0)
+    second_image(0, 7)
+    lax.fori_loop(3, 17, both, 0)
+    for s in (0, 1):
+        first_image(17, s)
+    lax.fori_loop(15, 17, only(second_image), 0)
+    second_image(17, 0)
 
     gram[...] = jnp.zeros((96, 256), F32)
 
-    def third_image(g, sums):
+    def third_image(g, s):
+        i = 8 * g + s
+        second_ref[i - 8] = image(y1[i], y1[i - 1], y1[i + 1], q1, g, s, lane48)
+
+    def products(g, sums):
         left, every = [], []
         sums = list(sums)
         for s in range(8):
             i = 8 * g + s
             r = i - 8
-            y0r, y1r = y0[i], y1[i]
-            f2 = image(y1r, y1[i - 1], y1[i + 1], q1, g, s, lane48)
-            second_ref[r] = f2
-            b, f1 = rows_ref[r], first_ref[r]
+            b, f1, f2, y0r, y1r = rows_ref[r], first_ref[r], second_ref[r], y0[i], y1[i]
             left.append(jnp.concatenate([basis(i + 8), y0r[32:48], y1r[32:48]], axis=0))
             every.append(jnp.concatenate([b, w_ref[r], f1, f2], axis=0))
             pairs = ((y0r, b), (y0r, f1), (y1r, f1), (y1r, f2))
@@ -328,8 +335,16 @@
         gram[:, 0:144] += fast_dot(left, high, NT) + fast_dot(left, low, NT)
         return tuple(sums)
 
+    def last_stage(g, sums):
+        sums = products(g - 1, sums)
+        for s in range(8):
+            third_image(g, s)
+        return sums
+
     zero = jnp.zeros((32, 128), F32)
-    sums = lax.fori_loop(1, 17, third_image, (zero, zero, zero, zero))
+    lax.fori_loop(1, 2, only(third_image), 0)
+    sums = lax.fori_loop(2, 17, last_stage, (zero, zero, zero, zero))
+    sums = lax.fori_loop(16, 17, products, sums)
 
     a0, a1 = gram[0:48, 0:128] + gram[48:96, 0:128], gram[0:48, 128:256] + gram[48:96, 128:256]
     zr, w0, t0, w1, t1 = a0[0:16], a0[16:32], a0[32:48], a1[16:32], a1[32:48]
@@ -363,10 +378,10 @@
         out_ref[8 * d : 8 * d + 8] = jnp.where(row8 < 6, sent, jnp.where(row8 == 6, line, 0.0))
 
 
-def batched_inverse(a, lane, row):
-    base = lane - lane % 16
-    for k in range(0, 16, 2):
-        at_k, at_n = lane % 16 == k, lane % 16 == k + 1
+def batched_inverse(a, lane, row, size):
+    base = lane - lane % size
+    for k in range(0, size, 2):
+        at_k, at_n = lane % size == k, lane % size == k + 1
         left = jnp.take_along_axis(a, base + k, axis=1)
         right = jnp.take_along_axis(a, base + k + 1, axis=1)
         p, q, r, t = left[k : k + 1], right[k : k + 1], left[k + 1 : k + 2], right[k + 1 : k + 2]
@@ -380,17 +395,17 @@
     return a
 
 
-def block_inverse(matrix, low, high):
-    lane = lanes((16, 128))
-    row = lax.broadcasted_iota(jnp.int32, (16, 128), 0)
-    compact = jnp.where(lane % 16 == row, 1.0, 0.0)
-    for n in range(low // 16, high // 16):
-        compact = jnp.where(lane // 16 == n, matrix[16 * n : 16 * n + 16], compact)
-    compact = batched_inverse(compact, lane, row)
+def block_inverse(matrix, low, high, size=16):
+    lane = lanes((size, 128))
+    row = lax.broadcasted_iota(jnp.int32, (size, 128), 0)
+    compact = jnp.where(lane % size == row, 1.0, 0.0)
+    for n in range(low // size, high // size):
+        compact = jnp.where(lane // size == n, matrix[size * n : size * n + size], compact)
+    compact = batched_inverse(compact, lane, row, size)
     parts = []
-    for n in range(8):
-        active = low <= 16 * n < high
-        parts.append(jnp.where(lane // 16 == n, compact, 0.0) if active else jnp.zeros((16, 128), F32))
+    for n in range(128 // size):
+        active = low <= size * n < high
+        parts.append(jnp.where(lane // size == n, compact, 0.0) if active else jnp.zeros((size, 128), F32))
     return jnp.concatenate(parts, axis=0)
 
 
@@ -454,14 +469,14 @@
     across = dot(outer, e[0:128, 128:256])
     schur = e[128:256, 128:256] - dot(e[128:256, 0:128], across)
     steps = []
-    for low, high in ((0, 64), (64, 96), (96, 112)):
+    for low, high in ((0, 64), (64, 96)):
         inv = block_inverse(schur, low, high)
         link = jnp.where((row >= low) & (row < high) & (lane >= high), schur, 0.0)
         x = dot(inv, link)
         keep = jnp.where((row >= high) & (lane >= high), schur, 0.0)
         schur = keep - dot(link, x, TN)
         steps.append((inv, jnp.where((row == lane) & (row >= high), 1.0, 0.0) - x))
-    inner = block_inverse(schur, 112, 128)
+    inner = block_inverse(schur, 96, 128, 32)
     for inv, y in reversed(steps):
         inner = inv + dot(dot(y, inner), y, NT)
     half = dot(across, inner)
@@ -477,13 +492,18 @@
     right_top, right_bottom = ordered(-half, inner)
     top_left, bottom_left = ordered(left_top.T, right_top.T)
     top_right, bottom_right = ordered(left_bottom.T, right_bottom.T)
-    ei[0:128, 0:128] = top_left
-    ei[0:128, 128:256] = top_right
-    ei[128:256, 0:128] = bottom_left
-    ei[128:256, 128:256] = bottom_right
+    inverse = jnp.concatenate(
+        [jnp.concatenate([top_left, bottom_left], axis=0), jnp.concatenate([top_right, bottom_right], axis=0)],
+        axis=1,
+    )
+    for n, part in enumerate(parts_of(inverse, 3)):
+        ei[n] = part
 
     def solve(z):
-        return dot(z, ei[...])
+        rows = [part.astype(F32) for part in parts_of(z, 3)]
+        rows = jnp.concatenate(rows + [jnp.zeros_like(z)], axis=0).astype(jnp.bfloat16)
+        a, b, c = (fast_dot(rows, ei[n]) for n in range(3))
+        return a[0:4] + (a[4:8] + b[0:4]) + (a[8:12] + b[4:8] + c[0:4])
 
     def apply(n, v):
         c = [by_lane[20 + 6 * n + d : 21 + 6 * n + d] for d in range(6)]
@@ -713,7 +733,7 @@
         scratch_shapes=[
             vmem(256, 128),
             vmem(256, 256),
-            vmem(256, 256),
+            pltpu.VMEM((3, 256, 256), jnp.bfloat16),
             vmem(272, 128),
             vmem(272, 128),
             vmem(32, 128),

time: 95.5 us -> 89.7 us (0.939)
  Pallas kernels: 44.1 us -> 38.3 us
    pallas_call x1, Pallas kernels: 22.5 us -> 18 us  [body(): pl.pallas_call(fields_kernel, out_shape=(kept(128, 48, 128), kept(128, 48...]
    pallas_call x1, Pallas kernels: 10.1 us -> 8.77 us  [body(): pl.pallas_call(coarse_kernel, out_shape=shape_of(256, 128), compiler_para...]
where the time goes in v5:
time: 89.7 us; the launch traced here: 89.4 us
  Pallas kernels  38.3 us (43%)
  blocking collectives  33.6 us (37%)
  starting transfers between devices  12.5 us (14%)
  waiting for transfers between devices  4.22 us (5%)
    all_to_all x1, blocking collectives, body(): lax.all_to_all(sent, ROW + COL, 0, 0, tiled=True).reshape(-1, 128)  25 us
    pallas_call x1, Pallas kernels, body(): pl.pallas_call(fields_kernel, out_shape=(kept(128, 48, 128), kept(128, 48...  18 us
    pallas_call x1, Pallas kernels, body(): pl.pallas_call(coarse_kernel, out_shape=shape_of(256, 128), compiler_para...  8.77 us
    all_to_all x1, blocking collectives, body(): lax.all_to_all(found.reshape(cols, 32, 128), COL, 0, 0, tiled=True)  8.59 us
    pallas_call x1, Pallas kernels, body(): pl.pallas_call(outputs_kernel, grid=(8,), out_shape=(shape_of(32, 128, 12...  7.41 us
    ppermute x1, starting transfers between devices, body(): top = lax.ppermute(last_rows, ROW, down)  4.36 us
    ppermute x1, starting transfers between devices, body(): beside_right = lax.ppermute(own, COL, [(b, a) for a, b in right])  3.83 us
    ppermute x1, starting transfers between devices, body(): beside_left = lax.ppermute(own, COL, right)  3.02 us
  transfers between devices with their start and end apart: 4, of which 3 were waited for; matrix products, arithmetic and copies ran while one was open for 0% of the time, Pallas kernels for 2%

profile of v5, /device:TPU:1, one launch (start us, length us, event | category | flops | bytes accessed | tf_op | source)
XLA Modules:
  0.0 89.4 jit_solution(14668540897273410676)
XLA Ops:
  0.6 0.0 copy-start
  0.7 0.1 pad_add_fusion.place_ref
  0.7 1.9 %shard_map.95 = (f32[1024,128]{1,0:T(8,128)S(1)}, f32[3,40,128]{2,1,0:T(8,128)S(1)}, f32[3,40,128]{2,1,0:T(8,128)S(1)}) custom-call(s32[2]{0:T(128)S(1)} %pad_add_fusion.place_ref, f32[8]{0:T(128)} %edge_hbm.1, f32[8]{0:T(128)} %pad_hbm.1, f32[32,128,128]{2,1,0:T(8,128)} %load_hbm.1, s32[128,128]{1,0:T(8,128)} %label_hbm.1, f32[128,128]{1,0:T(8,128)} %bump_hbm.1, ...), custom_call_target="tpu_custom_call" | custom-call | tf_op jit(solution)/shard_map/pallas_call | solution.py:661
  2.7 4.4 %collective-permute-start = (f32[3,40,128]{2,1,0:T(8,128)S(1)}, f32[3,40,128]{2,1,0:T(8,128)S(1)}, u32[]{:S(2)}, u32[]{:S(2)}) collective-permute-start(f32[3,40,128]{2,1,0:T(8,128)S(1)} %get-tuple-element.14), channel_id=1, source_target_pairs={{0,8},{8,16},{16,24},{24,32},{32,40},{40,48},{48,56},{56,64},{64,7... | collective-permute-start | bytes 184328 | tf_op jit(solution)/shard_map/ppermute | solution.py:682
  7.0 1.3 %collective-permute-start.1 = (f32[3,40,128]{2,1,0:T(8,128)S(1)}, f32[3,40,128]{2,1,0:T(8,128)S(1)}, u32[]{:S(2)}, u32[]{:S(2)}) collective-permute-start(f32[3,40,128]{2,1,0:T(8,128)S(1)} %get-tuple-element.15), channel_id=1, source_target_pairs={{8,0},{16,8},{24,16},{32,24},{40,32},{48,40},{56,48},{64,56},{72,6... | collective-permute-start | bytes 184328 | tf_op jit(solution)/shard_map/ppermute | solution.py:681
  8.3 0.0 copy-done
  8.4 2.1 %shard_map.96 = (f32[128,32,128]{2,1,0:T(8,128)S(1)}, f32[9,40,128]{2,1,0:T(8,128)S(1)}) custom-call(f32[4096,128]{1,0:T(8,128)S(1)} %bitcast.8, f32[1024,128]{1,0:T(8,128)S(1)} %get-tuple-element.12.grid_ref), custom_call_target="tpu_custom_call" | custom-call | tf_op jit(solution)/shard_map/pallas_call | solution.py:683
  10.4 0.0 collective-permute-done.top_ref
  10.4 1.8 %collective-permute-done.1.bottom_ref = f32[3,40,128]{2,1,0:T(8,128)S(1)} collective-permute-done((f32[3,40,128]{2,1,0:T(8,128)S(1)}, f32[3,40,128]{2,1,0:T(8,128)S(1)}, u32[]{:S(2)}, u32[]{:S(2)}) %collective-permute-start.1) | collective-permute-done | bytes 61472 | tf_op jit(solution)/shard_map/ppermute | solution.py:681
  12.2 0.1 shard_map.97.own_ref
  12.3 3.8 %collective-permute-start.3 = (f32[9,40,128]{2,1,0:T(8,128)S(1)}, f32[9,40,128]{2,1,0:T(8,128)S(1)}, u32[]{:S(2)}, u32[]{:S(2)}) collective-permute-start(f32[9,40,128]{2,1,0:T(8,128)S(1)} %shard_map.97.own_ref), channel_id=1, source_target_pairs={{1,0},{2,1},{3,2},{4,3},{5,4},{6,5},{7,6},{9,8},{10,9},{11,10},{12... | collective-permute-start | bytes 552968 | tf_op jit(solution)/shard_map/ppermute | solution.py:695
  16.1 3.0 %collective-permute-start.2 = (f32[9,40,128]{2,1,0:T(8,128)S(1)}, f32[9,40,128]{2,1,0:T(8,128)S(1)}, u32[]{:S(2)}, u32[]{:S(2)}) collective-permute-start(f32[9,40,128]{2,1,0:T(8,128)S(1)} %shard_map.97.own_ref), channel_id=1, source_target_pairs={{0,1},{1,2},{2,3},{3,4},{4,5},{5,6},{6,7},{8,9},{9,10},{10,11},{11... | collective-permute-start | bytes 552968 | tf_op jit(solution)/shard_map/ppermute | solution.py:694
  19.2 1.3 %collective-permute-done.3.right_ref = f32[9,40,128]{2,1,0:T(8,128)S(1)} collective-permute-done((f32[9,40,128]{2,1,0:T(8,128)S(1)}, f32[9,40,128]{2,1,0:T(8,128)S(1)}, u32[]{:S(2)}, u32[]{:S(2)}) %collective-permute-start.3) | collective-permute-done | bytes 184352 | tf_op jit(solution)/shard_map/ppermute | solution.py:695
  20.4 1.2 %collective-permute-done.2.left_ref = f32[9,40,128]{2,1,0:T(8,128)S(1)} collective-permute-done((f32[9,40,128]{2,1,0:T(8,128)S(1)}, f32[9,40,128]{2,1,0:T(8,128)S(1)}, u32[]{:S(2)}, u32[]{:S(2)}) %collective-permute-start.2) | collective-permute-done | bytes 184352 | tf_op jit(solution)/shard_map/ppermute | solution.py:694
  21.6 18.0 %shard_map.98 = (f32[128,48,128]{2,1,0:T(8,128)S(1)}, f32[128,48,128]{2,1,0:T(8,128)S(1)}, f32[128,16,128]{2,1,0:T(8,128)S(1)}, f32[6,160,128]{2,1,0:T(8,128)S(1)}, f32[64,128]{1,0:T(8,128)S(1)}) custom-call(s32[2]{0:T(128)S(1)} %pad_add_fusion.place_ref, f32[128,32,128]{2,1,0:T(8,128)S(1)} %get-tuple-element.13.rows_ref, ...), custom_call_target="tpu_custom_call" | custom-call | tf_op jit(solution)/shard_map/pallas_call | solution.py:696
  39.6 25.0 %all_to_all.10 = f32[128,8,128]{2,1,0:T(8,128)S(1)} all-to-all(f32[128,8,128]{2,1,0:T(8,128)S(1)} %bitcast.13), channel_id=1, replica_groups=mesh['row_0'=4,'row_1'=4,'col_0'=4,'col_1'=2] {'row_0','row_1','col_0','..., dimensions={0} | all-to-all | bytes 1048576 | tf_op jit(solution)/shard_map/all_to_all | solution.py:726
  64.6 8.8 %shard_map.99 = f32[256,128]{1,0:T(8,128)S(1)} custom-call(s32[2]{0:T(128)S(1)} %pad_add_fusion.place_ref, f32[1024,128]{1,0:T(8,128)S(1)} %bitcast.9), custom_call_target="tpu_custom_call" | custom-call | tf_op jit(solution)/shard_map/pallas_call | solution.py:727
  73.4 8.6 %all_to_all.11 = f32[8,32,128]{2,1,0:T(8,128)S(1)} all-to-all(f32[8,32,128]{2,1,0:T(8,128)S(1)} %bitcast.11), channel_id=1, replica_groups=mesh['row_0'=4,'row_1'=4,'col_0'=4,'col_1'=2] {'col_0','col_1'}, dimensions={0} | all-to-all | bytes 262144 | tf_op jit(solution)/shard_map/all_to_all | solution.py:742
  82.0 7.4 %shard_map.100 = (f32[32,128,128]{2,1,0:T(8,128)}, f32[32,128,128]{2,1,0:T(8,128)}) custom-call(s32[2]{0:T(128)S(1)} %pad_add_fusion.place_ref, f32[128,32,128]{2,1,0:T(8,128)S(1)} %get-tuple-element.13.rows_ref, f32[128,48,128]{2,1,0:T(8,128)S(1)} %get-tuple-element.17.first_ref, f32[128,48,128]{2,1,0:T(8,128)S(1)} %get-tuple-element.18.second_ref, ...), custom_call_target="tpu_custom_call" | custom-call | tf_op jit(solution)/shard_map/pallas_call | solution.py:744
  (1 shorter events, 0.0 us)
Async XLA Ops:
  0.6 7.7 %copy-start = (f32[32,128,128]{2,1,0:T(8,128)S(1)}, f32[32,128,128]{2,1,0:T(8,128)}, u32[]{:S(2)}) copy-start(f32[32,128,128]{2,1,0:T(8,128)} %load_hbm.1) | copy-start | bytes 6291460
  2.7 7.8 %collective-permute-start = (f32[3,40,128]{2,1,0:T(8,128)S(1)}, f32[3,40,128]{2,1,0:T(8,128)S(1)}, u32[]{:S(2)}, u32[]{:S(2)}) collective-permute-start(f32[3,40,128]{2,1,0:T(8,128)S(1)} %get-tuple-element.14), channel_id=1, source_target_pairs={{0,8},{8,16},{16,24},{24,32},{32,40},{40,48},{48,56},{56,64},{64,7... | collective-permute-start | bytes 184328 | tf_op jit(solution)/shard_map/ppermute | solution.py:682
  7.0 5.2 %collective-permute-start.1 = (f32[3,40,128]{2,1,0:T(8,128)S(1)}, f32[3,40,128]{2,1,0:T(8,128)S(1)}, u32[]{:S(2)}, u32[]{:S(2)}) collective-permute-start(f32[3,40,128]{2,1,0:T(8,128)S(1)} %get-tuple-element.15), channel_id=1, source_target_pairs={{8,0},{16,8},{24,16},{32,24},{40,32},{48,40},{56,48},{64,56},{72,6... | collective-permute-start | bytes 184328 | tf_op jit(solution)/shard_map/ppermute | solution.py:681
  12.3 8.1 %collective-permute-start.3 = (f32[9,40,128]{2,1,0:T(8,128)S(1)}, f32[9,40,128]{2,1,0:T(8,128)S(1)}, u32[]{:S(2)}, u32[]{:S(2)}) collective-permute-start(f32[9,40,128]{2,1,0:T(8,128)S(1)} %shard_map.97.own_ref), channel_id=1, source_target_pairs={{1,0},{2,1},{3,2},{4,3},{5,4},{6,5},{7,6},{9,8},{10,9},{11,10},{12... | collective-permute-start | bytes 552968 | tf_op jit(solution)/shard_map/ppermute | solution.py:695
  16.1 5.5 %collective-permute-start.2 = (f32[9,40,128]{2,1,0:T(8,128)S(1)}, f32[9,40,128]{2,1,0:T(8,128)S(1)}, u32[]{:S(2)}, u32[]{:S(2)}) collective-permute-start(f32[9,40,128]{2,1,0:T(8,128)S(1)} %shard_map.97.own_ref), channel_id=1, source_target_pairs={{0,1},{1,2},{2,3},{3,4},{4,5},{5,6},{6,7},{8,9},{9,10},{10,11},{11... | collective-permute-start | bytes 552968 | tf_op jit(solution)/shard_map/ppermute | solution.py:694

commit v6 on v5

--- a/solution.py
+++ b/solution.py
@@ -54,7 +54,7 @@
 
 def prepare_kernel(
     place_ref, edge_hbm, pad_hbm, load_hbm, label_hbm, bump_hbm, across_hbm, down_hbm, pad_class_hbm,
-    grid_ref, first_ref, last_ref, edge_ref, pad_ref, load_ref, load_end_ref, label_ref, across_ref, down_ref, pad_class_ref, done,
+    grid_ref, far_ref, near_ref, edge_ref, pad_ref, load_ref, load_end_ref, label_ref, across_ref, down_ref, pad_class_ref, done,
 ):
     copies = [
         pltpu.make_async_copy(source, target, done.at[n])
@@ -94,10 +94,14 @@
     grid_ref[512:640] = lookup(pad_ref, pad_class_ref[...])
     grid_ref[640:1024] = jnp.zeros((384, 128), F32)
     for n in range(HALO):
-        first_ref[n, 0:32] = load_ref[:, n]
-        first_ref[n, 32:40] = grid_ref[pl.ds(n, 8, stride=128), :]
-        last_ref[n, 0:32] = load_end_ref[:, 8 - HALO + n]
-        last_ref[n, 32:40] = grid_ref[pl.ds(128 - HALO + n, 8, stride=128), :]
+        even = pr % 2 == 0
+        first, last = load_ref[:, n], load_end_ref[:, 8 - HALO + n]
+        far_ref[n, 0:32] = jnp.where(even, first, last)
+        near_ref[n, 0:32] = jnp.where(even, last, first)
+        first = grid_ref[pl.ds(n, 8, stride=128), :]
+        last = grid_ref[pl.ds(128 - HALO + n, 8, stride=128), :]
+        far_ref[n, 32:40] = jnp.where(even, first, last)
+        near_ref[n, 32:40] = jnp.where(even, last, first)
 
 
 def pack_kernel(load_ref, grid_ref, rows_ref, own_ref):
@@ -124,8 +128,11 @@
     lax.fori_loop(1, 8, step, 0)
 
 
-def corner_kernel(own_ref, top_ref, bottom_ref, out_ref):
+def corner_kernel(place_ref, own_ref, far_ref, near_ref, out_ref, top_ref, bottom_ref):
     lane = lanes((SUB, 128)) // 8
+    even = place_ref[0] % 2 == 0
+    top_ref[...] = jnp.where(even, far_ref[...], near_ref[...])
+    bottom_ref[...] = jnp.where(even, near_ref[...], far_ref[...])
     for g in range(GROUPS):
         out_ref[g] = own_ref[g]
     start, end = own_ref[0], own_ref[8]
@@ -139,7 +146,7 @@
 
 
 def fields_kernel(
-    place_ref, rows_ref, grid_ref, top_ref, bottom_ref, own_ref, left_ref, right_ref,
+    place_ref, rows_ref, grid_ref, top_ref, bottom_ref, own_ref, far_ref, near_ref,
     first_ref, second_ref, w_ref, coef_ref, out_ref,
     ext, so, ss, sz_o, sz_s, y0_o, y0_s, qz, q0, q1, sc, y0, y1, gram,
 ):
@@ -182,7 +189,8 @@
 
     def strips(g, _):
         o_row = own_ref[g]
-        s_row = jnp.where(lanes((SUB, 128)) % 8 < 3, left_ref[g], right_ref[g])
+        on_left = (lanes((SUB, 128)) % 8 < 3) == (pc % 2 == 0)
+        s_row = jnp.where(on_left, far_ref[g], near_ref[g])
         so[g + 1], ss[g + 1] = o_row, s_row
         lefts = pair_left(o_row[RIGHT : RIGHT + 1], s_row[RIGHT : RIGHT + 1], lane1)
         for side, (row, ref, ll) in enumerate(((o_row, so, lefts[0]), (s_row, ss, lefts[1]))):
@@ -357,25 +365,30 @@
         moved = jnp.where(slot == k, roll(matrices, (128 - k) % 128), moved)
     common = jnp.zeros((16, 128), F32)
     for n in range(5):
-        start = 20 + 6 * n
-        common = jnp.where((lane16 >= start) & (lane16 < start + 6), roll(moved, (start - 24 * n) % 128), common)
+        for start, offset, count in ((20 + 2 * n, 0, 2), (30 + 3 * n, 3, 3)):
+            hit = (lane16 >= start) & (lane16 < start + count)
+            common = jnp.where(hit, roll(moved, (start - offset - 24 * n) % 128), common)
     lines = []
     diagonal = lanes((32, 128)) == lax.broadcasted_iota(jnp.int32, (32, 128), 0)
     for total in sums:
         column = jnp.sum(total, axis=1, keepdims=True)
         lines.append(jnp.sum(jnp.where(diagonal, column, 0.0), axis=0, keepdims=True))
-    lane8, row8 = lanes((8, 128)), lax.broadcasted_iota(jnp.int32, (8, 128), 0)
+    row4, lane4 = lax.broadcasted_iota(jnp.int32, (4, 128), 0), lanes((4, 128))
     for d in range(8):
         message = common
         for n, (x, z) in enumerate(((w0, 0), (w0, 48), (w0, 96), (zr, 0), (t0, 96))):
             hit = (lane16 >= 4 * n) & (lane16 < 4 * n + 4)
             message = jnp.where(hit, roll(x, (4 * n - z - 4 * d) % 128), message)
-        upper = roll(roll(message, 10, 0), 64)
-        sent = jnp.where(lane8 < 64, message[0:8], upper[0:8])
+        middle, last = roll(message, 45), roll(message, 90)
+        sent = jnp.where(lane4 < 45, message[0:4], jnp.where(lane4 < 90, middle[4:8], last[8:12]))
         line = jnp.zeros((1, 128), F32)
         for n in range(4):
-            line = jnp.where((lane1 >= 4 * n) & (lane1 < 4 * n + 4), roll(lines[n], (4 * n - 4 * d) % 128), line)
-        out_ref[8 * d : 8 * d + 8] = jnp.where(row8 < 6, sent, jnp.where(row8 == 6, line, 0.0))
+            start = 120 + 4 * n if n < 2 else 112 + 4 * n
+            line = jnp.where((lane1 >= start) & (lane1 < start + 4), roll(lines[n], (start - 4 * d) % 128), line)
+            if n == 1:
+                first_two, line = line, jnp.zeros((1, 128), F32)
+        total = jnp.where(row4 == 0, first_two, jnp.where(row4 == 1, line, 0.0))
+        out_ref[4 * d : 4 * d + 4] = jnp.where(lane4 < 120, sent, total)
 
 
 def batched_inverse(a, lane, row, size):
@@ -413,35 +426,34 @@
     pr, pc = place_ref[0], place_ref[1]
     sub8 = lax.broadcasted_iota(jnp.int32, (8, 128), 0)
 
+    lane8 = lanes((8, 128))
     for p in range(16):
-        sums = {}
+        even, odd = jnp.zeros((8, 128), F32), jnp.zeros((8, 128), F32)
         for dr in range(3):
             r = p + 1 - dr
             if not 0 <= r < 16:
                 continue
-            for dq in range(4):
-                k = 4 * dr + dq
-                piece = in_ref[pl.ds(64 * r + k % 6, 8, stride=8), :]
-                if dq == 0:
-                    piece = jnp.where(sub8 < 7, roll(piece, 7, 0), 0.0)
-                elif dq == 3:
-                    piece = jnp.where(sub8 >= 1, roll(piece, 1, 0), 0.0)
-                key = ((dq + 1) % 2, k >= 6)
-                sums[key] = sums[key] + piece if key in sums else piece
-        for par in range(2):
-            total = jnp.zeros((8, 128), F32)
-            if (par, False) in sums:
-                total = total + sums[par, False]
-            if (par, True) in sums:
-                total = total + roll(sums[par, True], 64)
-            g[pl.ds(16 * p + par, 8, stride=2), :] = total
-    tally = jnp.sum(in_ref[pl.ds(6, 128, stride=8), :], axis=0, keepdims=True)
+            at = [in_ref[pl.ds(32 * r + dq, 8, stride=4), :] for dq in range(4)]
+            pair = (
+                at[1] + jnp.where(sub8 >= 1, roll(at[3], 1, 0), 0.0),
+                at[2] + jnp.where(sub8 < 7, roll(at[0], 7, 0), 0.0),
+            )
+            hit = lane8 < (30 if dr == 2 else 45)
+            even, odd = (
+                old + jnp.where(hit, roll(new, (128 - 45 * dr) % 128) if dr else new, 0.0)
+                for old, new in zip((even, odd), pair)
+            )
+        g[pl.ds(16 * p, 8, stride=2), :] = even
+        g[pl.ds(16 * p + 1, 8, stride=2), :] = odd
+    tally = [
+        roll(jnp.sum(in_ref[pl.ds(n, 128, stride=4), :], axis=0, keepdims=True), 8 + 8 * n) for n in range(2)
+    ]
+    tally = jnp.where(lanes((1, 128)) < 8, tally[0], tally[1])
     tally = jnp.broadcast_to(tally, (128, 128)).T
     bb, bu, uu, uuu = (tally[4 * n : 4 * n + 4, 0:1] for n in range(4))
     by_lane = jnp.concatenate([g[0:128].T, g[128:256].T], axis=1)
 
     lane16, row16 = lanes((16, 128)), lax.broadcasted_iota(jnp.int32, (16, 128), 0)
-    base = 20 + 6 * 3
     for p in range(16):
         own = g[16 * p : 16 * p + 16]
         terms = [(own, d, dp, dq) for d, dp, dq in ((0, 0, 0), (1, 0, 1))]
@@ -457,7 +469,8 @@
             h, off = target // 128, target % 128
             q = row16 + dq
             hit = (lane16 == off + q) & (q >= 0) & (q < 16)
-            value = jnp.broadcast_to(x[:, base + d : base + d + 1], (16, 128))
+            at = 26 + d if d < 2 else 36 + d
+            value = jnp.broadcast_to(x[:, at : at + 1], (16, 128))
             halves[h] = jnp.where(hit, value, halves[h])
         at = POS[p] * 16
         e[at : at + 16, 0:128] = halves[0]
@@ -506,7 +519,7 @@
         return a[0:4] + (a[4:8] + b[0:4]) + (a[8:12] + b[4:8] + c[0:4])
 
     def apply(n, v):
-        c = [by_lane[20 + 6 * n + d : 21 + 6 * n + d] for d in range(6)]
+        c = {d: by_lane[at : at + 1] for d, at in enumerate((20 + 2 * n, 21 + 2 * n, 0, 30 + 3 * n, 31 + 3 * n, 32 + 3 * n))}
         total = c[0] * v
         for d, step in ((1, 1), (3, 15), (4, 16), (5, 17)):
             total = total + c[d] * roll(v, 256 - step) + roll(c[d] * v, step)
@@ -641,6 +654,11 @@
             sol_ref[:, 8 * part + n] = inv * (e[32:64] - p1 * b - p2 * u) + e[64:96]
 
 
+def swapped(value, axis, start):
+    pairs = [(i, i + 1) for i in range(start, lax.axis_size(axis) - 1, 2)]
+    return lax.ppermute(value, axis, pairs + [(b, a) for a, b in pairs])
+
+
 def shape_of(*dims):
     return jax.ShapeDtypeStruct(dims, F32)
 
@@ -658,7 +676,7 @@
     rows, cols = lax.axis_size(ROW), lax.axis_size(COL)
     place = jnp.stack([pr, pc]).astype(jnp.int32)
     loads = load_currents.reshape(-1, 128)
-    grid, first_rows, last_rows = pl.pallas_call(
+    grid, far_rows, near_rows = pl.pallas_call(
         prepare_kernel,
         out_shape=(kept(1024, 128), shape_of(HALO, SUB, 128), shape_of(HALO, SUB, 128)),
         compiler_params=limited,
@@ -677,9 +695,8 @@
             )
         ),
     )
-    down = [(i, i + 1) for i in range(rows - 1)]
-    bottom = lax.ppermute(first_rows, ROW, [(b, a) for a, b in down])
-    top = lax.ppermute(last_rows, ROW, down)
+    far_rows = swapped(far_rows, ROW, 1)
+    near_rows = swapped(near_rows, ROW, 0)
     by_rows, own = pl.pallas_call(
         pack_kernel,
         out_shape=(kept(128, 32, 128), kept(GROUPS, SUB, 128)),
@@ -687,12 +704,15 @@
         in_specs=[whole] * 2,
         out_specs=(whole,) * 2,
     )(loads, grid)
-    own = pl.pallas_call(
-        corner_kernel, out_shape=shape_of(GROUPS, SUB, 128), in_specs=[whole] * 3, out_specs=whole, compiler_params=limited
-    )(own, top, bottom)
-    right = [(i, i + 1) for i in range(cols - 1)]
-    beside_left = lax.ppermute(own, COL, right)
-    beside_right = lax.ppermute(own, COL, [(b, a) for a, b in right])
+    own, top, bottom = pl.pallas_call(
+        corner_kernel,
+        out_shape=(shape_of(GROUPS, SUB, 128), kept(HALO, SUB, 128), kept(HALO, SUB, 128)),
+        compiler_params=limited,
+        in_specs=[scalars] + [whole] * 3,
+        out_specs=(whole,) * 3,
+    )(place, own, far_rows, near_rows)
+    near_columns = swapped(own, COL, 0)
+    far_columns = swapped(own, COL, 1)
     first, second, w, coef, payload = pl.pallas_call(
         fields_kernel,
         out_shape=(
@@ -700,7 +720,7 @@
             kept(128, 48, 128),
             kept(128, 16, 128),
             kept(6, 160, 128),
-            shape_of(64, 128),
+            shape_of(32, 128),
         ),
         compiler_params=limited,
         in_specs=[scalars] + [whole] * 7,
@@ -721,8 +741,8 @@
             vmem(144, 48, 128),
             vmem(96, 256),
         ],
-    )(place, by_rows, grid, top, bottom, own, beside_left, beside_right)
-    sent = jnp.broadcast_to(payload.reshape(1, cols, 8, 128), (rows, cols, 8, 128)).reshape(-1, 8, 128)
+    )(place, by_rows, grid, top, bottom, own, far_columns, near_columns)
+    sent = jnp.broadcast_to(payload.reshape(1, cols, 4, 128), (rows, cols, 4, 128)).reshape(-1, 4, 128)
     everything = lax.all_to_all(sent, ROW + COL, 0, 0, tiled=True).reshape(-1, 128)
     found = pl.pallas_call(
         coarse_kernel,

time: 89.7 us -> 83.7 us (0.933)
  blocking collectives: 33.6 us -> 29.5 us
  starting transfers between devices: 12.5 us -> 10.5 us
    all_to_all x1, blocking collectives: 25 us -> 21 us  [body(): lax.all_to_all(sent, ROW + COL, 0, 0, tiled=True).reshape(-1, 128)]
    ppermute x4, starting transfers between devices: 12.5 us -> 10.5 us  [swapped(): return lax.ppermute(value, axis, pairs + [(b, a) for a, b in pairs])]
  transfers between devices with their start and end apart: 4 -> 4, of which waited for: 3 -> 1; matrix products, arithmetic and copies ran while one was open for 0% -> 0% of each run, Pallas kernels for 2% -> 2%
where the time goes in v6:
time: 83.7 us; the launch traced here: 83.4 us
  Pallas kernels  38.8 us (46%)
  blocking collectives  29.5 us (35%)
  starting transfers between devices  10.5 us (13%)
  waiting for transfers between devices  3.82 us (5%)
    all_to_all x1, blocking collectives, body(): lax.all_to_all(sent, ROW + COL, 0, 0, tiled=True).reshape(-1, 128)  21 us
    pallas_call x1, Pallas kernels, body(): pl.pallas_call(fields_kernel, out_shape=(kept(128, 48, 128), kept(128, 48...  18 us
    ppermute x4, starting transfers between devices, swapped(): return lax.ppermute(value, axis, pairs + [(b, a) for a, b in pairs])  10.5 us
    pallas_call x1, Pallas kernels, body(): pl.pallas_call(coarse_kernel, out_shape=shape_of(256, 128), compiler_para...  8.7 us
    all_to_all x1, blocking collectives, body(): lax.all_to_all(found.reshape(cols, 32, 128), COL, 0, 0, tiled=True)  8.51 us
    pallas_call x1, Pallas kernels, body(): pl.pallas_call(outputs_kernel, grid=(8,), out_shape=(shape_of(32, 128, 12...  7.38 us
    ppermute x4, waiting for transfers between devices, swapped(): return lax.ppermute(value, axis, pairs + [(b, a) for a, b in pairs])  3.82 us
    pallas_call x1, Pallas kernels, body(): pl.pallas_call(pack_kernel, out_shape=(kept(128, 32, 128), kept(GROUPS, S...  2.08 us
  transfers between devices with their start and end apart: 4, of which 1 were waited for; matrix products, arithmetic and copies ran while one was open for 0% of the time, Pallas kernels for 2%

profile of v6, /device:TPU:1, one launch (start us, length us, event | category | flops | bytes accessed | tf_op | source)
XLA Modules:
  0.0 83.4 jit_solution(5625611557118011525)
XLA Ops:
  0.6 0.0 copy-start
  0.7 0.1 pad_add_fusion.place_ref
  0.7 2.0 %shard_map.95 = (f32[1024,128]{1,0:T(8,128)S(1)}, f32[3,40,128]{2,1,0:T(8,128)S(1)}, f32[3,40,128]{2,1,0:T(8,128)S(1)}) custom-call(s32[2]{0:T(128)S(1)} %pad_add_fusion.place_ref, f32[8]{0:T(128)} %edge_hbm.1, f32[8]{0:T(128)} %pad_hbm.1, f32[32,128,128]{2,1,0:T(8,128)} %load_hbm.1, s32[128,128]{1,0:T(8,128)} %label_hbm.1, f32[128,128]{1,0:T(8,128)} %bump_hbm.1, ...), custom_call_target="tpu_custom_call" | custom-call | tf_op jit(solution)/shard_map/pallas_call | solution.py:679
  2.7 0.7 collective-permute-start
  3.4 5.4 %collective-permute-start.1 = (f32[3,40,128]{2,1,0:T(8,128)S(1)}, f32[3,40,128]{2,1,0:T(8,128)S(1)}, u32[]{:S(2)}, u32[]{:S(2)}) collective-permute-start(f32[3,40,128]{2,1,0:T(8,128)S(1)} %get-tuple-element.19), channel_id=1, source_target_pairs={{0,8},{16,24},{32,40},{48,56},{64,72},{80,88},{96,104},{112,120},{... | collective-permute-start | bytes 184328 | tf_op jit(solution)/shard_map/ppermute | solution.py:659
  8.8 0.0 copy-done
  8.8 2.1 %shard_map.96 = (f32[128,32,128]{2,1,0:T(8,128)S(1)}, f32[9,40,128]{2,1,0:T(8,128)S(1)}) custom-call(f32[4096,128]{1,0:T(8,128)S(1)} %bitcast.8, f32[1024,128]{1,0:T(8,128)S(1)} %get-tuple-element.15.grid_ref), custom_call_target="tpu_custom_call" | custom-call | tf_op jit(solution)/shard_map/pallas_call | solution.py:700
  10.9 0.0 collective-permute-done.far_ref
  10.9 0.0 collective-permute-done.1.near_ref
  10.9 0.6 shard_map.97
  11.6 1.4 %collective-permute-start.3 = (f32[9,40,128]{2,1,0:T(8,128)S(1)}, f32[9,40,128]{2,1,0:T(8,128)S(1)}, u32[]{:S(2)}, u32[]{:S(2)}) collective-permute-start(f32[9,40,128]{2,1,0:T(8,128)S(1)} %get-tuple-element.22.own_ref), channel_id=1, source_target_pairs={{0,1},{2,3},{4,5},{6,7},{1,0},{3,2},{5,4},{7,6},{8,9},{10,11},{12,... | collective-permute-start | bytes 552968 | tf_op jit(solution)/shard_map/ppermute | solution.py:659
  13.0 3.0 %collective-permute-start.2 = (f32[9,40,128]{2,1,0:T(8,128)S(1)}, f32[9,40,128]{2,1,0:T(8,128)S(1)}, u32[]{:S(2)}, u32[]{:S(2)}) collective-permute-start(f32[9,40,128]{2,1,0:T(8,128)S(1)} %get-tuple-element.22.own_ref), channel_id=1, source_target_pairs={{1,2},{3,4},{5,6},{2,1},{4,3},{6,5},{9,10},{11,12},{13,14},{10,9},... | collective-permute-start | bytes 552968 | tf_op jit(solution)/shard_map/ppermute | solution.py:659
  16.0 0.0 collective-permute-done.3.near_ref
  16.0 3.8 %collective-permute-done.2.far_ref = f32[9,40,128]{2,1,0:T(8,128)S(1)} collective-permute-done((f32[9,40,128]{2,1,0:T(8,128)S(1)}, f32[9,40,128]{2,1,0:T(8,128)S(1)}, u32[]{:S(2)}, u32[]{:S(2)}) %collective-permute-start.2) | collective-permute-done | bytes 184352 | tf_op jit(solution)/shard_map/ppermute | solution.py:659
  19.8 18.0 %shard_map.98 = (f32[128,48,128]{2,1,0:T(8,128)S(1)}, f32[128,48,128]{2,1,0:T(8,128)S(1)}, f32[128,16,128]{2,1,0:T(8,128)S(1)}, f32[6,160,128]{2,1,0:T(8,128)S(1)}, f32[32,128]{1,0:T(8,128)S(1)}) custom-call(s32[2]{0:T(128)S(1)} %pad_add_fusion.place_ref, f32[128,32,128]{2,1,0:T(8,128)S(1)} %get-tuple-element.16.rows_ref, ...), custom_call_target="tpu_custom_call" | custom-call | tf_op jit(solution)/shard_map/pallas_call | solution.py:716
  37.9 21.0 %all_to_all.10 = f32[128,4,128]{2,1,0:T(4,128)S(1)} all-to-all(f32[128,4,128]{2,1,0:T(4,128)S(1)} %bitcast.13), channel_id=1, replica_groups=mesh['row_0'=4,'row_1'=4,'col_0'=4,'col_1'=2] {'row_0','row_1','col_0','..., dimensions={0} | all-to-all | bytes 524288 | tf_op jit(solution)/shard_map/all_to_all | solution.py:746
  58.8 8.7 %shard_map.99 = f32[256,128]{1,0:T(8,128)S(1)} custom-call(s32[2]{0:T(128)S(1)} %pad_add_fusion.place_ref, f32[512,128]{1,0:T(8,128)S(1)} %bitcast.9), custom_call_target="tpu_custom_call" | custom-call | tf_op jit(solution)/shard_map/pallas_call | solution.py:747
  67.6 8.5 %all_to_all.11 = f32[8,32,128]{2,1,0:T(8,128)S(1)} all-to-all(f32[8,32,128]{2,1,0:T(8,128)S(1)} %bitcast.11), channel_id=1, replica_groups=mesh['row_0'=4,'row_1'=4,'col_0'=4,'col_1'=2] {'col_0','col_1'}, dimensions={0} | all-to-all | bytes 262144 | tf_op jit(solution)/shard_map/all_to_all | solution.py:762
  76.1 7.4 %shard_map.100 = (f32[32,128,128]{2,1,0:T(8,128)}, f32[32,128,128]{2,1,0:T(8,128)}) custom-call(s32[2]{0:T(128)S(1)} %pad_add_fusion.place_ref, f32[128,32,128]{2,1,0:T(8,128)S(1)} %get-tuple-element.16.rows_ref, f32[128,48,128]{2,1,0:T(8,128)S(1)} %get-tuple-element.23.first_ref, f32[128,48,128]{2,1,0:T(8,128)S(1)} %get-tuple-element.24.second_ref, ...), custom_call_target="tpu_custom_call" | custom-call | tf_op jit(solution)/shard_map/pallas_call | solution.py:764
  (1 shorter events, 0.0 us)
Async XLA Ops:
  0.6 8.2 %copy-start = (f32[32,128,128]{2,1,0:T(8,128)S(1)}, f32[32,128,128]{2,1,0:T(8,128)}, u32[]{:S(2)}) copy-start(f32[32,128,128]{2,1,0:T(8,128)} %load_hbm.1) | copy-start | bytes 6291460
  2.7 8.2 %collective-permute-start = (f32[3,40,128]{2,1,0:T(8,128)S(1)}, f32[3,40,128]{2,1,0:T(8,128)S(1)}, u32[]{:S(2)}, u32[]{:S(2)}) collective-permute-start(f32[3,40,128]{2,1,0:T(8,128)S(1)} %get-tuple-element.18), channel_id=1, source_target_pairs={{8,16},{24,32},{40,48},{56,64},{72,80},{88,96},{104,112},{16,8},{3... | collective-permute-start | bytes 184328 | tf_op jit(solution)/shard_map/ppermute | solution.py:659
  3.4 7.5 %collective-permute-start.1 = (f32[3,40,128]{2,1,0:T(8,128)S(1)}, f32[3,40,128]{2,1,0:T(8,128)S(1)}, u32[]{:S(2)}, u32[]{:S(2)}) collective-permute-start(f32[3,40,128]{2,1,0:T(8,128)S(1)} %get-tuple-element.19), channel_id=1, source_target_pairs={{0,8},{16,24},{32,40},{48,56},{64,72},{80,88},{96,104},{112,120},{... | collective-permute-start | bytes 184328 | tf_op jit(solution)/shard_map/ppermute | solution.py:659
  11.6 4.4 %collective-permute-start.3 = (f32[9,40,128]{2,1,0:T(8,128)S(1)}, f32[9,40,128]{2,1,0:T(8,128)S(1)}, u32[]{:S(2)}, u32[]{:S(2)}) collective-permute-start(f32[9,40,128]{2,1,0:T(8,128)S(1)} %get-tuple-element.22.own_ref), channel_id=1, source_target_pairs={{0,1},{2,3},{4,5},{6,7},{1,0},{3,2},{5,4},{7,6},{8,9},{10,11},{12,... | collective-permute-start | bytes 552968 | tf_op jit(solution)/shard_map/ppermute | solution.py:659
  13.0 6.8 %collective-permute-start.2 = (f32[9,40,128]{2,1,0:T(8,128)S(1)}, f32[9,40,128]{2,1,0:T(8,128)S(1)}, u32[]{:S(2)}, u32[]{:S(2)}) collective-permute-start(f32[9,40,128]{2,1,0:T(8,128)S(1)} %get-tuple-element.22.own_ref), channel_id=1, source_target_pairs={{1,2},{3,4},{5,6},{2,1},{4,3},{6,5},{9,10},{11,12},{13,14},{10,9},... | collective-permute-start | bytes 552968 | tf_op jit(solution)/shard_map/ppermute | solution.py:659

commit v7 on v6

--- a/solution.py
+++ b/solution.py
@@ -53,7 +53,7 @@
 
 
 def prepare_kernel(
-    place_ref, edge_hbm, pad_hbm, load_hbm, label_hbm, bump_hbm, across_hbm, down_hbm, pad_class_hbm,
+    edge_hbm, pad_hbm, load_hbm, label_hbm, bump_hbm, across_hbm, down_hbm, pad_class_hbm,
     grid_ref, far_ref, near_ref, edge_ref, pad_ref, load_ref, load_end_ref, label_ref, across_ref, down_ref, pad_class_ref, done,
 ):
     copies = [
@@ -76,7 +76,7 @@
         copy.start()
     for copy in copies:
         copy.wait()
-    pr, pc = place_ref[0], place_ref[1]
+    pr, pc = lax.axis_index(ROW), lax.axis_index(COL)
     shape = (128, 128)
     row, lane = lax.broadcasted_iota(jnp.int32, shape, 0), lanes(shape)
 
@@ -128,9 +128,11 @@
     lax.fori_loop(1, 8, step, 0)
 
 
-def corner_kernel(place_ref, own_ref, far_ref, near_ref, out_ref, top_ref, bottom_ref):
+def corner_kernel(
+    own_ref, far_ref, near_ref, out_ref, top_ref, bottom_ref, far_out_ref, near_out_ref
+):
     lane = lanes((SUB, 128)) // 8
-    even = place_ref[0] % 2 == 0
+    even = lax.axis_index(ROW) % 2 == 0
     top_ref[...] = jnp.where(even, far_ref[...], near_ref[...])
     bottom_ref[...] = jnp.where(even, near_ref[...], far_ref[...])
     for g in range(GROUPS):
@@ -143,14 +145,23 @@
         end = jnp.where(lane == s, roll(bottom_ref[n], (8 * s + 3) % 128), end)
     out_ref[0] = start
     out_ref[8] = end
+    low = lanes((SUB, 128)) % 8 < 4
+    to_right_first = lax.axis_index(COL) % 2 == 1
+    for h in range(5):
+        here = out_ref[2 * h]
+        after = out_ref[2 * h + 1] if h < 4 else here
+        right = jnp.where(low, here, roll(after, 4))
+        left = jnp.where(low, roll(here, 125), roll(after, 1))
+        far_out_ref[h] = jnp.where(to_right_first, right, left)
+        near_out_ref[h] = jnp.where(to_right_first, left, right)
 
 
 def fields_kernel(
-    place_ref, rows_ref, grid_ref, top_ref, bottom_ref, own_ref, far_ref, near_ref,
+    rows_ref, grid_ref, top_ref, bottom_ref, own_ref, far_ref, near_ref,
     first_ref, second_ref, w_ref, coef_ref, out_ref,
     ext, so, ss, sz_o, sz_s, y0_o, y0_s, qz, q0, q1, sc, y0, y1, gram,
 ):
-    pr, pc = place_ref[0], place_ref[1]
+    pr, pc = lax.axis_index(ROW), lax.axis_index(COL)
     lane1 = lanes((1, 128))
     lane16 = lanes((16, 128))
     lane48 = lanes((48, 128))
@@ -187,10 +198,14 @@
     def below(here, after, lane):
         return roll(jnp.where(lane < 8, after, here), 120)
 
+    even = pc % 2 == 0
+
     def strips(g, _):
         o_row = own_ref[g]
-        on_left = (lanes((SUB, 128)) % 8 < 3) == (pc % 2 == 0)
-        s_row = jnp.where(on_left, far_ref[g], near_ref[g])
+        far, near = far_ref[g // 2], near_ref[g // 2]
+        on_left, on_right = jnp.where(even, far, near), jnp.where(even, near, far)
+        turn = 124 * (g % 2)
+        s_row = jnp.where(lanes((SUB, 128)) % 8 < 3, roll(on_left, turn), roll(on_right, 3 + turn))
         so[g + 1], ss[g + 1] = o_row, s_row
         lefts = pair_left(o_row[RIGHT : RIGHT + 1], s_row[RIGHT : RIGHT + 1], lane1)
         for side, (row, ref, ll) in enumerate(((o_row, so, lefts[0]), (s_row, ss, lefts[1]))):
@@ -296,13 +311,6 @@
             first_ref[8 * g - 8 + s] = f1
         y1[i] = coef(5, g, s) * f1
 
-    def both(g, _):
-        for s in range(8):
-            second_image(g - 2, s)
-        for s in range(8):
-            first_image(g, s)
-        return 0
-
     def only(work):
         def step(g, _):
             for s in range(8):
@@ -313,12 +321,11 @@
 
     for s in (6, 7):
         first_image(0, s)
-    lax.fori_loop(1, 3, only(first_image), 0)
-    second_image(0, 7)
-    lax.fori_loop(3, 17, both, 0)
+    lax.fori_loop(1, 17, only(first_image), 0)
     for s in (0, 1):
         first_image(17, s)
-    lax.fori_loop(15, 17, only(second_image), 0)
+    second_image(0, 7)
+    lax.fori_loop(1, 17, only(second_image), 0)
     second_image(17, 0)
 
     gram[...] = jnp.zeros((96, 256), F32)
@@ -422,8 +429,8 @@
     return jnp.concatenate(parts, axis=0)
 
 
-def coarse_kernel(place_ref, in_ref, out_ref, g, e, ei, first, second, near):
-    pr, pc = place_ref[0], place_ref[1]
+def coarse_kernel(in_ref, out_ref, g, e, ei, first, second, near):
+    pr, pc = lax.axis_index(ROW), lax.axis_index(COL)
     sub8 = lax.broadcasted_iota(jnp.int32, (8, 128), 0)
 
     lane8 = lanes((8, 128))
@@ -600,14 +607,14 @@
 
 
 def outputs_kernel(
-    place_ref, rows_ref, first_ref, second_ref, w_ref, grid_ref, coef_ref, m_ref, sol_ref, res_ref,
+    rows_ref, first_ref, second_ref, w_ref, grid_ref, coef_ref, m_ref, sol_ref, res_ref,
     left_ref, step_ref, window_ref,
 ):
     block = pl.program_id(0)
 
     @pl.when(block == 0)
     def _():
-        pr, pc = place_ref[0], place_ref[1]
+        pr, pc = lax.axis_index(ROW), lax.axis_index(COL)
         slot = lax.broadcasted_iota(jnp.int32, (16, 128), 0)
         region_row = pr - 1 + slot // 4
         region_col = 2 * pc - 1 + slot % 4
@@ -636,16 +643,16 @@
             step_ref[n] = jnp.broadcast_to(m[0:32, 64 + n : 65 + n], (32, 128))
 
     left, window = left_ref[...], window_ref[...]
-    for part in range(2):
+    for part in range(4):
         rows = []
         for n in range(8):
-            r = 16 * block + 8 * part + n
+            r = 32 * block + 8 * part + n
             z = jnp.where(grid_ref[pl.ds(r, 1), :] == window, grid_ref[pl.ds(128 + r, 1), :], 0.0)
             rows.append(jnp.concatenate([z, w_ref[r], first_ref[r, 32:48], second_ref[r, 32:48]], axis=0))
         r1, r2, r3 = parts_of(jnp.concatenate(rows, axis=1), 3)
         d = fast_dot(left, jnp.concatenate([r1, r2, r1, r2, r3, r1], axis=0))
         for n in range(8):
-            r = 16 * block + 8 * part + n
+            r = 32 * block + 8 * part + n
             b, u, uu = rows_ref[r], first_ref[r, 0:32], second_ref[r, 0:32]
             e = d[:, 128 * n : 128 * n + 128]
             inv = coef_ref[5, pl.ds(r + 16, 1), :]
@@ -672,21 +679,18 @@
 
 
 def body(load_currents, labels, bump_height, horizontal_class, vertical_class, pad_class, edge_table, pad_table):
-    pr, pc = lax.axis_index(ROW), lax.axis_index(COL)
     rows, cols = lax.axis_size(ROW), lax.axis_size(COL)
-    place = jnp.stack([pr, pc]).astype(jnp.int32)
     loads = load_currents.reshape(-1, 128)
     grid, far_rows, near_rows = pl.pallas_call(
         prepare_kernel,
         out_shape=(kept(1024, 128), shape_of(HALO, SUB, 128), shape_of(HALO, SUB, 128)),
         compiler_params=limited,
-        in_specs=[scalars] + [outside] * 8,
+        in_specs=[outside] * 8,
         out_specs=(whole,) * 3,
         scratch_shapes=[pltpu.SMEM((8,), F32), pltpu.SMEM((8,), F32), vmem(32, 8, 128), vmem(32, 8, 128)]
         + [pltpu.VMEM((128, 128), jnp.int32)] * 4
         + [pltpu.SemaphoreType.DMA((9,))],
     )(
-        place,
         *(
             pltpu.with_memory_space_constraint(x, pltpu.HBM)
             for x in (
@@ -704,15 +708,16 @@
         in_specs=[whole] * 2,
         out_specs=(whole,) * 2,
     )(loads, grid)
-    own, top, bottom = pl.pallas_call(
+    own, top, bottom, far_columns, near_columns = pl.pallas_call(
         corner_kernel,
-        out_shape=(shape_of(GROUPS, SUB, 128), kept(HALO, SUB, 128), kept(HALO, SUB, 128)),
+        out_shape=(kept(GROUPS, SUB, 128), kept(HALO, SUB, 128), kept(HALO, SUB, 128))
+        + (shape_of(5, SUB, 128),) * 2,
         compiler_params=limited,
-        in_specs=[scalars] + [whole] * 3,
-        out_specs=(whole,) * 3,
-    )(place, own, far_rows, near_rows)
-    near_columns = swapped(own, COL, 0)
-    far_columns = swapped(own, COL, 1)
+        in_specs=[whole] * 3,
+        out_specs=(whole,) * 5,
+    )(own, far_rows, near_rows)
+    far_columns = swapped(far_columns, COL, 1)
+    near_columns = swapped(near_columns, COL, 0)
     first, second, w, coef, payload = pl.pallas_call(
         fields_kernel,
         out_shape=(
@@ -723,7 +728,7 @@
             shape_of(32, 128),
         ),
         compiler_params=limited,
-        in_specs=[scalars] + [whole] * 7,
+        in_specs=[whole] * 7,
         out_specs=(whole,) * 5,
         scratch_shapes=[
             vmem(5, 160, 128),
@@ -741,14 +746,14 @@
             vmem(144, 48, 128),
             vmem(96, 256),
         ],
-    )(place, by_rows, grid, top, bottom, own, far_columns, near_columns)
+    )(by_rows, grid, top, bottom, own, far_columns, near_columns)
     sent = jnp.broadcast_to(payload.reshape(1, cols, 4, 128), (rows, cols, 4, 128)).reshape(-1, 4, 128)
     everything = lax.all_to_all(sent, ROW + COL, 0, 0, tiled=True).reshape(-1, 128)
     found = pl.pallas_call(
         coarse_kernel,
         out_shape=shape_of(256, 128),
         compiler_params=limited,
-        in_specs=[scalars, whole],
+        in_specs=[whole],
         out_specs=whole,
         scratch_shapes=[
             vmem(256, 128),
@@ -758,18 +763,18 @@
             vmem(272, 128),
             vmem(32, 128),
         ],
-    )(place, everything)
+    )(everything)
     matrix = lax.all_to_all(found.reshape(cols, 32, 128), COL, 0, 0, tiled=True).reshape(-1, 128)
-    by_block = pl.BlockSpec((32, 16, 128), lambda k: (0, k, 0))
+    by_block = pl.BlockSpec((32, 32, 128), lambda k: (0, k, 0))
     return pl.pallas_call(
         outputs_kernel,
-        grid=(8,),
+        grid=(4,),
         out_shape=(shape_of(32, 128, 128), shape_of(32, 128, 128)),
         compiler_params=limited,
-        in_specs=[scalars] + [whole] * 7,
+        in_specs=[whole] * 7,
         out_specs=(by_block, by_block),
         scratch_shapes=[pltpu.VMEM((96, 384), jnp.bfloat16), vmem(2, 32, 128), vmem(16, 128)],
-    )(place, by_rows, first, second, w, grid, coef, matrix)
+    )(by_rows, first, second, w, grid, coef, matrix)
 
 
 def solution(mesh):

time: 83.7 us -> 79 us (0.944)
  Pallas kernels: 38.8 us -> 35.2 us
  waiting for transfers between devices: 3.82 us -> 2.24 us
    ppermute x4, waiting for transfers between devices: 3.82 us -> 2.24 us  [swapped(): return lax.ppermute(value, axis, pairs + [(b, a) for a, b in pairs])]
    pallas_call x2, Pallas kernels: 8.03 us -> 6.72 us  [the longest x1 6.53 us: body(): pl.pallas_call(outputs_kernel, grid=(4,), out_shape=(shape_of(32, 128, 12...]
    pallas_call x1, Pallas kernels: 18 us -> 16.7 us  [body(): pl.pallas_call(fields_kernel, out_shape=(kept(128, 48, 128), kept(128, 48...]
  transfers between devices with their start and end apart: 4 -> 4, of which waited for: 1 -> 1; matrix products, arithmetic and copies ran while one was open for 0% -> 0% of each run, Pallas kernels for 2% -> 3%
where the time goes in v7:
time: 79 us; the launch traced here: 78.8 us
  Pallas kernels  35.2 us (45%)
  blocking collectives  30 us (38%)
  starting transfers between devices  10.5 us (13%)
  waiting for transfers between devices  2.24 us (3%)
    all_to_all x1, blocking collectives, body(): lax.all_to_all(sent, ROW + COL, 0, 0, tiled=True).reshape(-1, 128)  21.5 us
    pallas_call x1, Pallas kernels, body(): pl.pallas_call(fields_kernel, out_shape=(kept(128, 48, 128), kept(128, 48...  16.7 us
    ppermute x4, starting transfers between devices, swapped(): return lax.ppermute(value, axis, pairs + [(b, a) for a, b in pairs])  10.5 us
    all_to_all x1, blocking collectives, body(): lax.all_to_all(found.reshape(cols, 32, 128), COL, 0, 0, tiled=True)  8.51 us
    pallas_call x1, Pallas kernels, body(): pl.pallas_call(coarse_kernel, out_shape=shape_of(256, 128), compiler_para...  8.16 us
    pallas_call x1, Pallas kernels, body(): pl.pallas_call(outputs_kernel, grid=(4,), out_shape=(shape_of(32, 128, 12...  6.53 us
    ppermute x4, waiting for transfers between devices, swapped(): return lax.ppermute(value, axis, pairs + [(b, a) for a, b in pairs])  2.24 us
    pallas_call x1, Pallas kernels, body(): pl.pallas_call(pack_kernel, out_shape=(kept(128, 32, 128), kept(GROUPS, S...  2.08 us
  transfers between devices with their start and end apart: 4, of which 1 were waited for; matrix products, arithmetic and copies ran while one was open for 0% of the time, Pallas kernels for 3%

profile of v7, /device:TPU:1, one launch (start us, length us, event | category | flops | bytes accessed | tf_op | source)
XLA Modules:
  0.0 78.8 jit_solution(16093218858168307095)
XLA Ops:
  0.6 0.0 copy-start
  0.6 1.6 %shard_map.95 = (f32[1024,128]{1,0:T(8,128)S(1)}, f32[3,40,128]{2,1,0:T(8,128)S(1)}, f32[3,40,128]{2,1,0:T(8,128)S(1)}) custom-call(f32[8]{0:T(128)} %edge_hbm.1, f32[8]{0:T(128)} %pad_hbm.1, f32[32,128,128]{2,1,0:T(8,128)} %load_hbm.1, s32[128,128]{1,0:T(8,128)} %label_hbm.1, f32[128,128]{1,0:T(8,128)} %bump_hbm.1, s32[128,128]{1,0:T(8,128)} %across_hbm.1, ...), custom_call_target="tpu_custom_call" | custom-call | tf_op jit(solution)/shard_map/pallas_call | solution.py:684
  2.2 0.7 collective-permute-start
  2.9 5.4 %collective-permute-start.1 = (f32[3,40,128]{2,1,0:T(8,128)S(1)}, f32[3,40,128]{2,1,0:T(8,128)S(1)}, u32[]{:S(2)}, u32[]{:S(2)}) collective-permute-start(f32[3,40,128]{2,1,0:T(8,128)S(1)} %get-tuple-element.21), channel_id=1, source_target_pairs={{0,8},{16,24},{32,40},{48,56},{64,72},{80,88},{96,104},{112,120},{... | collective-permute-start | bytes 184328 | tf_op jit(solution)/shard_map/ppermute | solution.py:666
  8.3 0.0 copy-done
  8.3 2.1 %shard_map.96 = (f32[128,32,128]{2,1,0:T(8,128)S(1)}, f32[9,40,128]{2,1,0:T(8,128)S(1)}) custom-call(f32[4096,128]{1,0:T(8,128)S(1)} %bitcast.6, f32[1024,128]{1,0:T(8,128)S(1)} %get-tuple-element.17.grid_ref), custom_call_target="tpu_custom_call" | custom-call | tf_op jit(solution)/shard_map/pallas_call | solution.py:704
  10.4 0.0 collective-permute-done.far_ref
  10.4 0.0 collective-permute-done.1.near_ref
  10.4 0.2 shard_map.97
  10.6 4.3 %collective-permute-start.2 = (f32[5,40,128]{2,1,0:T(8,128)S(1)}, f32[5,40,128]{2,1,0:T(8,128)S(1)}, u32[]{:S(2)}, u32[]{:S(2)}) collective-permute-start(f32[5,40,128]{2,1,0:T(8,128)S(1)} %get-tuple-element.25), channel_id=1, source_target_pairs={{1,2},{3,4},{5,6},{2,1},{4,3},{6,5},{9,10},{11,12},{13,14},{10,9},... | collective-permute-start | bytes 307208 | tf_op jit(solution)/shard_map/ppermute | solution.py:666
  15.0 0.1 collective-permute-start.3
  15.1 2.2 %collective-permute-done.2.far_ref = f32[5,40,128]{2,1,0:T(8,128)S(1)} collective-permute-done((f32[5,40,128]{2,1,0:T(8,128)S(1)}, f32[5,40,128]{2,1,0:T(8,128)S(1)}, u32[]{:S(2)}, u32[]{:S(2)}) %collective-permute-start.2) | collective-permute-done | bytes 102432 | tf_op jit(solution)/shard_map/ppermute | solution.py:666
  17.3 0.0 collective-permute-done.3.near_ref
  17.3 16.7 %shard_map.98 = (f32[128,48,128]{2,1,0:T(8,128)S(1)}, f32[128,48,128]{2,1,0:T(8,128)S(1)}, f32[128,16,128]{2,1,0:T(8,128)S(1)}, f32[6,160,128]{2,1,0:T(8,128)S(1)}, f32[32,128]{1,0:T(8,128)S(1)}) custom-call(f32[128,32,128]{2,1,0:T(8,128)S(1)} %get-tuple-element.18.rows_ref, f32[1024,128]{1,0:T(8,128)S(1)} %get-tuple-element.17.grid_ref, ...), custom_call_target="tpu_custom_call" | custom-call | tf_op jit(solution)/shard_map/pallas_call | solution.py:721
  34.1 21.5 %all_to_all.10 = f32[128,4,128]{2,1,0:T(4,128)S(1)} all-to-all(f32[128,4,128]{2,1,0:T(4,128)S(1)} %bitcast.11), channel_id=1, replica_groups=mesh['row_0'=4,'row_1'=4,'col_0'=4,'col_1'=2] {'row_0','row_1','col_0','..., dimensions={0} | all-to-all | bytes 524288 | tf_op jit(solution)/shard_map/all_to_all | solution.py:751
  55.6 8.2 %shard_map.99 = f32[256,128]{1,0:T(8,128)S(1)} custom-call(f32[512,128]{1,0:T(8,128)S(1)} %bitcast.7), custom_call_target="tpu_custom_call" | custom-call | tf_op jit(solution)/shard_map/pallas_call | solution.py:752
  63.7 8.5 %all_to_all.11 = f32[8,32,128]{2,1,0:T(8,128)S(1)} all-to-all(f32[8,32,128]{2,1,0:T(8,128)S(1)} %bitcast.9), channel_id=1, replica_groups=mesh['row_0'=4,'row_1'=4,'col_0'=4,'col_1'=2] {'col_0','col_1'}, dimensions={0} | all-to-all | bytes 262144 | tf_op jit(solution)/shard_map/all_to_all | solution.py:767
  72.3 6.5 %shard_map.100 = (f32[32,128,128]{2,1,0:T(8,128)}, f32[32,128,128]{2,1,0:T(8,128)}) custom-call(f32[128,32,128]{2,1,0:T(8,128)S(1)} %get-tuple-element.18.rows_ref, f32[128,48,128]{2,1,0:T(8,128)S(1)} %get-tuple-element.27.first_ref, f32[128,48,128]{2,1,0:T(8,128)S(1)} %get-tuple-element.28.second_ref, f32[128,16,128]{2,1,0:T(8,128)S(1)} %get-tuple-element.29.w_ref, ...), custom_call_target="tpu_custom_call" | custom-call | tf_op jit(solution)/shard_map/pallas_call | solution.py:769
  (1 shorter events, 0.0 us)
Async XLA Ops:
  0.6 7.7 %copy-start = (f32[32,128,128]{2,1,0:T(8,128)S(1)}, f32[32,128,128]{2,1,0:T(8,128)}, u32[]{:S(2)}) copy-start(f32[32,128,128]{2,1,0:T(8,128)} %load_hbm.1) | copy-start | bytes 6291460
  2.2 8.2 %collective-permute-start = (f32[3,40,128]{2,1,0:T(8,128)S(1)}, f32[3,40,128]{2,1,0:T(8,128)S(1)}, u32[]{:S(2)}, u32[]{:S(2)}) collective-permute-start(f32[3,40,128]{2,1,0:T(8,128)S(1)} %get-tuple-element.20), channel_id=1, source_target_pairs={{8,16},{24,32},{40,48},{56,64},{72,80},{88,96},{104,112},{16,8},{3... | collective-permute-start | bytes 184328 | tf_op jit(solution)/shard_map/ppermute | solution.py:666
  2.9 7.5 %collective-permute-start.1 = (f32[3,40,128]{2,1,0:T(8,128)S(1)}, f32[3,40,128]{2,1,0:T(8,128)S(1)}, u32[]{:S(2)}, u32[]{:S(2)}) collective-permute-start(f32[3,40,128]{2,1,0:T(8,128)S(1)} %get-tuple-element.21), channel_id=1, source_target_pairs={{0,8},{16,24},{32,40},{48,56},{64,72},{80,88},{96,104},{112,120},{... | collective-permute-start | bytes 184328 | tf_op jit(solution)/shard_map/ppermute | solution.py:666
  10.6 6.7 %collective-permute-start.2 = (f32[5,40,128]{2,1,0:T(8,128)S(1)}, f32[5,40,128]{2,1,0:T(8,128)S(1)}, u32[]{:S(2)}, u32[]{:S(2)}) collective-permute-start(f32[5,40,128]{2,1,0:T(8,128)S(1)} %get-tuple-element.25), channel_id=1, source_target_pairs={{1,2},{3,4},{5,6},{2,1},{4,3},{6,5},{9,10},{11,12},{13,14},{10,9},... | collective-permute-start | bytes 307208 | tf_op jit(solution)/shard_map/ppermute | solution.py:666
  15.0 2.3 %collective-permute-start.3 = (f32[5,40,128]{2,1,0:T(8,128)S(1)}, f32[5,40,128]{2,1,0:T(8,128)S(1)}, u32[]{:S(2)}, u32[]{:S(2)}) collective-permute-start(f32[5,40,128]{2,1,0:T(8,128)S(1)} %get-tuple-element.26), channel_id=1, source_target_pairs={{0,1},{2,3},{4,5},{6,7},{1,0},{3,2},{5,4},{7,6},{8,9},{10,11},{12,... | collective-permute-start | bytes 307208 | tf_op jit(solution)/shard_map/ppermute | solution.py:666

commit v8 on v7

--- a/solution.py
+++ b/solution.py
@@ -10,7 +10,6 @@
 ROW = ("row_0", "row_1")
 COL = ("col_0", "col_1")
 F32 = jnp.float32
-precise = lax.Precision.HIGHEST
 
 LAB, BUMP, RIGHT, DOWN, PAD = 32, 33, 34, 35, 36
 SUB = 40
@@ -24,11 +23,6 @@
 whole = pl.BlockSpec(memory_space=pltpu.VMEM)
 outside = pl.BlockSpec(memory_space=pltpu.HBM)
 limited = pltpu.CompilerParams(vmem_limit_bytes=32 * 2**20)
-scalars = pl.BlockSpec(memory_space=pltpu.SMEM)
-
-
-def dot(a, b, dims=NN):
-    return lax.dot_general(a, b, dims, precision=precise, preferred_element_type=F32)
 
 
 def parts_of(x, count):
@@ -42,6 +36,17 @@
 
 def fast_dot(a, b, dims=NN):
     return lax.dot_general(a, b, dims, preferred_element_type=F32)
+
+
+def dot(a, b, dims=NN):
+    (at_a,), (at_b,) = dims[0]
+    a1, a2, a3 = parts_of(a, 3)
+    b1, b2, b3 = parts_of(b, 3)
+    return fast_dot(
+        jnp.concatenate([a3, a1, a2, a2, a1, a1], axis=at_a),
+        jnp.concatenate([b1, b3, b2, b1, b2, b1], axis=at_b),
+        dims,
+    )
 
 
 def lanes(shape):
@@ -159,7 +164,7 @@
 def fields_kernel(
     rows_ref, grid_ref, top_ref, bottom_ref, own_ref, far_ref, near_ref,
     first_ref, second_ref, w_ref, coef_ref, out_ref,
-    ext, so, ss, sz_o, sz_s, y0_o, y0_s, qz, q0, q1, sc, y0, y1, gram,
+    ext, so, ss, sz_o, sz_s, y0_o, y0_s, qz, q0, q1, u0, u1, sc, y0, y1, gram,
 ):
     pr, pc = lax.axis_index(ROW), lax.axis_index(COL)
     lane1 = lanes((1, 128))
@@ -277,8 +282,10 @@
     def coef(n, g, s):
         return coef_ref[n, pl.ds(8 * g + 8 + s, 1), :]
 
-    def image(here, up, down, strip, g, s, lane):
-        other = roll(strip[g], 125 - 8 * s)
+    def unpacked(strip, g, s):
+        return roll(strip[g], 125 - 8 * s)
+
+    def image(here, up, down, other, g, s, lane):
         left = roll(jnp.where(lane == 127, other, here), 1)
         right = roll(jnp.where(lane == 0, other, here), 127)
         return (
@@ -294,7 +301,7 @@
 
     def first_image(g, s):
         r, j = 8 * g - 8 + s, 8 * g + 8 + s
-        w = image(basis(j), basis(j - 1), basis(j + 1), qz, g, s, lane16)
+        w = image(basis(j), basis(j - 1), basis(j + 1), unpacked(qz, g, s), g, s, lane16)
         if owned(g):
             b = rows_ref[r]
             w_ref[r] = w
@@ -303,10 +310,12 @@
         inv = coef(5, g, s)
         y0[8 * g + s, 0:32] = inv * b
         y0[8 * g + s, 32:48] = inv * w
+        u0[8 * g + s] = unpacked(q0, g, s)
+        u1[8 * g + s] = unpacked(q1, g, s)
 
     def second_image(g, s):
         i = 8 * g + s
-        f1 = image(y0[i], y0[i - 1], y0[i + 1], q0, g, s, lane48)
+        f1 = image(y0[i], y0[i - 1], y0[i + 1], u0[i], g, s, lane48)
         if owned(g):
             first_ref[8 * g - 8 + s] = f1
         y1[i] = coef(5, g, s) * f1
@@ -325,14 +334,20 @@
     for s in (0, 1):
         first_image(17, s)
     second_image(0, 7)
-    lax.fori_loop(1, 17, only(second_image), 0)
+
+    def second_pair(t, _):
+        for s in range(16):
+            second_image(2 * t + 1 + s // 8, s % 8)
+        return 0
+
+    lax.fori_loop(0, 8, second_pair, 0)
     second_image(17, 0)
 
     gram[...] = jnp.zeros((96, 256), F32)
 
     def third_image(g, s):
         i = 8 * g + s
-        second_ref[i - 8] = image(y1[i], y1[i - 1], y1[i + 1], q1, g, s, lane48)
+        second_ref[i - 8] = image(y1[i], y1[i - 1], y1[i + 1], u1[i], g, s, lane48)
 
     def products(g, sums):
         left, every = [], []
@@ -395,7 +410,13 @@
             if n == 1:
                 first_two, line = line, jnp.zeros((1, 128), F32)
         total = jnp.where(row4 == 0, first_two, jnp.where(row4 == 1, line, 0.0))
-        out_ref[4 * d : 4 * d + 4] = jnp.where(lane4 < 120, sent, total)
+        sent = jnp.where(lane4 < 120, sent, total)
+        if d % 2 == 0:
+            before = sent
+            continue
+        pair = jnp.concatenate([before, sent], axis=0)
+        for r in range(16):
+            out_ref[32 * r + 4 * d - 4 : 32 * r + 4 * d + 4] = pair
 
 
 def batched_inverse(a, lane, row, size):
@@ -725,7 +746,7 @@
             kept(128, 48, 128),
             kept(128, 16, 128),
             kept(6, 160, 128),
-            shape_of(32, 128),
+            shape_of(512, 128),
         ),
         compiler_params=limited,
         in_specs=[whole] * 7,
@@ -741,13 +762,15 @@
             vmem(2 * GROUPS, 16, 128),
             vmem(2 * GROUPS, 48, 128),
             vmem(2 * GROUPS, 48, 128),
+            vmem(144, 48, 128),
+            vmem(144, 48, 128),
             vmem(2, GROUPS, 8, 128),
             vmem(144, 48, 128),
             vmem(144, 48, 128),
             vmem(96, 256),
         ],
     )(by_rows, grid, top, bottom, own, far_columns, near_columns)
-    sent = jnp.broadcast_to(payload.reshape(1, cols, 4, 128), (rows, cols, 4, 128)).reshape(-1, 4, 128)
+    sent = payload.reshape(-1, 4, 128)
     everything = lax.all_to_all(sent, ROW + COL, 0, 0, tiled=True).reshape(-1, 128)
     found = pl.pallas_call(
         coarse_kernel,

time: 79 us -> 77.7 us (0.984)
  Pallas kernels: 35.2 us -> 34 us
where the time goes in v8:
time: 77.7 us; the launch traced here: 77.5 us
  Pallas kernels  34 us (44%)
  blocking collectives  30 us (39%)
  starting transfers between devices  10.5 us (14%)
  waiting for transfers between devices  2.24 us (3%)
    all_to_all x1, blocking collectives, body(): lax.all_to_all(sent, ROW + COL, 0, 0, tiled=True).reshape(-1, 128)  21.5 us
    pallas_call x1, Pallas kernels, body(): pl.pallas_call(fields_kernel, out_shape=(kept(128, 48, 128), kept(128, 48...  16 us
    ppermute x4, starting transfers between devices, swapped(): return lax.ppermute(value, axis, pairs + [(b, a) for a, b in pairs])  10.5 us
    all_to_all x1, blocking collectives, body(): lax.all_to_all(found.reshape(cols, 32, 128), COL, 0, 0, tiled=True)  8.51 us
    pallas_call x1, Pallas kernels, body(): pl.pallas_call(coarse_kernel, out_shape=shape_of(256, 128), compiler_para...  7.61 us
    pallas_call x1, Pallas kernels, body(): pl.pallas_call(outputs_kernel, grid=(4,), out_shape=(shape_of(32, 128, 12...  6.53 us
    ppermute x4, waiting for transfers between devices, swapped(): return lax.ppermute(value, axis, pairs + [(b, a) for a, b in pairs])  2.24 us
    pallas_call x1, Pallas kernels, body(): pl.pallas_call(pack_kernel, out_shape=(kept(128, 32, 128), kept(GROUPS, S...  2.08 us
  transfers between devices with their start and end apart: 4, of which 1 were waited for; matrix products, arithmetic and copies ran while one was open for 0% of the time, Pallas kernels for 3%

profile of v8, /device:TPU:1, one launch (start us, length us, event | category | flops | bytes accessed | tf_op | source)
XLA Modules:
  0.0 77.5 jit_solution(6170730919862308107)
XLA Ops:
  0.6 0.0 copy-start
  0.6 1.6 %shard_map.95 = (f32[1024,128]{1,0:T(8,128)S(1)}, f32[3,40,128]{2,1,0:T(8,128)S(1)}, f32[3,40,128]{2,1,0:T(8,128)S(1)}) custom-call(f32[8]{0:T(128)} %edge_hbm.1, f32[8]{0:T(128)} %pad_hbm.1, f32[32,128,128]{2,1,0:T(8,128)} %load_hbm.1, s32[128,128]{1,0:T(8,128)} %label_hbm.1, f32[128,128]{1,0:T(8,128)} %bump_hbm.1, s32[128,128]{1,0:T(8,128)} %across_hbm.1, ...), custom_call_target="tpu_custom_call" | custom-call | tf_op jit(solution)/shard_map/pallas_call | solution.py:705
  2.2 0.7 collective-permute-start
  2.9 5.4 %collective-permute-start.1 = (f32[3,40,128]{2,1,0:T(8,128)S(1)}, f32[3,40,128]{2,1,0:T(8,128)S(1)}, u32[]{:S(2)}, u32[]{:S(2)}) collective-permute-start(f32[3,40,128]{2,1,0:T(8,128)S(1)} %get-tuple-element.21), channel_id=1, source_target_pairs={{0,8},{16,24},{32,40},{48,56},{64,72},{80,88},{96,104},{112,120},{... | collective-permute-start | bytes 184328 | tf_op jit(solution)/shard_map/ppermute | solution.py:687
  8.3 0.0 copy-done
  8.3 2.1 %shard_map.96 = (f32[128,32,128]{2,1,0:T(8,128)S(1)}, f32[9,40,128]{2,1,0:T(8,128)S(1)}) custom-call(f32[4096,128]{1,0:T(8,128)S(1)} %bitcast.5, f32[1024,128]{1,0:T(8,128)S(1)} %get-tuple-element.17.grid_ref), custom_call_target="tpu_custom_call" | custom-call | tf_op jit(solution)/shard_map/pallas_call | solution.py:725
  10.4 0.0 collective-permute-done.far_ref
  10.4 0.0 collective-permute-done.1.near_ref
  10.4 0.2 shard_map.97
  10.6 4.3 %collective-permute-start.2 = (f32[5,40,128]{2,1,0:T(8,128)S(1)}, f32[5,40,128]{2,1,0:T(8,128)S(1)}, u32[]{:S(2)}, u32[]{:S(2)}) collective-permute-start(f32[5,40,128]{2,1,0:T(8,128)S(1)} %get-tuple-element.25), channel_id=1, source_target_pairs={{1,2},{3,4},{5,6},{2,1},{4,3},{6,5},{9,10},{11,12},{13,14},{10,9},... | collective-permute-start | bytes 307208 | tf_op jit(solution)/shard_map/ppermute | solution.py:687
  15.0 0.1 collective-permute-start.3
  15.1 2.2 %collective-permute-done.2.far_ref = f32[5,40,128]{2,1,0:T(8,128)S(1)} collective-permute-done((f32[5,40,128]{2,1,0:T(8,128)S(1)}, f32[5,40,128]{2,1,0:T(8,128)S(1)}, u32[]{:S(2)}, u32[]{:S(2)}) %collective-permute-start.2) | collective-permute-done | bytes 102432 | tf_op jit(solution)/shard_map/ppermute | solution.py:687
  17.3 0.0 collective-permute-done.3.near_ref
  17.3 16.0 %shard_map.98 = (f32[128,48,128]{2,1,0:T(8,128)S(1)}, f32[128,48,128]{2,1,0:T(8,128)S(1)}, f32[128,16,128]{2,1,0:T(8,128)S(1)}, f32[6,160,128]{2,1,0:T(8,128)S(1)}, f32[512,128]{1,0:T(8,128)S(1)}) custom-call(f32[128,32,128]{2,1,0:T(8,128)S(1)} %get-tuple-element.18.rows_ref, f32[1024,128]{1,0:T(8,128)S(1)} %get-tuple-element.17.grid_ref, ...), custom_call_target="tpu_custom_call" | custom-call | tf_op jit(solution)/shard_map/pallas_call | solution.py:742
  33.3 21.5 %all_to_all.10 = f32[128,4,128]{2,1,0:T(4,128)S(1)} all-to-all(f32[128,4,128]{2,1,0:T(4,128)S(1)} %bitcast.9), channel_id=1, replica_groups=mesh['row_0'=4,'row_1'=4,'col_0'=4,'col_1'=2] {'row_0','row_1','col_0','..., dimensions={0} | all-to-all | bytes 524288 | tf_op jit(solution)/shard_map/all_to_all | solution.py:774
  54.8 7.6 %shard_map.99 = f32[256,128]{1,0:T(8,128)S(1)} custom-call(f32[512,128]{1,0:T(8,128)S(1)} %bitcast.6), custom_call_target="tpu_custom_call" | custom-call | tf_op jit(solution)/shard_map/pallas_call | solution.py:775
  62.5 8.5 %all_to_all.11 = f32[8,32,128]{2,1,0:T(8,128)S(1)} all-to-all(f32[8,32,128]{2,1,0:T(8,128)S(1)} %bitcast.8), channel_id=1, replica_groups=mesh['row_0'=4,'row_1'=4,'col_0'=4,'col_1'=2] {'col_0','col_1'}, dimensions={0} | all-to-all | bytes 262144 | tf_op jit(solution)/shard_map/all_to_all | solution.py:790
  71.0 6.5 %shard_map.100 = (f32[32,128,128]{2,1,0:T(8,128)}, f32[32,128,128]{2,1,0:T(8,128)}) custom-call(f32[128,32,128]{2,1,0:T(8,128)S(1)} %get-tuple-element.18.rows_ref, f32[128,48,128]{2,1,0:T(8,128)S(1)} %get-tuple-element.27.first_ref, f32[128,48,128]{2,1,0:T(8,128)S(1)} %get-tuple-element.28.second_ref, f32[128,16,128]{2,1,0:T(8,128)S(1)} %get-tuple-element.29.w_ref, ...), custom_call_target="tpu_custom_call" | custom-call | tf_op jit(solution)/shard_map/pallas_call | solution.py:792
Async XLA Ops:
  0.6 7.7 %copy-start = (f32[32,128,128]{2,1,0:T(8,128)S(1)}, f32[32,128,128]{2,1,0:T(8,128)}, u32[]{:S(2)}) copy-start(f32[32,128,128]{2,1,0:T(8,128)} %load_hbm.1) | copy-start | bytes 6291460
  2.2 8.2 %collective-permute-start = (f32[3,40,128]{2,1,0:T(8,128)S(1)}, f32[3,40,128]{2,1,0:T(8,128)S(1)}, u32[]{:S(2)}, u32[]{:S(2)}) collective-permute-start(f32[3,40,128]{2,1,0:T(8,128)S(1)} %get-tuple-element.20), channel_id=1, source_target_pairs={{8,16},{24,32},{40,48},{56,64},{72,80},{88,96},{104,112},{16,8},{3... | collective-permute-start | bytes 184328 | tf_op jit(solution)/shard_map/ppermute | solution.py:687
  2.9 7.5 %collective-permute-start.1 = (f32[3,40,128]{2,1,0:T(8,128)S(1)}, f32[3,40,128]{2,1,0:T(8,128)S(1)}, u32[]{:S(2)}, u32[]{:S(2)}) collective-permute-start(f32[3,40,128]{2,1,0:T(8,128)S(1)} %get-tuple-element.21), channel_id=1, source_target_pairs={{0,8},{16,24},{32,40},{48,56},{64,72},{80,88},{96,104},{112,120},{... | collective-permute-start | bytes 184328 | tf_op jit(solution)/shard_map/ppermute | solution.py:687
  10.6 6.7 %collective-permute-start.2 = (f32[5,40,128]{2,1,0:T(8,128)S(1)}, f32[5,40,128]{2,1,0:T(8,128)S(1)}, u32[]{:S(2)}, u32[]{:S(2)}) collective-permute-start(f32[5,40,128]{2,1,0:T(8,128)S(1)} %get-tuple-element.25), channel_id=1, source_target_pairs={{1,2},{3,4},{5,6},{2,1},{4,3},{6,5},{9,10},{11,12},{13,14},{10,9},... | collective-permute-start | bytes 307208 | tf_op jit(solution)/shard_map/ppermute | solution.py:687
  15.0 2.3 %collective-permute-start.3 = (f32[5,40,128]{2,1,0:T(8,128)S(1)}, f32[5,40,128]{2,1,0:T(8,128)S(1)}, u32[]{:S(2)}, u32[]{:S(2)}) collective-permute-start(f32[5,40,128]{2,1,0:T(8,128)S(1)} %get-tuple-element.26), channel_id=1, source_target_pairs={{0,1},{2,3},{4,5},{6,7},{1,0},{3,2},{5,4},{7,6},{8,9},{10,11},{12,... | collective-permute-start | bytes 307208 | tf_op jit(solution)/shard_map/ppermute | solution.py:687

commit v9 on v8

--- a/solution.py
+++ b/solution.py
@@ -352,8 +352,8 @@
     def products(g, sums):
         left, every = [], []
         sums = list(sums)
-        for s in range(8):
-            i = 8 * g + s
+        for s in range(16):
+            i = 16 * g + 8 + s
             r = i - 8
             b, f1, f2, y0r, y1r = rows_ref[r], first_ref[r], second_ref[r], y0[i], y1[i]
             left.append(jnp.concatenate([basis(i + 8), y0r[32:48], y1r[32:48]], axis=0))
@@ -365,16 +365,20 @@
         gram[:, 0:144] += fast_dot(left, high, NT) + fast_dot(left, low, NT)
         return tuple(sums)
 
-    def last_stage(g, sums):
-        sums = products(g - 1, sums)
-        for s in range(8):
-            third_image(g, s)
+    def third_pair(t, _):
+        for s in range(16):
+            third_image(2 * t + 1 + s // 8, s % 8)
+        return 0
+
+    def last_stage(t, sums):
+        sums = products(t - 1, sums)
+        third_pair(t, 0)
         return sums
 
     zero = jnp.zeros((32, 128), F32)
-    lax.fori_loop(1, 2, only(third_image), 0)
-    sums = lax.fori_loop(2, 17, last_stage, (zero, zero, zero, zero))
-    sums = lax.fori_loop(16, 17, products, sums)
+    lax.fori_loop(0, 1, third_pair, 0)
+    sums = lax.fori_loop(1, 8, last_stage, (zero, zero, zero, zero))
+    sums = lax.fori_loop(7, 8, products, sums)
 
     a0, a1 = gram[0:48, 0:128] + gram[48:96, 0:128], gram[0:48, 128:256] + gram[48:96, 128:256]
     zr, w0, t0, w1, t1 = a0[0:16], a0[16:32], a0[32:48], a1[16:32], a1[32:48]

time: 77.7 us -> 77.1 us (level)
  no operation moved by 1% of the time
where the time goes in v9:
time: 77.1 us; the launch traced here: 76.9 us
  Pallas kernels  33.5 us (43%)
  blocking collectives  30 us (39%)
  starting transfers between devices  10.5 us (14%)
  waiting for transfers between devices  2.24 us (3%)
    all_to_all x1, blocking collectives, body(): lax.all_to_all(sent, ROW + COL, 0, 0, tiled=True).reshape(-1, 128)  21.5 us
    pallas_call x1, Pallas kernels, body(): pl.pallas_call(fields_kernel, out_shape=(kept(128, 48, 128), kept(128, 48...  15.4 us
    ppermute x4, starting transfers between devices, swapped(): return lax.ppermute(value, axis, pairs + [(b, a) for a, b in pairs])  10.5 us
    all_to_all x1, blocking collectives, body(): lax.all_to_all(found.reshape(cols, 32, 128), COL, 0, 0, tiled=True)  8.52 us
    pallas_call x1, Pallas kernels, body(): pl.pallas_call(coarse_kernel, out_shape=shape_of(256, 128), compiler_para...  7.61 us
    pallas_call x1, Pallas kernels, body(): pl.pallas_call(outputs_kernel, grid=(4,), out_shape=(shape_of(32, 128, 12...  6.53 us
    ppermute x4, waiting for transfers between devices, swapped(): return lax.ppermute(value, axis, pairs + [(b, a) for a, b in pairs])  2.24 us
    pallas_call x1, Pallas kernels, body(): pl.pallas_call(pack_kernel, out_shape=(kept(128, 32, 128), kept(GROUPS, S...  2.08 us
  transfers between devices with their start and end apart: 4, of which 1 were waited for; matrix products, arithmetic and copies ran while one was open for 0% of the time, Pallas kernels for 3%

profile of v9, /device:TPU:1, one launch (start us, length us, event | category | flops | bytes accessed | tf_op | source)
XLA Modules:
  0.0 76.9 jit_solution(11332603837455658679)
XLA Ops:
  0.6 0.0 copy-start
  0.6 1.6 %shard_map.95 = (f32[1024,128]{1,0:T(8,128)S(1)}, f32[3,40,128]{2,1,0:T(8,128)S(1)}, f32[3,40,128]{2,1,0:T(8,128)S(1)}) custom-call(f32[8]{0:T(128)} %edge_hbm.1, f32[8]{0:T(128)} %pad_hbm.1, f32[32,128,128]{2,1,0:T(8,128)} %load_hbm.1, s32[128,128]{1,0:T(8,128)} %label_hbm.1, f32[128,128]{1,0:T(8,128)} %bump_hbm.1, s32[128,128]{1,0:T(8,128)} %across_hbm.1, ...), custom_call_target="tpu_custom_call" | custom-call | tf_op jit(solution)/shard_map/pallas_call | solution.py:709
  2.2 0.7 collective-permute-start
  2.9 5.4 %collective-permute-start.1 = (f32[3,40,128]{2,1,0:T(8,128)S(1)}, f32[3,40,128]{2,1,0:T(8,128)S(1)}, u32[]{:S(2)}, u32[]{:S(2)}) collective-permute-start(f32[3,40,128]{2,1,0:T(8,128)S(1)} %get-tuple-element.21), channel_id=1, source_target_pairs={{0,8},{16,24},{32,40},{48,56},{64,72},{80,88},{96,104},{112,120},{... | collective-permute-start | bytes 184328 | tf_op jit(solution)/shard_map/ppermute | solution.py:691
  8.3 0.0 copy-done
  8.3 2.1 %shard_map.96 = (f32[128,32,128]{2,1,0:T(8,128)S(1)}, f32[9,40,128]{2,1,0:T(8,128)S(1)}) custom-call(f32[4096,128]{1,0:T(8,128)S(1)} %bitcast.5, f32[1024,128]{1,0:T(8,128)S(1)} %get-tuple-element.17.grid_ref), custom_call_target="tpu_custom_call" | custom-call | tf_op jit(solution)/shard_map/pallas_call | solution.py:729
  10.4 0.0 collective-permute-done.far_ref
  10.4 0.0 collective-permute-done.1.near_ref
  10.4 0.2 shard_map.97
  10.6 4.3 %collective-permute-start.2 = (f32[5,40,128]{2,1,0:T(8,128)S(1)}, f32[5,40,128]{2,1,0:T(8,128)S(1)}, u32[]{:S(2)}, u32[]{:S(2)}) collective-permute-start(f32[5,40,128]{2,1,0:T(8,128)S(1)} %get-tuple-element.25), channel_id=1, source_target_pairs={{1,2},{3,4},{5,6},{2,1},{4,3},{6,5},{9,10},{11,12},{13,14},{10,9},... | collective-permute-start | bytes 307208 | tf_op jit(solution)/shard_map/ppermute | solution.py:691
  15.0 0.1 collective-permute-start.3
  15.1 2.2 %collective-permute-done.2.far_ref = f32[5,40,128]{2,1,0:T(8,128)S(1)} collective-permute-done((f32[5,40,128]{2,1,0:T(8,128)S(1)}, f32[5,40,128]{2,1,0:T(8,128)S(1)}, u32[]{:S(2)}, u32[]{:S(2)}) %collective-permute-start.2) | collective-permute-done | bytes 102432 | tf_op jit(solution)/shard_map/ppermute | solution.py:691
  17.3 0.0 collective-permute-done.3.near_ref
  17.3 15.4 %shard_map.98 = (f32[128,48,128]{2,1,0:T(8,128)S(1)}, f32[128,48,128]{2,1,0:T(8,128)S(1)}, f32[128,16,128]{2,1,0:T(8,128)S(1)}, f32[6,160,128]{2,1,0:T(8,128)S(1)}, f32[512,128]{1,0:T(8,128)S(1)}) custom-call(f32[128,32,128]{2,1,0:T(8,128)S(1)} %get-tuple-element.18.rows_ref, f32[1024,128]{1,0:T(8,128)S(1)} %get-tuple-element.17.grid_ref, ...), custom_call_target="tpu_custom_call" | custom-call | tf_op jit(solution)/shard_map/pallas_call | solution.py:746
  32.8 21.5 %all_to_all.10 = f32[128,4,128]{2,1,0:T(4,128)S(1)} all-to-all(f32[128,4,128]{2,1,0:T(4,128)S(1)} %bitcast.9), channel_id=1, replica_groups=mesh['row_0'=4,'row_1'=4,'col_0'=4,'col_1'=2] {'row_0','row_1','col_0','..., dimensions={0} | all-to-all | bytes 524288 | tf_op jit(solution)/shard_map/all_to_all | solution.py:778
  54.3 7.6 %shard_map.99 = f32[256,128]{1,0:T(8,128)S(1)} custom-call(f32[512,128]{1,0:T(8,128)S(1)} %bitcast.6), custom_call_target="tpu_custom_call" | custom-call | tf_op jit(solution)/shard_map/pallas_call | solution.py:779
  61.9 8.5 %all_to_all.11 = f32[8,32,128]{2,1,0:T(8,128)S(1)} all-to-all(f32[8,32,128]{2,1,0:T(8,128)S(1)} %bitcast.8), channel_id=1, replica_groups=mesh['row_0'=4,'row_1'=4,'col_0'=4,'col_1'=2] {'col_0','col_1'}, dimensions={0} | all-to-all | bytes 262144 | tf_op jit(solution)/shard_map/all_to_all | solution.py:794
  70.4 6.5 %shard_map.100 = (f32[32,128,128]{2,1,0:T(8,128)}, f32[32,128,128]{2,1,0:T(8,128)}) custom-call(f32[128,32,128]{2,1,0:T(8,128)S(1)} %get-tuple-element.18.rows_ref, f32[128,48,128]{2,1,0:T(8,128)S(1)} %get-tuple-element.27.first_ref, f32[128,48,128]{2,1,0:T(8,128)S(1)} %get-tuple-element.28.second_ref, f32[128,16,128]{2,1,0:T(8,128)S(1)} %get-tuple-element.29.w_ref, ...), custom_call_target="tpu_custom_call" | custom-call | tf_op jit(solution)/shard_map/pallas_call | solution.py:796
Async XLA Ops:
  0.6 7.7 %copy-start = (f32[32,128,128]{2,1,0:T(8,128)S(1)}, f32[32,128,128]{2,1,0:T(8,128)}, u32[]{:S(2)}) copy-start(f32[32,128,128]{2,1,0:T(8,128)} %load_hbm.1) | copy-start | bytes 6291460
  2.2 8.2 %collective-permute-start = (f32[3,40,128]{2,1,0:T(8,128)S(1)}, f32[3,40,128]{2,1,0:T(8,128)S(1)}, u32[]{:S(2)}, u32[]{:S(2)}) collective-permute-start(f32[3,40,128]{2,1,0:T(8,128)S(1)} %get-tuple-element.20), channel_id=1, source_target_pairs={{8,16},{24,32},{40,48},{56,64},{72,80},{88,96},{104,112},{16,8},{3... | collective-permute-start | bytes 184328 | tf_op jit(solution)/shard_map/ppermute | solution.py:691
  2.9 7.5 %collective-permute-start.1 = (f32[3,40,128]{2,1,0:T(8,128)S(1)}, f32[3,40,128]{2,1,0:T(8,128)S(1)}, u32[]{:S(2)}, u32[]{:S(2)}) collective-permute-start(f32[3,40,128]{2,1,0:T(8,128)S(1)} %get-tuple-element.21), channel_id=1, source_target_pairs={{0,8},{16,24},{32,40},{48,56},{64,72},{80,88},{96,104},{112,120},{... | collective-permute-start | bytes 184328 | tf_op jit(solution)/shard_map/ppermute | solution.py:691
  10.6 6.7 %collective-permute-start.2 = (f32[5,40,128]{2,1,0:T(8,128)S(1)}, f32[5,40,128]{2,1,0:T(8,128)S(1)}, u32[]{:S(2)}, u32[]{:S(2)}) collective-permute-start(f32[5,40,128]{2,1,0:T(8,128)S(1)} %get-tuple-element.25), channel_id=1, source_target_pairs={{1,2},{3,4},{5,6},{2,1},{4,3},{6,5},{9,10},{11,12},{13,14},{10,9},... | collective-permute-start | bytes 307208 | tf_op jit(solution)/shard_map/ppermute | solution.py:691
  15.0 2.3 %collective-permute-start.3 = (f32[5,40,128]{2,1,0:T(8,128)S(1)}, f32[5,40,128]{2,1,0:T(8,128)S(1)}, u32[]{:S(2)}, u32[]{:S(2)}) collective-permute-start(f32[5,40,128]{2,1,0:T(8,128)S(1)} %get-tuple-element.26), channel_id=1, source_target_pairs={{0,1},{2,3},{4,5},{6,7},{1,0},{3,2},{5,4},{7,6},{8,9},{10,11},{12,... | collective-permute-start | bytes 307208 | tf_op jit(solution)/shard_map/ppermute | solution.py:691

commit v10 on v9

--- a/solution.py
+++ b/solution.py
@@ -311,13 +311,13 @@
         y0[8 * g + s, 0:32] = inv * b
         y0[8 * g + s, 32:48] = inv * w
         u0[8 * g + s] = unpacked(q0, g, s)
-        u1[8 * g + s] = unpacked(q1, g, s)
 
     def second_image(g, s):
         i = 8 * g + s
         f1 = image(y0[i], y0[i - 1], y0[i + 1], u0[i], g, s, lane48)
         if owned(g):
             first_ref[8 * g - 8 + s] = f1
+            u1[i] = unpacked(q1, g, s)
         y1[i] = coef(5, g, s) * f1
 
     def only(work):

time: 77.1 us -> 76.1 us (0.987)
  Pallas kernels: 33.5 us -> 32.4 us
    pallas_call x1, Pallas kernels: 15.4 us -> 14.3 us  [body(): pl.pallas_call(fields_kernel, out_shape=(kept(128, 48, 128), kept(128, 48...]
where the time goes in v10:
time: 76.1 us; the launch traced here: 75.8 us
  Pallas kernels  32.4 us (43%)
  blocking collectives  30 us (39%)
  starting transfers between devices  10.5 us (14%)
  waiting for transfers between devices  2.24 us (3%)
    all_to_all x1, blocking collectives, body(): lax.all_to_all(sent, ROW + COL, 0, 0, tiled=True).reshape(-1, 128)  21.5 us
    pallas_call x1, Pallas kernels, body(): pl.pallas_call(fields_kernel, out_shape=(kept(128, 48, 128), kept(128, 48...  14.3 us
    ppermute x4, starting transfers between devices, swapped(): return lax.ppermute(value, axis, pairs + [(b, a) for a, b in pairs])  10.5 us
    all_to_all x1, blocking collectives, body(): lax.all_to_all(found.reshape(cols, 32, 128), COL, 0, 0, tiled=True)  8.51 us
    pallas_call x1, Pallas kernels, body(): pl.pallas_call(coarse_kernel, out_shape=shape_of(256, 128), compiler_para...  7.62 us
    pallas_call x1, Pallas kernels, body(): pl.pallas_call(outputs_kernel, grid=(4,), out_shape=(shape_of(32, 128, 12...  6.53 us
    ppermute x4, waiting for transfers between devices, swapped(): return lax.ppermute(value, axis, pairs + [(b, a) for a, b in pairs])  2.24 us
    pallas_call x1, Pallas kernels, body(): pl.pallas_call(pack_kernel, out_shape=(kept(128, 32, 128), kept(GROUPS, S...  2.08 us
  transfers between devices with their start and end apart: 4, of which 1 were waited for; matrix products, arithmetic and copies ran while one was open for 0% of the time, Pallas kernels for 3%

profile of v10, /device:TPU:1, one launch (start us, length us, event | category | flops | bytes accessed | tf_op | source)
XLA Modules:
  0.0 75.8 jit_solution(11826978530148562014)
XLA Ops:
  0.6 0.0 copy-start
  0.6 1.6 %shard_map.95 = (f32[1024,128]{1,0:T(8,128)S(1)}, f32[3,40,128]{2,1,0:T(8,128)S(1)}, f32[3,40,128]{2,1,0:T(8,128)S(1)}) custom-call(f32[8]{0:T(128)} %edge_hbm.1, f32[8]{0:T(128)} %pad_hbm.1, f32[32,128,128]{2,1,0:T(8,128)} %load_hbm.1, s32[128,128]{1,0:T(8,128)} %label_hbm.1, f32[128,128]{1,0:T(8,128)} %bump_hbm.1, s32[128,128]{1,0:T(8,128)} %across_hbm.1, ...), custom_call_target="tpu_custom_call" | custom-call | tf_op jit(solution)/shard_map/pallas_call | solution.py:709
  2.2 0.7 collective-permute-start
  2.9 5.4 %collective-permute-start.1 = (f32[3,40,128]{2,1,0:T(8,128)S(1)}, f32[3,40,128]{2,1,0:T(8,128)S(1)}, u32[]{:S(2)}, u32[]{:S(2)}) collective-permute-start(f32[3,40,128]{2,1,0:T(8,128)S(1)} %get-tuple-element.21), channel_id=1, source_target_pairs={{0,8},{16,24},{32,40},{48,56},{64,72},{80,88},{96,104},{112,120},{... | collective-permute-start | bytes 184328 | tf_op jit(solution)/shard_map/ppermute | solution.py:691
  8.3 0.0 copy-done
  8.3 2.1 %shard_map.96 = (f32[128,32,128]{2,1,0:T(8,128)S(1)}, f32[9,40,128]{2,1,0:T(8,128)S(1)}) custom-call(f32[4096,128]{1,0:T(8,128)S(1)} %bitcast.5, f32[1024,128]{1,0:T(8,128)S(1)} %get-tuple-element.17.grid_ref), custom_call_target="tpu_custom_call" | custom-call | tf_op jit(solution)/shard_map/pallas_call | solution.py:729
  10.4 0.0 collective-permute-done.far_ref
  10.4 0.0 collective-permute-done.1.near_ref
  10.4 0.2 shard_map.97
  10.6 4.3 %collective-permute-start.2 = (f32[5,40,128]{2,1,0:T(8,128)S(1)}, f32[5,40,128]{2,1,0:T(8,128)S(1)}, u32[]{:S(2)}, u32[]{:S(2)}) collective-permute-start(f32[5,40,128]{2,1,0:T(8,128)S(1)} %get-tuple-element.25), channel_id=1, source_target_pairs={{1,2},{3,4},{5,6},{2,1},{4,3},{6,5},{9,10},{11,12},{13,14},{10,9},... | collective-permute-start | bytes 307208 | tf_op jit(solution)/shard_map/ppermute | solution.py:691
  15.0 0.1 collective-permute-start.3
  15.1 2.2 %collective-permute-done.2.far_ref = f32[5,40,128]{2,1,0:T(8,128)S(1)} collective-permute-done((f32[5,40,128]{2,1,0:T(8,128)S(1)}, f32[5,40,128]{2,1,0:T(8,128)S(1)}, u32[]{:S(2)}, u32[]{:S(2)}) %collective-permute-start.2) | collective-permute-done | bytes 102432 | tf_op jit(solution)/shard_map/ppermute | solution.py:691
  17.3 0.0 collective-permute-done.3.near_ref
  17.3 14.3 %shard_map.98 = (f32[128,48,128]{2,1,0:T(8,128)S(1)}, f32[128,48,128]{2,1,0:T(8,128)S(1)}, f32[128,16,128]{2,1,0:T(8,128)S(1)}, f32[6,160,128]{2,1,0:T(8,128)S(1)}, f32[512,128]{1,0:T(8,128)S(1)}) custom-call(f32[128,32,128]{2,1,0:T(8,128)S(1)} %get-tuple-element.18.rows_ref, f32[1024,128]{1,0:T(8,128)S(1)} %get-tuple-element.17.grid_ref, ...), custom_call_target="tpu_custom_call" | custom-call | tf_op jit(solution)/shard_map/pallas_call | solution.py:746
  31.7 21.5 %all_to_all.10 = f32[128,4,128]{2,1,0:T(4,128)S(1)} all-to-all(f32[128,4,128]{2,1,0:T(4,128)S(1)} %bitcast.9), channel_id=1, replica_groups=mesh['row_0'=4,'row_1'=4,'col_0'=4,'col_1'=2] {'row_0','row_1','col_0','..., dimensions={0} | all-to-all | bytes 524288 | tf_op jit(solution)/shard_map/all_to_all | solution.py:778
  53.2 7.6 %shard_map.99 = f32[256,128]{1,0:T(8,128)S(1)} custom-call(f32[512,128]{1,0:T(8,128)S(1)} %bitcast.6), custom_call_target="tpu_custom_call" | custom-call | tf_op jit(solution)/shard_map/pallas_call | solution.py:779
  60.8 8.5 %all_to_all.11 = f32[8,32,128]{2,1,0:T(8,128)S(1)} all-to-all(f32[8,32,128]{2,1,0:T(8,128)S(1)} %bitcast.8), channel_id=1, replica_groups=mesh['row_0'=4,'row_1'=4,'col_0'=4,'col_1'=2] {'col_0','col_1'}, dimensions={0} | all-to-all | bytes 262144 | tf_op jit(solution)/shard_map/all_to_all | solution.py:794
  69.3 6.5 %shard_map.100 = (f32[32,128,128]{2,1,0:T(8,128)}, f32[32,128,128]{2,1,0:T(8,128)}) custom-call(f32[128,32,128]{2,1,0:T(8,128)S(1)} %get-tuple-element.18.rows_ref, f32[128,48,128]{2,1,0:T(8,128)S(1)} %get-tuple-element.27.first_ref, f32[128,48,128]{2,1,0:T(8,128)S(1)} %get-tuple-element.28.second_ref, f32[128,16,128]{2,1,0:T(8,128)S(1)} %get-tuple-element.29.w_ref, ...), custom_call_target="tpu_custom_call" | custom-call | tf_op jit(solution)/shard_map/pallas_call | solution.py:796
Async XLA Ops:
  0.6 7.7 %copy-start = (f32[32,128,128]{2,1,0:T(8,128)S(1)}, f32[32,128,128]{2,1,0:T(8,128)}, u32[]{:S(2)}) copy-start(f32[32,128,128]{2,1,0:T(8,128)} %load_hbm.1) | copy-start | bytes 6291460
  2.2 8.2 %collective-permute-start = (f32[3,40,128]{2,1,0:T(8,128)S(1)}, f32[3,40,128]{2,1,0:T(8,128)S(1)}, u32[]{:S(2)}, u32[]{:S(2)}) collective-permute-start(f32[3,40,128]{2,1,0:T(8,128)S(1)} %get-tuple-element.20), channel_id=1, source_target_pairs={{8,16},{24,32},{40,48},{56,64},{72,80},{88,96},{104,112},{16,8},{3... | collective-permute-start | bytes 184328 | tf_op jit(solution)/shard_map/ppermute | solution.py:691
  2.9 7.5 %collective-permute-start.1 = (f32[3,40,128]{2,1,0:T(8,128)S(1)}, f32[3,40,128]{2,1,0:T(8,128)S(1)}, u32[]{:S(2)}, u32[]{:S(2)}) collective-permute-start(f32[3,40,128]{2,1,0:T(8,128)S(1)} %get-tuple-element.21), channel_id=1, source_target_pairs={{0,8},{16,24},{32,40},{48,56},{64,72},{80,88},{96,104},{112,120},{... | collective-permute-start | bytes 184328 | tf_op jit(solution)/shard_map/ppermute | solution.py:691
  10.6 6.7 %collective-permute-start.2 = (f32[5,40,128]{2,1,0:T(8,128)S(1)}, f32[5,40,128]{2,1,0:T(8,128)S(1)}, u32[]{:S(2)}, u32[]{:S(2)}) collective-permute-start(f32[5,40,128]{2,1,0:T(8,128)S(1)} %get-tuple-element.25), channel_id=1, source_target_pairs={{1,2},{3,4},{5,6},{2,1},{4,3},{6,5},{9,10},{11,12},{13,14},{10,9},... | collective-permute-start | bytes 307208 | tf_op jit(solution)/shard_map/ppermute | solution.py:691
  15.0 2.3 %collective-permute-start.3 = (f32[5,40,128]{2,1,0:T(8,128)S(1)}, f32[5,40,128]{2,1,0:T(8,128)S(1)}, u32[]{:S(2)}, u32[]{:S(2)}) collective-permute-start(f32[5,40,128]{2,1,0:T(8,128)S(1)} %get-tuple-element.26), channel_id=1, source_target_pairs={{0,1},{2,3},{4,5},{6,7},{1,0},{3,2},{5,4},{7,6},{8,9},{10,11},{12,... | collective-permute-start | bytes 307208 | tf_op jit(solution)/shard_map/ppermute | solution.py:691

commit v11 on v10

--- a/solution.py
+++ b/solution.py
@@ -261,8 +261,8 @@
             ref[g + 1, 0:32] = inv * source[g + 1, 0:32]
             ref[g + 1, 32:48] = inv * w[side]
         y = y0_s[g + 1]
-        q0[2 * g] = y
-        q0[2 * g + 1] = roll(y, 64)
+        for s in range(16):
+            u0[16 * g + s] = roll(y, (125 - 8 * s) % 128)
         return 0
 
     lax.fori_loop(0, GROUPS, strip_first, 0, unroll=3)
@@ -310,7 +310,6 @@
         inv = coef(5, g, s)
         y0[8 * g + s, 0:32] = inv * b
         y0[8 * g + s, 32:48] = inv * w
-        u0[8 * g + s] = unpacked(q0, g, s)
 
     def second_image(g, s):
         i = 8 * g + s

time: 76.1 us -> 76.8 us (level)
  no operation moved by 1% of the time
where the time goes in v11:
time: 76.8 us; the launch traced here: 76.6 us
  Pallas kernels  33.1 us (43%)
  blocking collectives  30 us (39%)
  starting transfers between devices  10.5 us (14%)
  waiting for transfers between devices  2.24 us (3%)
    all_to_all x1, blocking collectives, body(): lax.all_to_all(sent, ROW + COL, 0, 0, tiled=True).reshape(-1, 128)  21.5 us
    pallas_call x1, Pallas kernels, body(): pl.pallas_call(fields_kernel, out_shape=(kept(128, 48, 128), kept(128, 48...  15.1 us
    ppermute x4, starting transfers between devices, swapped(): return lax.ppermute(value, axis, pairs + [(b, a) for a, b in pairs])  10.5 us
    all_to_all x1, blocking collectives, body(): lax.all_to_all(found.reshape(cols, 32, 128), COL, 0, 0, tiled=True)  8.51 us
    pallas_call x1, Pallas kernels, body(): pl.pallas_call(coarse_kernel, out_shape=shape_of(256, 128), compiler_para...  7.61 us
    pallas_call x1, Pallas kernels, body(): pl.pallas_call(outputs_kernel, grid=(4,), out_shape=(shape_of(32, 128, 12...  6.53 us
    ppermute x4, waiting for transfers between devices, swapped(): return lax.ppermute(value, axis, pairs + [(b, a) for a, b in pairs])  2.24 us
    pallas_call x1, Pallas kernels, body(): pl.pallas_call(pack_kernel, out_shape=(kept(128, 32, 128), kept(GROUPS, S...  2.08 us
  transfers between devices with their start and end apart: 4, of which 1 were waited for; matrix products, arithmetic and copies ran while one was open for 0% of the time, Pallas kernels for 3%

profile of v11, /device:TPU:1, one launch (start us, length us, event | category | flops | bytes accessed | tf_op | source)
XLA Modules:
  0.0 76.6 jit_solution(342933802451511988)
XLA Ops:
  0.6 0.0 copy-start
  0.6 1.6 %shard_map.95 = (f32[1024,128]{1,0:T(8,128)S(1)}, f32[3,40,128]{2,1,0:T(8,128)S(1)}, f32[3,40,128]{2,1,0:T(8,128)S(1)}) custom-call(f32[8]{0:T(128)} %edge_hbm.1, f32[8]{0:T(128)} %pad_hbm.1, f32[32,128,128]{2,1,0:T(8,128)} %load_hbm.1, s32[128,128]{1,0:T(8,128)} %label_hbm.1, f32[128,128]{1,0:T(8,128)} %bump_hbm.1, s32[128,128]{1,0:T(8,128)} %across_hbm.1, ...), custom_call_target="tpu_custom_call" | custom-call | tf_op jit(solution)/shard_map/pallas_call | solution.py:708
  2.2 0.7 collective-permute-start
  2.9 5.4 %collective-permute-start.1 = (f32[3,40,128]{2,1,0:T(8,128)S(1)}, f32[3,40,128]{2,1,0:T(8,128)S(1)}, u32[]{:S(2)}, u32[]{:S(2)}) collective-permute-start(f32[3,40,128]{2,1,0:T(8,128)S(1)} %get-tuple-element.21), channel_id=1, source_target_pairs={{0,8},{16,24},{32,40},{48,56},{64,72},{80,88},{96,104},{112,120},{... | collective-permute-start | bytes 184328 | tf_op jit(solution)/shard_map/ppermute | solution.py:690
  8.3 0.0 copy-done
  8.3 2.1 %shard_map.96 = (f32[128,32,128]{2,1,0:T(8,128)S(1)}, f32[9,40,128]{2,1,0:T(8,128)S(1)}) custom-call(f32[4096,128]{1,0:T(8,128)S(1)} %bitcast.5, f32[1024,128]{1,0:T(8,128)S(1)} %get-tuple-element.17.grid_ref), custom_call_target="tpu_custom_call" | custom-call | tf_op jit(solution)/shard_map/pallas_call | solution.py:728
  10.4 0.0 collective-permute-done.far_ref
  10.4 0.0 collective-permute-done.1.near_ref
  10.4 0.2 shard_map.97
  10.6 4.3 %collective-permute-start.2 = (f32[5,40,128]{2,1,0:T(8,128)S(1)}, f32[5,40,128]{2,1,0:T(8,128)S(1)}, u32[]{:S(2)}, u32[]{:S(2)}) collective-permute-start(f32[5,40,128]{2,1,0:T(8,128)S(1)} %get-tuple-element.25), channel_id=1, source_target_pairs={{1,2},{3,4},{5,6},{2,1},{4,3},{6,5},{9,10},{11,12},{13,14},{10,9},... | collective-permute-start | bytes 307208 | tf_op jit(solution)/shard_map/ppermute | solution.py:690
  15.0 0.1 collective-permute-start.3
  15.1 2.2 %collective-permute-done.2.far_ref = f32[5,40,128]{2,1,0:T(8,128)S(1)} collective-permute-done((f32[5,40,128]{2,1,0:T(8,128)S(1)}, f32[5,40,128]{2,1,0:T(8,128)S(1)}, u32[]{:S(2)}, u32[]{:S(2)}) %collective-permute-start.2) | collective-permute-done | bytes 102432 | tf_op jit(solution)/shard_map/ppermute | solution.py:690
  17.3 0.0 collective-permute-done.3.near_ref
  17.3 15.1 %shard_map.98 = (f32[128,48,128]{2,1,0:T(8,128)S(1)}, f32[128,48,128]{2,1,0:T(8,128)S(1)}, f32[128,16,128]{2,1,0:T(8,128)S(1)}, f32[6,160,128]{2,1,0:T(8,128)S(1)}, f32[512,128]{1,0:T(8,128)S(1)}) custom-call(f32[128,32,128]{2,1,0:T(8,128)S(1)} %get-tuple-element.18.rows_ref, f32[1024,128]{1,0:T(8,128)S(1)} %get-tuple-element.17.grid_ref, ...), custom_call_target="tpu_custom_call" | custom-call | tf_op jit(solution)/shard_map/pallas_call | solution.py:745
  32.4 21.5 %all_to_all.10 = f32[128,4,128]{2,1,0:T(4,128)S(1)} all-to-all(f32[128,4,128]{2,1,0:T(4,128)S(1)} %bitcast.9), channel_id=1, replica_groups=mesh['row_0'=4,'row_1'=4,'col_0'=4,'col_1'=2] {'row_0','row_1','col_0','..., dimensions={0} | all-to-all | bytes 524288 | tf_op jit(solution)/shard_map/all_to_all | solution.py:777
  53.9 7.6 %shard_map.99 = f32[256,128]{1,0:T(8,128)S(1)} custom-call(f32[512,128]{1,0:T(8,128)S(1)} %bitcast.6), custom_call_target="tpu_custom_call" | custom-call | tf_op jit(solution)/shard_map/pallas_call | solution.py:778
  61.6 8.5 %all_to_all.11 = f32[8,32,128]{2,1,0:T(8,128)S(1)} all-to-all(f32[8,32,128]{2,1,0:T(8,128)S(1)} %bitcast.8), channel_id=1, replica_groups=mesh['row_0'=4,'row_1'=4,'col_0'=4,'col_1'=2] {'col_0','col_1'}, dimensions={0} | all-to-all | bytes 262144 | tf_op jit(solution)/shard_map/all_to_all | solution.py:793
  70.1 6.5 %shard_map.100 = (f32[32,128,128]{2,1,0:T(8,128)}, f32[32,128,128]{2,1,0:T(8,128)}) custom-call(f32[128,32,128]{2,1,0:T(8,128)S(1)} %get-tuple-element.18.rows_ref, f32[128,48,128]{2,1,0:T(8,128)S(1)} %get-tuple-element.27.first_ref, f32[128,48,128]{2,1,0:T(8,128)S(1)} %get-tuple-element.28.second_ref, f32[128,16,128]{2,1,0:T(8,128)S(1)} %get-tuple-element.29.w_ref, ...), custom_call_target="tpu_custom_call" | custom-call | tf_op jit(solution)/shard_map/pallas_call | solution.py:795
Async XLA Ops:
  0.6 7.7 %copy-start = (f32[32,128,128]{2,1,0:T(8,128)S(1)}, f32[32,128,128]{2,1,0:T(8,128)}, u32[]{:S(2)}) copy-start(f32[32,128,128]{2,1,0:T(8,128)} %load_hbm.1) | copy-start | bytes 6291460
  2.2 8.2 %collective-permute-start = (f32[3,40,128]{2,1,0:T(8,128)S(1)}, f32[3,40,128]{2,1,0:T(8,128)S(1)}, u32[]{:S(2)}, u32[]{:S(2)}) collective-permute-start(f32[3,40,128]{2,1,0:T(8,128)S(1)} %get-tuple-element.20), channel_id=1, source_target_pairs={{8,16},{24,32},{40,48},{56,64},{72,80},{88,96},{104,112},{16,8},{3... | collective-permute-start | bytes 184328 | tf_op jit(solution)/shard_map/ppermute | solution.py:690
  2.9 7.5 %collective-permute-start.1 = (f32[3,40,128]{2,1,0:T(8,128)S(1)}, f32[3,40,128]{2,1,0:T(8,128)S(1)}, u32[]{:S(2)}, u32[]{:S(2)}) collective-permute-start(f32[3,40,128]{2,1,0:T(8,128)S(1)} %get-tuple-element.21), channel_id=1, source_target_pairs={{0,8},{16,24},{32,40},{48,56},{64,72},{80,88},{96,104},{112,120},{... | collective-permute-start | bytes 184328 | tf_op jit(solution)/shard_map/ppermute | solution.py:690
  10.6 6.7 %collective-permute-start.2 = (f32[5,40,128]{2,1,0:T(8,128)S(1)}, f32[5,40,128]{2,1,0:T(8,128)S(1)}, u32[]{:S(2)}, u32[]{:S(2)}) collective-permute-start(f32[5,40,128]{2,1,0:T(8,128)S(1)} %get-tuple-element.25), channel_id=1, source_target_pairs={{1,2},{3,4},{5,6},{2,1},{4,3},{6,5},{9,10},{11,12},{13,14},{10,9},... | collective-permute-start | bytes 307208 | tf_op jit(solution)/shard_map/ppermute | solution.py:690
  15.0 2.3 %collective-permute-start.3 = (f32[5,40,128]{2,1,0:T(8,128)S(1)}, f32[5,40,128]{2,1,0:T(8,128)S(1)}, u32[]{:S(2)}, u32[]{:S(2)}) collective-permute-start(f32[5,40,128]{2,1,0:T(8,128)S(1)} %get-tuple-element.26), channel_id=1, source_target_pairs={{0,1},{2,3},{4,5},{6,7},{1,0},{3,2},{5,4},{7,6},{8,9},{10,11},{12,... | collective-permute-start | bytes 307208 | tf_op jit(solution)/shard_map/ppermute | solution.py:690

commit v12 on v10

--- a/solution.py
+++ b/solution.py
@@ -265,7 +265,7 @@
         q0[2 * g + 1] = roll(y, 64)
         return 0
 
-    lax.fori_loop(0, GROUPS, strip_first, 0, unroll=3)
+    lax.fori_loop(0, GROUPS, strip_first, 0, unroll=9)
 
     def strip_second(g, _):
         (u,) = strip_image(y0_o, y0_s, g, lane48, (1,))
@@ -274,7 +274,7 @@
         q1[2 * g + 1] = roll(y, 64)
         return 0
 
-    lax.fori_loop(0, GROUPS, strip_second, 0, unroll=3)
+    lax.fori_loop(0, GROUPS, strip_second, 0, unroll=9)
 
     def owned(g):
         return not isinstance(g, int)

time: 76.1 us -> 76.3 us (level)
  no operation moved by 1% of the time
where the time goes in v12:
time: 76.3 us; the launch traced here: 76.1 us
  Pallas kernels  32.6 us (43%)
  blocking collectives  30 us (39%)
  starting transfers between devices  10.5 us (14%)
  waiting for transfers between devices  2.24 us (3%)
    all_to_all x1, blocking collectives, body(): lax.all_to_all(sent, ROW + COL, 0, 0, tiled=True).reshape(-1, 128)  21.5 us
    pallas_call x1, Pallas kernels, body(): pl.pallas_call(fields_kernel, out_shape=(kept(128, 48, 128), kept(128, 48...  14.6 us
    ppermute x4, starting transfers between devices, swapped(): return lax.ppermute(value, axis, pairs + [(b, a) for a, b in pairs])  10.5 us
    all_to_all x1, blocking collectives, body(): lax.all_to_all(found.reshape(cols, 32, 128), COL, 0, 0, tiled=True)  8.52 us
    pallas_call x1, Pallas kernels, body(): pl.pallas_call(coarse_kernel, out_shape=shape_of(256, 128), compiler_para...  7.61 us
    pallas_call x1, Pallas kernels, body(): pl.pallas_call(outputs_kernel, grid=(4,), out_shape=(shape_of(32, 128, 12...  6.53 us
    ppermute x4, waiting for transfers between devices, swapped(): return lax.ppermute(value, axis, pairs + [(b, a) for a, b in pairs])  2.24 us
    pallas_call x1, Pallas kernels, body(): pl.pallas_call(pack_kernel, out_shape=(kept(128, 32, 128), kept(GROUPS, S...  2.08 us
  transfers between devices with their start and end apart: 4, of which 1 were waited for; matrix products, arithmetic and copies ran while one was open for 0% of the time, Pallas kernels for 3%

profile of v12, /device:TPU:1, one launch (start us, length us, event | category | flops | bytes accessed | tf_op | source)
XLA Modules:
  0.0 76.1 jit_solution(9117138329951690521)
XLA Ops:
  0.6 0.0 copy-start
  0.6 1.6 %shard_map.95 = (f32[1024,128]{1,0:T(8,128)S(1)}, f32[3,40,128]{2,1,0:T(8,128)S(1)}, f32[3,40,128]{2,1,0:T(8,128)S(1)}) custom-call(f32[8]{0:T(128)} %edge_hbm.1, f32[8]{0:T(128)} %pad_hbm.1, f32[32,128,128]{2,1,0:T(8,128)} %load_hbm.1, s32[128,128]{1,0:T(8,128)} %label_hbm.1, f32[128,128]{1,0:T(8,128)} %bump_hbm.1, s32[128,128]{1,0:T(8,128)} %across_hbm.1, ...), custom_call_target="tpu_custom_call" | custom-call | tf_op jit(solution)/shard_map/pallas_call | solution.py:709
  2.2 0.7 collective-permute-start
  2.9 5.4 %collective-permute-start.1 = (f32[3,40,128]{2,1,0:T(8,128)S(1)}, f32[3,40,128]{2,1,0:T(8,128)S(1)}, u32[]{:S(2)}, u32[]{:S(2)}) collective-permute-start(f32[3,40,128]{2,1,0:T(8,128)S(1)} %get-tuple-element.21), channel_id=1, source_target_pairs={{0,8},{16,24},{32,40},{48,56},{64,72},{80,88},{96,104},{112,120},{... | collective-permute-start | bytes 184328 | tf_op jit(solution)/shard_map/ppermute | solution.py:691
  8.3 0.0 copy-done
  8.3 2.1 %shard_map.96 = (f32[128,32,128]{2,1,0:T(8,128)S(1)}, f32[9,40,128]{2,1,0:T(8,128)S(1)}) custom-call(f32[4096,128]{1,0:T(8,128)S(1)} %bitcast.5, f32[1024,128]{1,0:T(8,128)S(1)} %get-tuple-element.17.grid_ref), custom_call_target="tpu_custom_call" | custom-call | tf_op jit(solution)/shard_map/pallas_call | solution.py:729
  10.4 0.0 collective-permute-done.far_ref
  10.4 0.0 collective-permute-done.1.near_ref
  10.4 0.2 shard_map.97
  10.6 4.3 %collective-permute-start.2 = (f32[5,40,128]{2,1,0:T(8,128)S(1)}, f32[5,40,128]{2,1,0:T(8,128)S(1)}, u32[]{:S(2)}, u32[]{:S(2)}) collective-permute-start(f32[5,40,128]{2,1,0:T(8,128)S(1)} %get-tuple-element.25), channel_id=1, source_target_pairs={{1,2},{3,4},{5,6},{2,1},{4,3},{6,5},{9,10},{11,12},{13,14},{10,9},... | collective-permute-start | bytes 307208 | tf_op jit(solution)/shard_map/ppermute | solution.py:691
  15.0 0.1 collective-permute-start.3
  15.1 2.2 %collective-permute-done.2.far_ref = f32[5,40,128]{2,1,0:T(8,128)S(1)} collective-permute-done((f32[5,40,128]{2,1,0:T(8,128)S(1)}, f32[5,40,128]{2,1,0:T(8,128)S(1)}, u32[]{:S(2)}, u32[]{:S(2)}) %collective-permute-start.2) | collective-permute-done | bytes 102432 | tf_op jit(solution)/shard_map/ppermute | solution.py:691
  17.3 0.0 collective-permute-done.3.near_ref
  17.3 14.6 %shard_map.98 = (f32[128,48,128]{2,1,0:T(8,128)S(1)}, f32[128,48,128]{2,1,0:T(8,128)S(1)}, f32[128,16,128]{2,1,0:T(8,128)S(1)}, f32[6,160,128]{2,1,0:T(8,128)S(1)}, f32[512,128]{1,0:T(8,128)S(1)}) custom-call(f32[128,32,128]{2,1,0:T(8,128)S(1)} %get-tuple-element.18.rows_ref, f32[1024,128]{1,0:T(8,128)S(1)} %get-tuple-element.17.grid_ref, ...), custom_call_target="tpu_custom_call" | custom-call | tf_op jit(solution)/shard_map/pallas_call | solution.py:746
  31.9 21.5 %all_to_all.10 = f32[128,4,128]{2,1,0:T(4,128)S(1)} all-to-all(f32[128,4,128]{2,1,0:T(4,128)S(1)} %bitcast.9), channel_id=1, replica_groups=mesh['row_0'=4,'row_1'=4,'col_0'=4,'col_1'=2] {'row_0','row_1','col_0','..., dimensions={0} | all-to-all | bytes 524288 | tf_op jit(solution)/shard_map/all_to_all | solution.py:778
  53.4 7.6 %shard_map.99 = f32[256,128]{1,0:T(8,128)S(1)} custom-call(f32[512,128]{1,0:T(8,128)S(1)} %bitcast.6), custom_call_target="tpu_custom_call" | custom-call | tf_op jit(solution)/shard_map/pallas_call | solution.py:779
  61.1 8.5 %all_to_all.11 = f32[8,32,128]{2,1,0:T(8,128)S(1)} all-to-all(f32[8,32,128]{2,1,0:T(8,128)S(1)} %bitcast.8), channel_id=1, replica_groups=mesh['row_0'=4,'row_1'=4,'col_0'=4,'col_1'=2] {'col_0','col_1'}, dimensions={0} | all-to-all | bytes 262144 | tf_op jit(solution)/shard_map/all_to_all | solution.py:794
  69.6 6.5 %shard_map.100 = (f32[32,128,128]{2,1,0:T(8,128)}, f32[32,128,128]{2,1,0:T(8,128)}) custom-call(f32[128,32,128]{2,1,0:T(8,128)S(1)} %get-tuple-element.18.rows_ref, f32[128,48,128]{2,1,0:T(8,128)S(1)} %get-tuple-element.27.first_ref, f32[128,48,128]{2,1,0:T(8,128)S(1)} %get-tuple-element.28.second_ref, f32[128,16,128]{2,1,0:T(8,128)S(1)} %get-tuple-element.29.w_ref, ...), custom_call_target="tpu_custom_call" | custom-call | tf_op jit(solution)/shard_map/pallas_call | solution.py:796
Async XLA Ops:
  0.6 7.7 %copy-start = (f32[32,128,128]{2,1,0:T(8,128)S(1)}, f32[32,128,128]{2,1,0:T(8,128)}, u32[]{:S(2)}) copy-start(f32[32,128,128]{2,1,0:T(8,128)} %load_hbm.1) | copy-start | bytes 6291460
  2.2 8.2 %collective-permute-start = (f32[3,40,128]{2,1,0:T(8,128)S(1)}, f32[3,40,128]{2,1,0:T(8,128)S(1)}, u32[]{:S(2)}, u32[]{:S(2)}) collective-permute-start(f32[3,40,128]{2,1,0:T(8,128)S(1)} %get-tuple-element.20), channel_id=1, source_target_pairs={{8,16},{24,32},{40,48},{56,64},{72,80},{88,96},{104,112},{16,8},{3... | collective-permute-start | bytes 184328 | tf_op jit(solution)/shard_map/ppermute | solution.py:691
  2.9 7.5 %collective-permute-start.1 = (f32[3,40,128]{2,1,0:T(8,128)S(1)}, f32[3,40,128]{2,1,0:T(8,128)S(1)}, u32[]{:S(2)}, u32[]{:S(2)}) collective-permute-start(f32[3,40,128]{2,1,0:T(8,128)S(1)} %get-tuple-element.21), channel_id=1, source_target_pairs={{0,8},{16,24},{32,40},{48,56},{64,72},{80,88},{96,104},{112,120},{... | collective-permute-start | bytes 184328 | tf_op jit(solution)/shard_map/ppermute | solution.py:691
  10.6 6.7 %collective-permute-start.2 = (f32[5,40,128]{2,1,0:T(8,128)S(1)}, f32[5,40,128]{2,1,0:T(8,128)S(1)}, u32[]{:S(2)}, u32[]{:S(2)}) collective-permute-start(f32[5,40,128]{2,1,0:T(8,128)S(1)} %get-tuple-element.25), channel_id=1, source_target_pairs={{1,2},{3,4},{5,6},{2,1},{4,3},{6,5},{9,10},{11,12},{13,14},{10,9},... | collective-permute-start | bytes 307208 | tf_op jit(solution)/shard_map/ppermute | solution.py:691
  15.0 2.3 %collective-permute-start.3 = (f32[5,40,128]{2,1,0:T(8,128)S(1)}, f32[5,40,128]{2,1,0:T(8,128)S(1)}, u32[]{:S(2)}, u32[]{:S(2)}) collective-permute-start(f32[5,40,128]{2,1,0:T(8,128)S(1)} %get-tuple-element.26), channel_id=1, source_target_pairs={{0,1},{2,3},{4,5},{6,7},{1,0},{3,2},{5,4},{7,6},{8,9},{10,11},{12,... | collective-permute-start | bytes 307208 | tf_op jit(solution)/shard_map/ppermute | solution.py:691
